TPU v7x, 256 devices: a whole 4x4x8 slice. The times are simulated.
256 devices in a mesh: row: 32 (over z, y), col: 8 (over x, core).
Axes of the slice: x: 4, y: 4, z: 8, core: 2. Of those that a mesh axis runs over, the one named last changes fastest.
Arguments:
- roll_embed: bfloat16 [512, 12288], P('col', 'row'), may hold values from -16 to 16
- expert_embed: bfloat16 [512, 16384], P('row', 'col'), may hold values from -16 to 16
- roll_weight: float32 [12288], P('row'), may hold values from 0.5 to 2
- expert_weight: float32 [16384], P('col'), may hold values from 0.5 to 2
Outputs:
- reward: float32 [12288], P('row')
- roll_pull: float32 [512, 12288], P('col', 'row')
- expert_pull: float32 [512, 16384], P('row', 'col')
All inputs are finite; a program needn't handle non-finite values.
Results may differ from a plain program's by a relative error of at most 0.0022.
Values may be sent and summed in bfloat16 or wider, within the bound.
No kernel may reach another device: no remote copies, remote signals or barrier semaphores. Data moves between devices by JAX's collectives and lax.ppermute only.
A program may use at most 64 MiB of HBM per device.

v0:
```python
import jax
import jax.numpy as jnp
from jax import lax
from jax.sharding import Mesh
from jax.sharding import PartitionSpec as P

ITERS = 3
ROW = ("row_0", "row_1")


blur = 0.05


def sent_to_all(x, axis):
    peers = lax.axis_size(axis)
    return lax.all_to_all(jnp.broadcast_to(x[None], (peers, *x.shape)), axis, 0, 0, tiled=True)


def gathered_once(x, axis):
    leaves = jax.tree.leaves(x)
    order = sorted(range(len(leaves)), key=lambda k: -leaves[k].size)
    width = (1, *leaves[order[0]].shape)[-1]
    lines = [
        jnp.pad(leaves[k].reshape(-1), (0, -leaves[k].size % width)).reshape(-1, width)
        for k in order
    ]
    both, at, found = (sent_to_all(jnp.concatenate(lines), axis), 0, {})
    for k, line in zip(order, lines):
        section = both[:, at : at + len(line)].reshape(len(both), -1)
        found[k] = section[:, : leaves[k].size].reshape(-1, *leaves[k].shape)
        at += len(line)
    numbers = iter(range(len(leaves)))
    return jax.tree.map(lambda _: found[next(numbers)], x)


def combined_pairwise(pieces, combine):
    while len(jax.tree.leaves(pieces)[0]) > 1:
        pieces = jax.vmap(combine)(
            *(jax.tree.map(lambda part: part[side::2], pieces) for side in (0, 1))
        )
    return jax.tree.map(lambda part: part[0], pieces)


def combined_all(x, axis, combine):
    pieces = gathered_once(x, axis)
    return combined_pairwise(pieces, combine)


def once_a_type(x, axis):
    leaves, found = (jax.tree.leaves(x), {})
    for leading, a in enumerate(leaves):
        if leading not in found:
            alike = [k for k, b in enumerate(leaves) if b.dtype == a.dtype]
            got = (
                gathered_once([leaves[k] for k in alike], axis)
                if len(alike) > 1
                else [sent_to_all(a, axis)]
            )
            for k, b in zip(alike, got):
                found[k] = b
    numbers = iter(range(len(leaves)))
    return jax.tree.map(lambda _: found[next(numbers)], x)


def combined_all_2(x, axis, combine):
    pieces = once_a_type(x, axis)
    return combined_pairwise(pieces, combine)


def joined_along(blocks, dim):
    shape = list(blocks.shape[1:])
    shape[dim] *= blocks.shape[0]
    return jnp.moveaxis(blocks, 0, dim).reshape(shape)


def collect(x, axis, dim):
    return joined_along(sent_to_all(x, axis), dim)


def gather_axes(x, axes, dim):
    filled = x
    for number in range(len(axes) - 1, -1, -1):
        filled = lax.all_gather(filled, axes[number], axis=dim, tiled=True)
    return filled


def cut_along(x, dim, peers):
    shape = x.shape
    blocks = x.reshape(*shape[:dim], peers, shape[dim] // peers, *shape[dim + 1 :])
    return jnp.moveaxis(blocks, dim, 0)


def sum_at_owner(x, axis, dim):
    blocks = cut_along(x, dim, lax.axis_size(axis))
    arrived = lax.all_to_all(blocks, axis, split_axis=0, concat_axis=0, tiled=True)
    return arrived.sum(axis=0)


def summed_rows(total, axes):
    for axis in axes:
        total = lax.psum_scatter(total, axis, scatter_dimension=0, tiled=True)
    return total


def combine(first, second):
    high = jnp.maximum(first[0], second[0])
    return (high, first[1] * jnp.exp(first[0] - high) + second[1] * jnp.exp(second[0] - high))


def combine_three(first, second):
    high = jnp.maximum(first[0], second[0])
    lower = jnp.exp(first[0] - high)
    upper = jnp.exp(second[0] - high)
    return (high, first[1] * lower + second[1] * upper, first[2] * lower + second[2] * upper)


def merge_over_col(top, total):
    high, summed = combined_all((top, total), "col", combine)
    return high + jnp.log(summed)


def merge_over_row(top, total):
    high, summed = combined_all_2((top, total), ROW, combine)
    return high + jnp.log(summed)


def shards(roll_embed, expert_embed, roll_weight, expert_weight):
    gathered_x = collect(roll_embed, "col", 0)
    gathered_y = gather_axes(expert_embed, ROW, 0)
    width = gathered_x.shape[0]
    rows = gathered_x.shape[1]
    cols = gathered_y.shape[1]
    block = min(512, cols)
    count = cols // block
    sqx = jnp.sum(jnp.square(gathered_x.astype(jnp.float32)), 0)
    sqy = jnp.sum(jnp.square(gathered_y.astype(jnp.float32)), 0)
    log_a = blur * jnp.log(roll_weight)
    log_b = blur * jnp.log(expert_weight)
    indices = jnp.arange(count, dtype=jnp.int32)

    def tile(start):
        ycols = lax.dynamic_slice_in_dim(gathered_y, start, block, 1)
        sq_cols = lax.dynamic_slice_in_dim(sqy, start, block, 0)
        cross = lax.dot_general(
            gathered_x, ycols, (((0,), (0,)), ((), ())), preferred_element_type=jnp.float32
        )
        return (sqx[:, None] + sq_cols[None, :] - 2.0 * cross) / width

    def row_pass(gvals):

        def row_step(carry, index):
            start = index * block
            cost = tile(start)
            g_cols = lax.dynamic_slice_in_dim(gvals, start, block, 0)
            score = (g_cols[None, :] - cost) / blur
            top = jnp.max(score, 1)
            total = jnp.sum(jnp.exp(score - top[:, None]), 1)
            return (combine(carry, (top, total)), None)

        init = (jnp.full((rows,), -1e30, jnp.float32), jnp.zeros((rows,), jnp.float32))
        (top, total), _ = lax.scan(row_step, init, indices)
        return merge_over_col(top, total)

    def col_pass(fvals):

        def col_step(carry, index):
            cost = tile(index * block)
            score = (fvals[:, None] - cost) / blur
            top = jnp.max(score, 0)
            total = jnp.sum(jnp.exp(score - top[None, :]), 0)
            return (carry, (top, total))

        _, (top, total) = lax.scan(col_step, 0.0, indices)
        return merge_over_row(top.reshape(cols), total.reshape(cols))

    fvals = jnp.zeros((rows,), jnp.float32)
    gvals = jnp.zeros((cols,), jnp.float32)
    for step_index in range(ITERS):
        fvals = log_a - blur * row_pass(gvals)
        gvals = log_b - blur * col_pass(fvals)

    def final(carry, index):
        start = index * block
        cost = tile(start)
        g_cols = lax.dynamic_slice_in_dim(gvals, start, block, 0)
        score = (g_cols[None, :] - cost) / blur
        top = jnp.max(score, 1)
        shifted = jnp.exp(score - top[:, None])
        local = (top, jnp.sum(shifted, 1), jnp.sum(shifted * cost, 1))
        plan = jnp.exp((fvals[:, None] + g_cols[None, :] - cost) / blur)
        return (combine_three(carry, local), plan.astype(jnp.bfloat16))

    init = (
        jnp.full((rows,), -1e30, jnp.float32),
        jnp.zeros((rows,), jnp.float32),
        jnp.zeros((rows,), jnp.float32),
    )
    (top, shifted_mass, shifted_cost), plan_blocks = lax.scan(final, init, indices)
    high, shifted_mass, shifted_cost = combined_all(
        (top, shifted_mass, shifted_cost), "col", combine_three
    )
    reward = -shifted_cost / shifted_mass
    rowmass = jnp.exp(fvals / blur + high) * shifted_mass
    y_blocks = gathered_y.reshape(width, count, block)
    pulled = sum_at_owner(
        jnp.einsum("fkb,krb->fr", y_blocks, plan_blocks, preferred_element_type=jnp.float32),
        "col",
        0,
    )
    roll_pull = rowmass[None, :] * roll_embed.astype(jnp.float32) - pulled
    own_rows = expert_embed.shape[0]
    xsum = summed_rows(
        jnp.einsum(
            "fr,krb->fkb", gathered_x, plan_blocks, preferred_element_type=jnp.float32
        ).reshape(own_rows * lax.axis_size(ROW), cols),
        ROW,
    )
    expert_pull = expert_weight[None, :] * expert_embed.astype(jnp.float32) - xsum
    return (reward, roll_pull, expert_pull)


def solution(mesh):
    torus = Mesh(mesh.devices.reshape(8, 4, mesh.shape["col"]), ("row_0", "row_1", "col"))
    placed = (P("col", ROW), P(ROW, "col"), P(ROW), P("col"))
    return jax.shard_map(
        shards,
        mesh=torus,
        in_specs=placed,
        out_specs=(P(ROW), P("col", ROW), P(ROW, "col")),
        check_vma=False,
    )
```

profile of v0, /device:TPU:2, one launch (start us, length us, event | category | flops | bytes accessed | tf_op | source)
XLA Modules:
  0.0 330.4 jit_solution(5801021546625313387)
XLA Ops:
  7.2 14.4 %all_gather.6 = bf16[64,2048]{1,0:T(8,128)(2,1)} all-gather(bf16[16,2048]{1,0:T(8,128)(2,1)} %param.19), channel_id=1, replica_groups=mesh['row_0'=8,'row_1'=4,'col'=8] {'row_1'}, dimensions={0}, use_global_device_ids=true | all-gather | bytes 327680 | tf_op jit(solution)/shard_map/all_gather | solution.py:83
  21.7 1.6 broadcast_in_dim.56
  23.3 4.8 %all-to-all-start = ((bf16[8,64,384]{2,1,0:T(8,128)(2,1)}), bf16[8,64,384]{2,1,0:T(8,128)(2,1)S(1)}, u32[]{:S(2)}, u32[]{:S(2)}) async-start(bf16[8,64,384]{2,1,0:T(8,128)(2,1)} %broadcast_in_dim.56), calls=%async_computation | async-start | bytes 786432 | tf_op jit(solution)/shard_map/all_to_all | solution.py:16
  28.1 7.5 %all-to-all-done = bf16[8,64,384]{2,1,0:T(8,128)(2,1)S(1)} async-done(((bf16[8,64,384]{2,1,0:T(8,128)(2,1)}), bf16[8,64,384]{2,1,0:T(8,128)(2,1)S(1)}, u32[]{:S(2)}, u32[]{:S(2)}) %all-to-all-start) | async-done | bytes 393248 | tf_op jit(solution)/shard_map/all_to_all | solution.py:16
  35.7 28.5 %all-gather.2.cloned.1.call-done = bf16[512,2048]{1,0:T(8,128)(2,1)} async-done(((bf16[64,2048]{1,0:T(8,128)(2,1)}), bf16[512,2048]{1,0:T(8,128)(2,1)}) %all-gather.2.cloned.1.call-update) | async-done | bytes 2097168 | tf_op jit(solution)/shard_map/all_gather | solution.py:83
  64.2 2.2 multiply_reduce_fusion.1
  66.4 8.2 %while.95 = (s32[]{:T(128)}, f32[384]{0:T(512)S(1)}, f32[384]{0:T(512)S(1)}, f32[384]{0:T(512)S(1)}, s32[4]{0:T(128)S(1)}, /*index=5*/f32[2048]{0:T(1024)S(1)}, ...) while((s32[]{:T(128)}, f32[384]{0:T(512)S(1)}, ...), condition=%wide.region_5.6_spmd.clone, body=%wide.region_2.5_spmd.clone.sunk | while | flops 203098368 | bytes 2512585 | solution.py:161
  66.5 0.6 dynamic_slice.150
  68.5 0.6 dynamic_slice.150
  70.6 0.6 dynamic_slice.150
  72.6 0.6 dynamic_slice.150
  74.7 0.6 broadcast_in_dim.61
  75.3 4.8 %all-to-all-start.1 = ((f32[8,2,384]{2,1,0:T(2,128)}), f32[8,2,384]{2,1,0:T(2,128)S(1)}, u32[]{:S(2)}, u32[]{:S(2)}) async-start(f32[8,2,384]{2,1,0:T(2,128)} %broadcast_in_dim.61), calls=%async_computation.1 | async-start | bytes 49152 | tf_op jit(solution)/shard_map/all_to_all | solution.py:16
  80.1 3.9 %all-to-all-done.1 = f32[8,2,384]{2,1,0:T(2,128)S(1)} async-done(((f32[8,2,384]{2,1,0:T(2,128)}), f32[8,2,384]{2,1,0:T(2,128)S(1)}, u32[]{:S(2)}, u32[]{:S(2)}) %all-to-all-start.1) | async-done | bytes 24608 | tf_op jit(solution)/shard_map/all_to_all | solution.py:16
  84.4 8.4 %while.92 = (s32[]{:T(128)}, f32[4,512]{1,0:T(4,128)S(1)}, f32[4,512]{1,0:T(4,128)S(1)}, f32[384]{0:T(512)S(1)}, f32[384]{0:T(512)S(1)}, /*index=5*/s32[4]{0:T(1...) while((s32[]{:T(128)}, f32[4,512]{1,0:T(4,128)S(1)}, ...), condition=%wide.region_9.10_spmd, body=%wide.region_6.9_spmd.sunk | while | flops 203095040 | bytes 2515151 | solution.py:173
  84.4 0.6 dynamic_slice.141
  86.5 0.6 dynamic_slice.141
  88.6 0.6 dynamic_slice.141
  90.7 0.6 dynamic_slice.141
  92.8 1.0 broadcast_in_dim.62
  93.9 7.1 %all-to-all-start.2 = ((f32[32,2,2048]{2,1,0:T(2,128)}), f32[32,2,2048]{2,1,0:T(2,128)S(1)}, u32[]{:S(2)}, u32[]{:S(2)}) async-start(f32[32,2,2048]{2,1,0:T(2,128)} %broadcast_in_dim.62), calls=%async_computation.2 | async-start | bytes 1048576 | tf_op jit(solution)/shard_map/all_to_all | solution.py:16
  101.0 17.7 %all-to-all-done.2 = f32[32,2,2048]{2,1,0:T(2,128)S(1)} async-done(((f32[32,2,2048]{2,1,0:T(2,128)}), f32[32,2,2048]{2,1,0:T(2,128)S(1)}, u32[]{:S(2)}, u32[]{:S(2)}) %all-to-all-start.2) | async-done | bytes 524320 | tf_op jit(solution)/shard_map/all_to_all | solution.py:16
  120.2 8.5 %while.96 = (s32[]{:T(128)}, f32[384]{0:T(512)S(1)}, f32[384]{0:T(512)S(1)}, s32[4]{0:T(128)S(1)}, f32[2048]{0:T(1024)S(1)}, /*index=5*/f32[384]{0:T(512)S(1)}, ...) while((s32[]{:T(128)}, f32[384]{0:T(512)S(1)}, ...), condition=%wide.region_13.14_spmd.clone, body=%wide.region_10.13_spmd.clone.sunk | while | flops 203098368 | bytes 2518741 | solution.py:161
  120.2 0.6 dynamic_slice.153
  122.3 0.6 dynamic_slice.153
  126.6 0.6 dynamic_slice.153
  128.7 0.6 broadcast_in_dim.63
  129.3 4.7 %all-to-all-start.3 = ((f32[8,2,384]{2,1,0:T(2,128)}), f32[8,2,384]{2,1,0:T(2,128)S(1)}, u32[]{:S(2)}, u32[]{:S(2)}) async-start(f32[8,2,384]{2,1,0:T(2,128)} %broadcast_in_dim.63), calls=%async_computation.3 | async-start | bytes 49152 | tf_op jit(solution)/shard_map/all_to_all | solution.py:16
  134.0 4.0 %all-to-all-done.3 = f32[8,2,384]{2,1,0:T(2,128)S(1)} async-done(((f32[8,2,384]{2,1,0:T(2,128)}), f32[8,2,384]{2,1,0:T(2,128)S(1)}, u32[]{:S(2)}, u32[]{:S(2)}) %all-to-all-start.3) | async-done | bytes 24608 | tf_op jit(solution)/shard_map/all_to_all | solution.py:16
  138.4 8.4 %while.93 = (s32[]{:T(128)}, f32[4,512]{1,0:T(4,128)S(1)}, f32[4,512]{1,0:T(4,128)S(1)}, f32[384]{0:T(512)S(1)}, f32[384]{0:T(512)S(1)}, /*index=5*/s32[4]{0:T(1...) while((s32[]{:T(128)}, f32[4,512]{1,0:T(4,128)S(1)}, ...), condition=%wide.region_17.18_spmd, body=%wide.region_14.17_spmd.sunk | while | flops 203095040 | bytes 2515151 | solution.py:173
  138.4 0.6 dynamic_slice.144
  140.5 0.6 dynamic_slice.144
  144.6 0.6 dynamic_slice.144
  146.8 1.0 broadcast_in_dim.64
  147.8 4.7 %all-to-all-start.4 = ((f32[32,2,2048]{2,1,0:T(2,128)}), f32[32,2,2048]{2,1,0:T(2,128)S(1)}, u32[]{:S(2)}, u32[]{:S(2)}) async-start(f32[32,2,2048]{2,1,0:T(2,128)} %broadcast_in_dim.64), calls=%async_computation.4 | async-start | bytes 1048576 | tf_op jit(solution)/shard_map/all_to_all | solution.py:16
  152.5 17.7 %all-to-all-done.4 = f32[32,2,2048]{2,1,0:T(2,128)S(1)} async-done(((f32[32,2,2048]{2,1,0:T(2,128)}), f32[32,2,2048]{2,1,0:T(2,128)S(1)}, u32[]{:S(2)}, u32[]{:S(2)}) %all-to-all-start.4) | async-done | bytes 524320 | tf_op jit(solution)/shard_map/all_to_all | solution.py:16
  171.6 8.5 %while.97 = (s32[]{:T(128)}, f32[384]{0:T(512)S(1)}, f32[384]{0:T(512)S(1)}, s32[4]{0:T(128)S(1)}, f32[2048]{0:T(1024)S(1)}, /*index=5*/f32[384]{0:T(512)S(1)}, ...) while((s32[]{:T(128)}, f32[384]{0:T(512)S(1)}, ...), condition=%wide.region_21.22_spmd.clone, body=%wide.region_18.21_spmd.clone.sunk | while | flops 203098368 | bytes 2518741 | solution.py:161
  173.8 0.6 dynamic_slice.157
  175.9 0.6 dynamic_slice.157
  180.2 0.6 broadcast_in_dim.65
  180.8 4.7 %all-to-all-start.5 = ((f32[8,2,384]{2,1,0:T(2,128)}), f32[8,2,384]{2,1,0:T(2,128)S(1)}, u32[]{:S(2)}, u32[]{:S(2)}) async-start(f32[8,2,384]{2,1,0:T(2,128)} %broadcast_in_dim.65), calls=%async_computation.5 | async-start | bytes 49152 | tf_op jit(solution)/shard_map/all_to_all | solution.py:16
  185.5 4.0 %all-to-all-done.5 = f32[8,2,384]{2,1,0:T(2,128)S(1)} async-done(((f32[8,2,384]{2,1,0:T(2,128)}), f32[8,2,384]{2,1,0:T(2,128)S(1)}, u32[]{:S(2)}, u32[]{:S(2)}) %all-to-all-start.5) | async-done | bytes 24608 | tf_op jit(solution)/shard_map/all_to_all | solution.py:16
  189.8 8.4 %while.94 = (s32[]{:T(128)}, f32[4,512]{1,0:T(4,128)S(1)}, f32[4,512]{1,0:T(4,128)S(1)}, f32[384]{0:T(512)S(1)}, f32[384]{0:T(512)S(1)}, /*index=5*/s32[4]{0:T(1...) while((s32[]{:T(128)}, f32[4,512]{1,0:T(4,128)S(1)}, ...), condition=%wide.region_25.26_spmd, body=%wide.region_22.25_spmd.sunk | while | flops 203095040 | bytes 2515151 | solution.py:173
  198.2 1.0 broadcast_in_dim.66
  199.3 4.7 %all-to-all-start.6 = ((f32[32,2,2048]{2,1,0:T(2,128)}), f32[32,2,2048]{2,1,0:T(2,128)S(1)}, u32[]{:S(2)}, u32[]{:S(2)}) async-start(f32[32,2,2048]{2,1,0:T(2,128)} %broadcast_in_dim.66), calls=%async_computation.6 | async-start | bytes 1048576 | tf_op jit(solution)/shard_map/all_to_all | solution.py:16
  204.2 17.4 %all-to-all-done.6 = f32[32,2,2048]{2,1,0:T(2,128)S(1)} async-done(((f32[32,2,2048]{2,1,0:T(2,128)}), f32[32,2,2048]{2,1,0:T(2,128)S(1)}, u32[]{:S(2)}, u32[]{:S(2)}) %all-to-all-start.6) | async-done | bytes 524320 | tf_op jit(solution)/shard_map/all_to_all | solution.py:16
  223.1 13.1 %while.98 = (s32[]{:T(128)}, f32[384]{0:T(512)S(1)}, f32[384]{0:T(512)S(1)}, f32[384]{0:T(512)S(1)}, bf16[4,384,512]{1,2,0:T(8,128)(2,1)}, /*index=5*/s32[4]{0:T...) while((s32[]{:T(128)}, f32[384]{0:T(512)S(1)}, ...), condition=%wide.region_30.31_spmd.clone, body=%wide.region_26.30_spmd.clone.sunk | while | flops 204673536 | bytes 3717874 | solution.py:198
  225.4 1.0 fusion.141
  228.6 1.0 fusion.141
  231.9 1.0 fusion.141
  235.2 1.0 fusion.141
  236.2 4.7 %fusion.90 = f32[4,512,512]{2,1,0:T(8,128)} fusion(bf16[4,384,512]{1,2,0:T(8,128)(2,1)} %get-tuple-element.366, bf16[512,384,1]{1,0,2:T(8,128)(2,1)S(1)} %bitcast.214), kind=kOutput, calls=%fused_computation.206 | convolution fusion | flops 805306368 | bytes 6160384 | tf_op jit(solution)/shard_map/fr,krb->fkb/dot_general | solution.py:213
  240.9 5.4 %copy.58 = f32[512,2048]{1,0:T(8,128)} copy(f32[512,2048]{0,1:T(8,128)} %bitcast.212) | data formatting | bytes 8388608 | tf_op jit(solution)/shard_map/reshape | solution.py:215
  246.2 2.5 copy.54
  248.8 0.6 broadcast_in_dim.67
  249.4 4.7 %all-to-all-start.7 = ((f32[8,3,384]{2,1,0:T(4,128)}), f32[8,3,384]{2,1,0:T(4,128)S(1)}, u32[]{:S(2)}, u32[]{:S(2)}) async-start(f32[8,3,384]{2,1,0:T(4,128)} %broadcast_in_dim.67), calls=%async_computation.7 | async-start | bytes 98304 | tf_op jit(solution)/shard_map/all_to_all | solution.py:16
  254.1 3.1 convolution_bitcast_fusion
  257.2 1.1 copy.57
  258.4 4.9 %all-to-all-start.8 = ((f32[8,64,384]{2,1,0:T(8,128)}), f32[8,64,384]{2,1,0:T(8,128)S(1)}, u32[]{:S(2)}, u32[]{:S(2)}) async-start(f32[8,64,384]{2,1,0:T(8,128)} %bitcast.31), calls=%async_computation.8 | async-start | bytes 1572864 | tf_op jit(solution)/shard_map/all_to_all | solution.py:95
  263.5 33.4 %reduce-scatter.3.cloned.1.call-done = f32[64,2048]{1,0:T(8,128)} async-done(((f32[512,2048]{1,0:T(8,128)}), f32[64,2048]{1,0:T(8,128)}) %reduce-scatter.3.cloned.1.call-update) | async-done | bytes 524304 | tf_op jit(solution)/shard_map/reduce_scatter | solution.py:101
  297.2 0.6 exponential_multiply_fusion
  297.8 0.7 multiply_subtract_fusion.1
  298.5 23.8 %reduce-scatter.5.cloned.1.call-done = f32[16,2048]{1,0:T(8,128)} async-done(((f32[64,2048]{1,0:T(8,128)}), f32[16,2048]{1,0:T(8,128)}) %reduce-scatter.5.cloned.1.call-update) | async-done | bytes 131088 | tf_op jit(solution)/shard_map/reduce_scatter | solution.py:101
  322.3 1.6 multiply_subtract_fusion
  (361 shorter events, 37.1 us)
Async XLA Ops:
  7.2 57.1 %all-gather.2.cloned.1.call-start = ((), (), s32[]{:S(2)}) async-start(), calls=%async_computation.11 | async-start | bytes 2359296 | tf_op jit(solution)/shard_map/all_gather | solution.py:83
  23.3 12.3 %all-to-all-start = ((bf16[8,64,384]{2,1,0:T(8,128)(2,1)}), bf16[8,64,384]{2,1,0:T(8,128)(2,1)S(1)}, u32[]{:S(2)}, u32[]{:S(2)}) async-start(bf16[8,64,384]{2,1,0:T(8,128)(2,1)} %broadcast_in_dim.56), calls=%async_computation | async-start | bytes 786432 | tf_op jit(solution)/shard_map/all_to_all | solution.py:16
  64.2 2.2 copy-start
  66.4 17.9 %copy-start.4 = (f32[384]{0:T(512)S(1)}, f32[384]{0:T(512)}, u32[]{:S(2)}) copy-start(f32[384]{0:T(512)} %param.20) | copy-start | bytes 4612
  75.3 8.7 %all-to-all-start.1 = ((f32[8,2,384]{2,1,0:T(2,128)}), f32[8,2,384]{2,1,0:T(2,128)S(1)}, u32[]{:S(2)}, u32[]{:S(2)}) async-start(f32[8,2,384]{2,1,0:T(2,128)} %broadcast_in_dim.61), calls=%async_computation.1 | async-start | bytes 49152 | tf_op jit(solution)/shard_map/all_to_all | solution.py:16
  93.9 24.8 %all-to-all-start.2 = ((f32[32,2,2048]{2,1,0:T(2,128)}), f32[32,2,2048]{2,1,0:T(2,128)S(1)}, u32[]{:S(2)}, u32[]{:S(2)}) async-start(f32[32,2,2048]{2,1,0:T(2,128)} %broadcast_in_dim.62), calls=%async_computation.2 | async-start | bytes 1048576 | tf_op jit(solution)/shard_map/all_to_all | solution.py:16
  119.2 0.9 copy-start.3
  129.3 8.7 %all-to-all-start.3 = ((f32[8,2,384]{2,1,0:T(2,128)}), f32[8,2,384]{2,1,0:T(2,128)S(1)}, u32[]{:S(2)}, u32[]{:S(2)}) async-start(f32[8,2,384]{2,1,0:T(2,128)} %broadcast_in_dim.63), calls=%async_computation.3 | async-start | bytes 49152 | tf_op jit(solution)/shard_map/all_to_all | solution.py:16
  147.8 22.4 %all-to-all-start.4 = ((f32[32,2,2048]{2,1,0:T(2,128)}), f32[32,2,2048]{2,1,0:T(2,128)S(1)}, u32[]{:S(2)}, u32[]{:S(2)}) async-start(f32[32,2,2048]{2,1,0:T(2,128)} %broadcast_in_dim.64), calls=%async_computation.4 | async-start | bytes 1048576 | tf_op jit(solution)/shard_map/all_to_all | solution.py:16
  180.8 8.7 %all-to-all-start.5 = ((f32[8,2,384]{2,1,0:T(2,128)}), f32[8,2,384]{2,1,0:T(2,128)S(1)}, u32[]{:S(2)}, u32[]{:S(2)}) async-start(f32[8,2,384]{2,1,0:T(2,128)} %broadcast_in_dim.65), calls=%async_computation.5 | async-start | bytes 49152 | tf_op jit(solution)/shard_map/all_to_all | solution.py:16
  199.3 22.3 %all-to-all-start.6 = ((f32[32,2,2048]{2,1,0:T(2,128)}), f32[32,2,2048]{2,1,0:T(2,128)S(1)}, u32[]{:S(2)}, u32[]{:S(2)}) async-start(f32[32,2,2048]{2,1,0:T(2,128)} %broadcast_in_dim.66), calls=%async_computation.6 | async-start | bytes 1048576 | tf_op jit(solution)/shard_map/all_to_all | solution.py:16
  204.0 93.0 %reduce-scatter.3.cloned.1.call-start = ((), (), s32[]{:S(2)}) async-start(), calls=%async_computation.12 | async-start | bytes 4718592 | tf_op jit(solution)/shard_map/reduce_scatter | solution.py:101
  249.4 9.0 %all-to-all-start.7 = ((f32[8,3,384]{2,1,0:T(4,128)}), f32[8,3,384]{2,1,0:T(4,128)S(1)}, u32[]{:S(2)}, u32[]{:S(2)}) async-start(f32[8,3,384]{2,1,0:T(4,128)} %broadcast_in_dim.67), calls=%async_computation.7 | async-start | bytes 98304 | tf_op jit(solution)/shard_map/all_to_all | solution.py:16
  258.4 39.5 %copy-start.2 = (bf16[64,384]{1,0:T(8,128)(2,1)S(1)}, bf16[64,384]{1,0:T(8,128)(2,1)}, u32[]{:S(2)}) copy-start(bf16[64,384]{1,0:T(8,128)(2,1)} %param.18) | copy-start | bytes 147460
  258.4 64.0 %copy-start.1 = (bf16[16,2048]{1,0:T(8,128)(2,1)S(1)}, bf16[16,2048]{1,0:T(8,128)(2,1)}, u32[]{:S(2)}) copy-start(bf16[16,2048]{1,0:T(8,128)(2,1)} %param.19) | copy-start | bytes 196612
  258.4 39.4 %all-to-all-start.8 = ((f32[8,64,384]{2,1,0:T(8,128)}), f32[8,64,384]{2,1,0:T(8,128)S(1)}, u32[]{:S(2)}, u32[]{:S(2)}) async-start(f32[8,64,384]{2,1,0:T(8,128)} %bitcast.31), calls=%async_computation.8 | async-start | bytes 1572864 | tf_op jit(solution)/shard_map/all_to_all | solution.py:95
  263.3 59.0 %reduce-scatter.5.cloned.1.call-start = ((), (), s32[]{:S(2)}) async-start(), calls=%async_computation.13 | async-start | bytes 655360 | tf_op jit(solution)/shard_map/reduce_scatter | solution.py:101
Sparse Core Ops, SparseCore 0:
  21.8 42.3 all-gather.1
  246.4 50.5 reduce-scatter.2
  299.5 22.8 reduce-scatter.4
where the time goes:
time: 332 us; the launch traced here: 330 us
  waiting for transfers between devices  158 us (48%)
  starting transfers between devices  45.4 us (14%)
  local copies, waits for them, and re-layouts  41.2 us (12%)
  matrix products  22.3 us (7%)
  loops' own time  19 us (6%)
  other arithmetic  15.6 us (5%)
  between operations  14.6 us (4%)
  blocking collectives  14.4 us (4%)
    all_to_all x8, waiting for transfers between devices, sent_to_all(): lax.all_to_all(jnp.broadcast_to(x[None], (peers, *x.shape)), axis, 0, 0,...  72.1 us
    reduce_scatter x2, waiting for transfers between devices, summed_rows(): total = lax.psum_scatter(total, axis, scatter_dimension=0, tiled=True)  57.2 us
    all_to_all x8, starting transfers between devices, sent_to_all(): lax.all_to_all(jnp.broadcast_to(x[None], (peers, *x.shape)), axis, 0, 0,...  40.2 us
    all_gather x1, waiting for transfers between devices, gather_axes(): filled = lax.all_gather(filled, axes[number], axis=dim, tiled=True)  28.5 us
    dynamic_slice x28, local copies, waits for them, and re-layouts, row_pass(): (top, total), _ = lax.scan(row_step, init, indices)  16.4 us
    dot_general x28, matrix products, tile(): lax.dot_general(gathered_x, ycols, (((0,), (0,)), ((), ())), preferred_el...  14.5 us
    all_gather x1, blocking collectives, gather_axes(): filled = lax.all_gather(filled, axes[number], axis=dim, tiled=True)  14.4 us
    another operation x3, loops' own time, col_pass(): _, (top, total) = lax.scan(col_step, 0.0, indices)  8.16 us
  transfers between devices with their start and end apart: 12, of which 10 were waited for; matrix products, arithmetic and copies ran while one was open for 3% of the time, Pallas kernels for 0%

commit v1 on v0

v1 whole, which is shorter than its diff:
```python
import functools
import math

import jax
import jax.numpy as jnp
from jax import lax
from jax.experimental import pallas as pl
from jax.experimental.pallas import tpu as pltpu
from jax.sharding import Mesh
from jax.sharding import PartitionSpec as P

ITERS = 3
BLUR = 0.05
LOG2E = 1.0 / math.log(2.0)
F32 = jnp.float32
BF16 = jnp.bfloat16
LANES = 128
STEP = 64


def cdiv(a, b):
    return -(-a // b)


def padded(n, m):
    return cdiv(n, m) * m


def log2_of(x):
    return jnp.log(x) * LOG2E


def merged(parts):
    high = jnp.max(parts, axis=0)
    return high + log2_of(jnp.sum(jnp.exp2(parts - high[None]), axis=0))


def rows_of_tiles(vec, tiles):
    return [vec[:, t * LANES : (t + 1) * LANES] for t in range(tiles)]


def to_column(lines, column_ref, tiles):
    for t in range(tiles):
        wide = jnp.broadcast_to(lines[t : t + 1, :], (LANES, LANES))
        column_ref[t * LANES : (t + 1) * LANES, :] = wide.T


def row_sweep(d_ref, column_ref, lines_ref):
    cols = d_ref.shape[0]
    chunks = cols // STEP
    tiles = d_ref.shape[1] // LANES

    def one(t, carry):
        lanes = pl.ds(pl.multiple_of(t * LANES, LANES), LANES)

        def score(c):
            at = slice(c * STEP, (c + 1) * STEP)
            return column_ref[at, :] + d_ref[at, lanes]

        top = score(0)
        for c in range(1, chunks):
            top = jnp.maximum(top, score(c))
        top = jnp.max(top, axis=0, keepdims=True)
        total = jnp.exp2(score(0) - top)
        for c in range(1, chunks):
            total = total + jnp.exp2(score(c) - top)
        total = jnp.sum(total, axis=0, keepdims=True)
        lines_ref[pl.ds(t, 1), :] = top + log2_of(total)
        return carry

    lax.fori_loop(0, tiles, one, 0)


def column_sweep(d_ref, lines, column_ref):
    cols = d_ref.shape[0]
    tiles = d_ref.shape[1] // LANES

    def one(c, carry):
        at = pl.ds(pl.multiple_of(c * STEP, STEP), STEP)

        def score(t):
            return lines[t : t + 1, :] + d_ref[at, t * LANES : (t + 1) * LANES]

        top = score(0)
        for t in range(1, tiles):
            top = jnp.maximum(top, score(t))
        top = jnp.max(top, axis=1, keepdims=True)
        total = jnp.exp2(score(0) - top)
        for t in range(1, tiles):
            total = total + jnp.exp2(score(t) - top)
        total = jnp.sum(total, axis=1, keepdims=True)
        column_ref[at, :] = jnp.broadcast_to(top + log2_of(total), (STEP, LANES))
        return carry

    lax.fori_loop(0, cols // STEP, one, 0)


def from_column(column_ref, lines_ref, tiles):
    for t in range(tiles):
        square = column_ref[t * LANES : (t + 1) * LANES, :].T
        lines_ref[t : t + 1, :] = square[0:1, :]


def setup_kernel(scale, here_ref, own_ref, other_ref, y_ref, la_ref, d_ref, sqx_ref, sqy_ref, out_ref,
                 x_ref, yc_ref, column_ref, lines_ref):
    core = here_ref[0]
    nrow, ncol = own_ref.shape[0], own_ref.shape[1]
    depth, width = own_ref.shape[2], own_ref.shape[3]
    yc_ref[...] = y_ref[...]
    for r in range(nrow):
        for c in range(ncol):
            mine = pl.multiple_of((2 * c + core) * depth, depth)
            theirs = pl.multiple_of((2 * c + 1 - core) * depth, depth)
            x_ref[pl.ds(mine, depth), r * width : (r + 1) * width] = own_ref[r, c]
            x_ref[pl.ds(theirs, depth), r * width : (r + 1) * width] = other_ref[r, c]
    tiles = x_ref.shape[1] // LANES
    sqx_ref[...] = jnp.zeros_like(sqx_ref)
    for t in range(tiles):
        part = x_ref[:, t * LANES : (t + 1) * LANES].astype(F32)
        sqx_ref[t : t + 1, :] = jnp.sum(part * part, axis=0, keepdims=True)
    ctiles = y_ref.shape[1] // LANES
    lines_ref[...] = jnp.zeros_like(lines_ref)
    for t in range(ctiles):
        part = y_ref[:, t * LANES : (t + 1) * LANES].astype(F32)
        lines_ref[t : t + 1, :] = jnp.sum(part * part, axis=0, keepdims=True)
    to_column(lines_ref[...], column_ref, ctiles)
    sqy_ref[...] = column_ref[...]
    column_ref[...] = column_ref[...] * (-0.5 * scale)
    for r in range(nrow):
        cross = lax.dot_general(
            y_ref[...], x_ref[:, r * width : (r + 1) * width], (((0,), (0,)), ((), ())),
            preferred_element_type=F32)
        d_ref[:, r * width : (r + 1) * width] = cross * scale
    lines_ref[...] = jnp.zeros_like(lines_ref)
    row_sweep(d_ref, column_ref, lines_ref)
    wtiles = width // LANES
    lines_ref[tiles : tiles + wtiles, :] = la_ref[0:wtiles, :]
    out_ref[...] = jnp.broadcast_to(lines_ref[...][None], out_ref.shape)


def row_kernel(parts_ref, lb_ref, d_ref, out_ref, column_ref, lines_ref):
    ctiles = d_ref.shape[0] // LANES
    g = lb_ref[...] - merged(parts_ref[...])
    to_column(g, column_ref, ctiles)
    lines_ref[...] = jnp.zeros_like(lines_ref)
    row_sweep(d_ref, column_ref, lines_ref)
    out_ref[...] = jnp.broadcast_to(lines_ref[...][None], out_ref.shape)


def column_kernel(parts_ref, la_ref, d_ref, f_ref, out_ref, column_ref, lines_ref):
    ctiles = d_ref.shape[0] // LANES
    f = la_ref[...] - merged(parts_ref[...])
    f_ref[...] = f
    column_sweep(d_ref, f, column_ref)
    lines_ref[...] = jnp.zeros_like(lines_ref)
    from_column(column_ref, lines_ref, ctiles)
    out_ref[...] = jnp.broadcast_to(lines_ref[...][None], out_ref.shape)


def three_pieces(v):
    high = v.astype(BF16)
    rest = v - high.astype(F32)
    mid = rest.astype(BF16)
    low = (rest - mid.astype(F32)).astype(BF16)
    return high, mid, low


def put_pieces(block_ref, at, values):
    block_ref[at] = jnp.zeros_like(block_ref[at])
    row = at[-1].start
    for n, v in enumerate(values):
        for m, piece in enumerate(three_pieces(v)):
            block_ref[at[:-1] + (slice(row + 3 * n + m, row + 3 * n + m + 1),)] = piece


def pieces_sum(block, row, n):
    return (
        block[row + 3 * n : row + 3 * n + 1].astype(F32)
        + block[row + 3 * n + 1 : row + 3 * n + 2].astype(F32)
        + block[row + 3 * n + 2 : row + 3 * n + 3].astype(F32)
    )


def plan_kernel(scale, emb, grid, here_ref, parts_ref, lb_ref, f_ref, sqx_ref, sqy_ref, d_ref, y_ref, x_ref,
                keep_ref, send_ref, sums_ref, xsum_ref, column_ref, plan_ref, ys_ref, lines_ref):
    core = here_ref[0]
    nrow, ncol, depth, width = grid
    cols, rows = d_ref.shape
    ctiles, tiles, chunks = cols // LANES, rows // LANES, cols // STEP
    g = lb_ref[...] - merged(parts_ref[...])
    to_column(g, column_ref, ctiles)
    back = 1.0 / emb
    unit = 2.0 / (emb * scale)

    def one(t, carry):
        lanes = pl.ds(pl.multiple_of(t * LANES, LANES), LANES)
        f = f_ref[pl.ds(t, 1), :]
        sq = sqx_ref[pl.ds(t, 1), :]
        mass = jnp.zeros((STEP, LANES), F32)
        paid = jnp.zeros((STEP, LANES), F32)
        for c in range(chunks):
            at = slice(c * STEP, (c + 1) * STEP)
            d = d_ref[at, lanes]
            p = jnp.exp2(column_ref[at, :] + d + f)
            plan_ref[at, lanes] = p.astype(BF16)
            mass = mass + p
            paid = paid + p * ((sq + sqy_ref[at, :]) * back - d * unit)
        lines_ref[0, pl.ds(t, 1), :] = jnp.sum(mass, axis=0, keepdims=True)
        lines_ref[1, pl.ds(t, 1), :] = jnp.sum(paid, axis=0, keepdims=True)
        return carry

    lax.fori_loop(0, tiles, one, 0)
    sums_ref[...] = jnp.zeros_like(sums_ref)
    wtiles = width // LANES
    for r in range(nrow):
        for w in range(wtiles):
            t = r * wtiles + w
            for n in range(2):
                sums_ref[r, n : n + 1, w * LANES : (w + 1) * LANES] = lines_ref[n, t : t + 1, :]
    for c in range(ncol):
        mine = pl.multiple_of((2 * c + core) * depth, depth)
        theirs = pl.multiple_of((2 * c + 1 - core) * depth, depth)
        ys_ref[c * depth : (c + 1) * depth, :] = y_ref[pl.ds(mine, depth), :]
        ys_ref[(ncol + c) * depth : (ncol + c + 1) * depth, :] = y_ref[pl.ds(theirs, depth), :]
    half = ncol * depth
    for r in range(nrow):
        part = plan_ref[:, r * width : (r + 1) * width]
        keep_ref[r] = lax.dot_general(
            ys_ref[:half, :], part, (((1,), (0,)), ((), ())), preferred_element_type=F32)
        send = lax.dot_general(
            ys_ref[half:, :], part, (((1,), (0,)), ((), ())), preferred_element_type=F32)
        send_ref[r, :half] = send.astype(BF16)
        put_pieces(send_ref, (r, slice(half, half + 16)), [sums_ref[r, n : n + 1] for n in range(2)])
    xsum = lax.dot_general(x_ref[...], plan_ref[...], (((1,), (1,)), ((), ())), preferred_element_type=F32)
    xsum_ref[...] = xsum.astype(BF16)


def pair_kernel(keep_ref, sums_ref, got_ref, out_ref):
    nrow, ncol, deep, width = out_ref.shape
    depth = deep - 16
    half = ncol * depth
    for r in range(nrow):
        extra = got_ref[r, half : half + 16]
        totals = [sums_ref[r, n : n + 1] + pieces_sum(extra, 0, n) for n in range(2)]
        for c in range(ncol):
            at = slice(c * depth, (c + 1) * depth)
            out_ref[r, c, :depth] = (keep_ref[r, at] + got_ref[r, at].astype(F32)).astype(BF16)
            put_pieces(out_ref, (r, c, slice(depth, depth + 16)), totals)


def roll_kernel(got_ref, x_ref, pull_ref, reward_ref):
    depth = x_ref.shape[0]
    total = got_ref[0].astype(F32)
    for k in range(1, got_ref.shape[0]):
        total = total + got_ref[k].astype(F32)
    mass = total[depth : depth + 1] + total[depth + 1 : depth + 2] + total[depth + 2 : depth + 3]
    paid = total[depth + 3 : depth + 4] + total[depth + 4 : depth + 5] + total[depth + 5 : depth + 6]
    reward_ref[...] = -paid / mass
    pull_ref[...] = mass * x_ref[...].astype(F32) - total[:depth]


def expert_kernel(got_ref, y_ref, b_ref, pull_ref):
    nz, ny, _, cols = got_ref.shape
    for q in range(ny):
        total = got_ref[0, q].astype(F32)
        for k in range(1, nz):
            total = total + got_ref[k, q].astype(F32)
        at = slice(q * cols, (q + 1) * cols)
        pull_ref[:, at] = b_ref[:, at] * y_ref[:, at].astype(F32) - total


def call(body, outs, scratch, *args, smem=0, limit=None):
    spec = pl.BlockSpec(memory_space=pltpu.VMEM)
    scalar = pl.BlockSpec(memory_space=pltpu.SMEM)
    return pl.pallas_call(
        body,
        out_shape=[jax.ShapeDtypeStruct(s, t) for s, t in outs],
        in_specs=[scalar] * smem + [spec] * (len(args) - smem),
        out_specs=[spec] * len(outs),
        scratch_shapes=[pltpu.VMEM(s, t) for s, t in scratch],
        compiler_params=pltpu.CompilerParams(vmem_limit_bytes=limit),
    )(*args)


def exchanged(x, axes):
    return lax.all_to_all(x, axes, split_axis=0, concat_axis=0, tiled=True)


def as_lines(v, lines):
    count = v.shape[0] // LANES
    return jnp.pad(v.reshape(count, LANES), ((0, lines - count), (0, 0)))


def swapped(x):
    return lax.ppermute(x, "core", [(0, 1), (1, 0)])


def shards(roll_embed, expert_embed, roll_weight, expert_weight):
    nz, ny, nx, nk = (lax.axis_size(a) for a in ("z", "y", "x", "core"))
    depth, width = roll_embed.shape
    thin, wide = expert_embed.shape
    emb = thin * nz * ny
    cols = wide // ny
    rows = width * ny
    scale = 2.0 * LOG2E / (emb * BLUR)
    core = lax.axis_index("core").astype(jnp.int32).reshape(1)
    quarter = lax.axis_index("y")

    y_blocks = jnp.moveaxis(expert_embed.reshape(thin, ny, cols), 1, 0)
    y_send = jnp.broadcast_to(y_blocks[None], (nz, ny, thin, cols)).reshape(nz * ny, thin, cols)
    x_send = jnp.broadcast_to(roll_embed[None], (ny * nx, depth, width))
    x_got = exchanged(x_send, ("y", "x"))
    x_other = swapped(x_got)
    y_all = exchanged(y_send, ("z", "y")).reshape(emb, cols)
    x_own = x_got.reshape(ny, nx, depth, width)
    x_other = x_other.reshape(ny, nx, depth, width)

    wtiles = width // LANES
    f_lines = padded(rows // LANES + wtiles, 8)
    g_lines = padded(cols // LANES, 8)
    la_own = as_lines(log2_of(roll_weight), 8)
    lb = as_lines(log2_of(lax.dynamic_slice_in_dim(expert_weight, quarter * cols, cols, 0)), g_lines)
    crowd = ny * nx * nk

    column = ((cols, LANES), F32)
    f_shape, g_shape = (crowd, f_lines, LANES), (nz, g_lines, LANES)
    d, sqx, sqy, out, x_all, y_all = call(
        functools.partial(setup_kernel, scale),
        [((cols, rows), F32), ((f_lines, LANES), F32), column, (f_shape, F32),
         ((emb, rows), BF16), ((emb, cols), BF16)],
        [column, ((f_lines, LANES), F32)],
        core, x_own, x_other, y_all, la_own, smem=1, limit=24 << 20)
    la = None
    for step in range(ITERS):
        if step:
            (out,) = call(row_kernel, [(f_shape, F32)], [column, ((f_lines, LANES), F32)],
                          got, lb, d, limit=12 << 20)
        got = exchanged(out, ("y", "x", "core"))
        if step == 0:
            firsts = got.reshape(ny, nx * nk, f_lines, LANES)[:, 0, rows // LANES : rows // LANES + wtiles]
            la = jnp.pad(firsts.reshape(rows // LANES, LANES), ((0, f_lines - rows // LANES), (0, 0)))
        f, out = call(column_kernel, [((f_lines, LANES), F32), (g_shape, F32)],
                      [column, ((g_lines, LANES), F32)], got, la, d, limit=12 << 20)
        got = exchanged(out, ("z",))

    grid = (ny, nx, depth, width)
    keep, send, sums, xsum = call(
        functools.partial(plan_kernel, scale, emb, grid),
        [((ny, nx * depth, width), F32), ((ny, nx * depth + 16, width), BF16), ((ny, 8, width), F32),
         ((emb, cols), BF16)],
        [column, ((cols, rows), BF16), ((emb, cols), BF16), ((2, f_lines, LANES), F32)],
        core, got, lb, f, sqx, sqy, d, y_all, x_all, smem=1, limit=32 << 20)
    xsum_got = exchanged(xsum.reshape(nz * ny, thin, cols), ("z", "y"))
    (pairs,) = call(pair_kernel, [((ny, nx, depth + 16, width), BF16)], [], keep, sums, swapped(send),
                    limit=16 << 20)
    pull_got = exchanged(pairs.reshape(ny * nx, depth + 16, width), ("y", "x"))
    (expert_pull,) = call(expert_kernel, [((thin, wide), F32)], [],
                          xsum_got.reshape(nz, ny, thin, cols), expert_embed, expert_weight.reshape(1, wide),
                          limit=8 << 20)
    roll_pull, reward = call(roll_kernel, [((depth, width), F32), ((1, width), F32)], [],
                             pull_got, roll_embed, limit=8 << 20)
    reward = reward.reshape(width)
    return (reward, roll_pull, expert_pull)


def solution(mesh):
    z, y = 8, 4
    torus = Mesh(mesh.devices.reshape(z, y, 4, 2), ("z", "y", "x", "core"))
    row, col = ("z", "y"), ("x", "core")
    return jax.shard_map(
        shards,
        mesh=torus,
        in_specs=(P(col, row), P(row, col), P(row), P(col)),
        out_specs=(P(row), P(col, row), P(row, col)),
        check_vma=False,
    )
```

time: 332 us -> 193 us (0.58)
  waiting for transfers between devices: 158 us -> 72.6 us
  blocking collectives: 14.4 us -> 45.6 us
  local copies, waits for them, and re-layouts: 41.2 us -> 15.6 us
  matrix products: 22.3 us -> 0 us
  Pallas kernels: 0 us -> 20.2 us
  loops' own time: 19 us -> 0 us
  other arithmetic: 15.6 us -> 0.69 us
  between operations: 14.6 us -> 0.83 us
  starting transfers between devices: 45.4 us -> 36.9 us
    reduce_scatter x2 -> x0, waiting for transfers between devices: 57.2 us -> none  [summed_rows(): total = lax.psum_scatter(total, axis, scatter_dimension=0, tiled=True)]
    all_to_all x0 -> x4, blocking collectives: none -> 45.6 us  [exchanged(): return lax.all_to_all(x, axes, split_axis=0, concat_axis=0, tiled=True)]
    all_gather x1 -> x0, waiting for transfers between devices: 28.5 us -> none  [gather_axes(): filled = lax.all_gather(filled, axes[number], axis=dim, tiled=True)]
    dot_general x30 -> x0, matrix products: 22.3 us -> none  [the longest x28 14.5 us: tile(): lax.dot_general(gathered_x, ycols, (((0,), (0,)), ((), ())), preferred_el...]
    pallas_call x0 -> x10, Pallas kernels: none -> 20.2 us  [call(): pl.pallas_call(body, out_shape=[jax.ShapeDtypeStruct(s, t) for s, t in ou...]
    dynamic_slice x68 -> x0, local copies, waits for them, and re-layouts: 19.5 us -> none  [the longest x28 16.4 us: row_pass(): (top, total), _ = lax.scan(row_step, init, indices)]
    another operation x7 -> x0, loops' own time: 19 us -> none  [the longest x3 8.16 us: col_pass(): _, (top, total) = lax.scan(col_step, 0.0, indices)]
    all_gather x1 -> x0, blocking collectives: 14.4 us -> none  [gather_axes(): filled = lax.all_gather(filled, axes[number], axis=dim, tiled=True)]
  transfers between devices with their start and end apart: 12 -> 8, of which waited for: 10 -> 7; matrix products, arithmetic and copies ran while one was open for 3% -> 0% of each run, Pallas kernels for 0% -> 1%
where the time goes in v1:
time: 193 us; the launch traced here: 192 us
  waiting for transfers between devices  72.6 us (38%)
  blocking collectives  45.6 us (24%)
  starting transfers between devices  36.9 us (19%)
  Pallas kernels  20.2 us (10%)
  local copies, waits for them, and re-layouts  15.6 us (8%)
    all_to_all x6, waiting for transfers between devices, exchanged(): return lax.all_to_all(x, axes, split_axis=0, concat_axis=0, tiled=True)  70.1 us
    all_to_all x4, blocking collectives, exchanged(): return lax.all_to_all(x, axes, split_axis=0, concat_axis=0, tiled=True)  45.6 us
    all_to_all x6, starting transfers between devices, exchanged(): return lax.all_to_all(x, axes, split_axis=0, concat_axis=0, tiled=True)  36.7 us
    pallas_call x10, Pallas kernels, call(): pl.pallas_call(body, out_shape=[jax.ShapeDtypeStruct(s, t) for s, t in ou...  20.2 us
    unnamed x43, local copies, waits for them, and re-layouts  12.8 us
  transfers between devices with their start and end apart: 8, of which 7 were waited for; matrix products, arithmetic and copies ran while one was open for 0% of the time, Pallas kernels for 1%

profile of v1, /device:TPU:2, one launch (start us, length us, event | category | flops | bytes accessed | tf_op | source)
XLA Modules:
  0.0 192.4 jit_solution(3668693935273780845)
XLA Ops:
  0.6 0.0 copy-start.15
  0.6 1.8 broadcast_in_dim.4
  2.5 0.0 copy-start.20
  2.5 7.6 %all-to-all-start = ((bf16[16,64,384]{2,1,0:T(8,128)(2,1)}), bf16[16,64,384]{2,1,0:T(8,128)(2,1)S(1)}, u32[]{:S(2)}, u32[]{:S(2)}) async-start(bf16[16,64,384]{2,1,0:T(8,128)(2,1)} %broadcast_in_dim.4), calls=%async_computation | async-start | bytes 1572864 | tf_op jit(solution)/shard_map/all_to_all | solution.py:286
  10.1 0.0 copy-done.15
  10.1 12.9 %all-to-all-done = bf16[16,64,384]{2,1,0:T(8,128)(2,1)S(1)} async-done(((bf16[16,64,384]{2,1,0:T(8,128)(2,1)}), bf16[16,64,384]{2,1,0:T(8,128)(2,1)S(1)}, u32[]{:S(2)}, u32[]{:S(2)}) %all-to-all-start) | async-done | bytes 786464 | tf_op jit(solution)/shard_map/all_to_all | solution.py:286
  23.1 0.9 broadcast_in_dim.5
  24.0 9.1 %all-to-all-start.1 = ((bf16[32,16,512]{2,1,0:T(8,128)(2,1)}), bf16[32,16,512]{2,1,0:T(8,128)(2,1)S(1)}, u32[]{:S(2)}, u32[]{:S(2)}) async-start(bf16[32,16,512]{2,1,0:T(8,128)(2,1)} %bitcast.4), calls=%async_computation.1 | async-start | bytes 1048576 | tf_op jit(solution)/shard_map/all_to_all | solution.py:286
  33.2 0.1 collective-permute-start
  33.3 0.0 copy-done.20
  33.3 16.3 %all-to-all-done.1 = bf16[32,16,512]{2,1,0:T(8,128)(2,1)S(1)} async-done(((bf16[32,16,512]{2,1,0:T(8,128)(2,1)}), bf16[32,16,512]{2,1,0:T(8,128)(2,1)S(1)}, u32[]{:S(2)}, u32[]{:S(2)}) %all-to-all-start.1) | async-done | bytes 524320 | tf_op jit(solution)/shard_map/all_to_all | solution.py:286
  49.6 0.0 copy-start.2
  49.6 0.8 copy-done.2
  50.4 0.0 collective-permute-done
  50.4 0.0 copy-start.8
  50.4 0.9 copy-done.8
  51.4 0.0 copy-done
  51.4 0.0 copy-start.1
  51.4 1.1 copy-done.1
  52.5 0.0 copy-start.3
  52.5 1.0 copy-done.3
  53.5 1.1 copy-done.9
  54.7 3.3 %shard_map.67 = (f32[512,1536]{1,0:T(8,128)S(1)}, f32[16,128]{1,0:T(8,128)S(1)}, f32[512,128]{1,0:T(8,128)S(1)}, f32[32,16,128]{2,1,0:T(8,128)S(1)}, bf16[512,15...) custom-call(s32[1]{0:T(128)} %bitcast.here_ref, bf16[4,4,64,384]{3,2,1,0:T(8,128)(2,1)S(1)} %bitcast.19, ...), custom_call_target="tpu_custom_call" | custom-call | tf_op jit(solution)/shard_map/pallas_call | solution.py:275
  57.9 0.0 copy-start.4
  57.9 1.2 copy-done.4
  59.1 0.8 copy-done.10
  59.9 0.7 copy-done.13
  60.6 0.7 copy-done.16
  61.4 6.9 %all-to-all-start.2 = ((f32[32,16,128]{2,1,0:T(8,128)}), f32[32,16,128]{2,1,0:T(8,128)S(1)}, u32[]{:S(2)}, u32[]{:S(2)}) async-start(f32[32,16,128]{2,1,0:T(8,128)} %copy-done.16), calls=%async_computation.2 | async-start | bytes 524288 | tf_op jit(solution)/shard_map/all_to_all | solution.py:286
  68.3 7.6 %all-to-all-done.2.parts_ref = f32[32,16,128]{2,1,0:T(8,128)S(1)} async-done(((f32[32,16,128]{2,1,0:T(8,128)}), f32[32,16,128]{2,1,0:T(8,128)S(1)}, u32[]{:S(2)}, u32[]{:S(2)}) %all-to-all-start.2) | async-done | bytes 262176 | tf_op jit(solution)/shard_map/all_to_all | solution.py:286
  75.9 0.0 copy-start.18
  75.9 2.7 %shard_map.68 = (f32[16,128]{1,0:T(8,128)}, f32[8,8,128]{2,1,0:T(8,128)}) custom-call(f32[32,16,128]{2,1,0:T(8,128)S(1)} %all-to-all-done.2.parts_ref, f32[16,128]{1,0:T(8,128)S(1)} %pad.13.la_ref, f32[512,1536]{1,0:T(8,128)S(1)} %get-tuple-element.20.d_ref), custom_call_target="tpu_custom_call" | custom-call | tf_op jit(solution)/shard_map/pallas_call | solution.py:275
  78.6 3.3 %all-to-all-start.3 = ((f32[8,8,128]{2,1,0:T(8,128)}), f32[8,8,128]{2,1,0:T(8,128)S(1)}, u32[]{:S(2)}, u32[]{:S(2)}) async-start(f32[8,8,128]{2,1,0:T(8,128)} %get-tuple-element.21), calls=%async_computation.3 | async-start | bytes 65536 | tf_op jit(solution)/shard_map/all_to_all | solution.py:286
  81.9 0.0 copy-done.18
  81.9 0.1 multiply_bitcast_fusion
  82.0 7.8 %all-to-all-done.3.parts_ref = f32[8,8,128]{2,1,0:T(8,128)S(1)} async-done(((f32[8,8,128]{2,1,0:T(8,128)}), f32[8,8,128]{2,1,0:T(8,128)S(1)}, u32[]{:S(2)}, u32[]{:S(2)}) %all-to-all-start.3) | async-done | bytes 32800 | tf_op jit(solution)/shard_map/all_to_all | solution.py:286
  89.9 1.6 shard_map.69
  91.5 12.4 %all_to_all.50.parts_ref = f32[32,16,128]{2,1,0:T(8,128)S(1)} all-to-all(f32[32,16,128]{2,1,0:T(8,128)S(1)} %shard_map.69), channel_id=1, replica_groups=mesh['z'=8,'y'=4,'x'=4,'core'=2] {'y','x','core'}, dimensions={0} | all-to-all | bytes 524288 | tf_op jit(solution)/shard_map/all_to_all | solution.py:286
  103.9 2.4 %shard_map.70 = (f32[16,128]{1,0:T(8,128)}, f32[8,8,128]{2,1,0:T(8,128)S(1)}) custom-call(f32[32,16,128]{2,1,0:T(8,128)S(1)} %all_to_all.50.parts_ref, f32[16,128]{1,0:T(8,128)S(1)} %pad.13.la_ref, f32[512,1536]{1,0:T(8,128)S(1)} %get-tuple-element.20.d_ref), custom_call_target="tpu_custom_call" | custom-call | tf_op jit(solution)/shard_map/pallas_call | solution.py:275
  106.3 10.4 %all_to_all.51.parts_ref = f32[8,8,128]{2,1,0:T(8,128)S(1)} all-to-all(f32[8,8,128]{2,1,0:T(8,128)S(1)} %get-tuple-element.22), channel_id=1, replica_groups=mesh['z'=8,'y'=4,'x'=4,'core'=2] {'z'}, dimensions={0} | all-to-all | bytes 65536 | tf_op jit(solution)/shard_map/all_to_all | solution.py:286
  116.7 1.6 shard_map.71
  118.3 12.4 %all_to_all.52.parts_ref = f32[32,16,128]{2,1,0:T(8,128)S(1)} all-to-all(f32[32,16,128]{2,1,0:T(8,128)S(1)} %shard_map.71), channel_id=1, replica_groups=mesh['z'=8,'y'=4,'x'=4,'core'=2] {'y','x','core'}, dimensions={0} | all-to-all | bytes 524288 | tf_op jit(solution)/shard_map/all_to_all | solution.py:286
  130.7 2.1 %shard_map.72 = (f32[16,128]{1,0:T(8,128)S(1)}, f32[8,8,128]{2,1,0:T(8,128)S(1)}) custom-call(f32[32,16,128]{2,1,0:T(8,128)S(1)} %all_to_all.52.parts_ref, f32[16,128]{1,0:T(8,128)S(1)} %pad.13.la_ref, f32[512,1536]{1,0:T(8,128)S(1)} %get-tuple-element.20.d_ref), custom_call_target="tpu_custom_call" | custom-call | tf_op jit(solution)/shard_map/pallas_call | solution.py:275
  132.8 10.4 %all_to_all.53.parts_ref = f32[8,8,128]{2,1,0:T(8,128)S(1)} all-to-all(f32[8,8,128]{2,1,0:T(8,128)S(1)} %get-tuple-element.23), channel_id=1, replica_groups=mesh['z'=8,'y'=4,'x'=4,'core'=2] {'z'}, dimensions={0} | all-to-all | bytes 65536 | tf_op jit(solution)/shard_map/all_to_all | solution.py:286
  143.2 0.0 copy-done.5
  143.2 0.0 copy-done.11
  143.2 0.0 copy-done.14
  143.2 3.7 %shard_map.73 = (f32[4,256,384]{2,1,0:T(8,128)S(1)}, bf16[4,272,384]{2,1,0:T(8,128)(2,1)S(1)}, f32[4,8,384]{2,1,0:T(8,128)S(1)}, bf16[512,512]{1,0:T(8,128)(2,1)S(1)}) custom-call(s32[1]{0:T(128)} %bitcast.here_ref, f32[8,8,128]{2,1,0:T(8,128)S(1)} %all_to_all.53.parts_ref, f32[8,128]{1,0:T(8,128)S(1)} %pad.14.lb_ref, ...), custom_call_target="tpu_custom_call" | custom-call | tf_op jit(solution)/shard_map/pallas_call | solution.py:275
  147.0 0.0 copy-start.6
  147.0 1.2 copy-done.6
  148.2 0.8 copy-done.12
  148.9 0.9 copy-done.19
  149.8 3.9 %all-to-all-start.9 = ((bf16[32,16,512]{2,1,0:T(8,128)(2,1)}), bf16[32,16,512]{2,1,0:T(8,128)(2,1)S(1)}, u32[]{:S(2)}, u32[]{:S(2)}) async-start(bf16[32,16,512]{2,1,0:T(8,128)(2,1)} %bitcast.24), calls=%async_computation.9 | async-start | bytes 1048576 | tf_op jit(solution)/shard_map/all_to_all | solution.py:286
  153.7 0.1 collective-permute-start.1
  153.8 2.6 %collective-permute-done.1.got_ref = bf16[4,272,384]{2,1,0:T(8,128)(2,1)S(1)} collective-permute-done((bf16[4,272,384]{2,1,0:T(8,128)(2,1)}, bf16[4,272,384]{2,1,0:T(8,128)(2,1)S(1)}, u32[]{:S(2)}, u32[]{:S(2)}) %collective-permute-start.1) | collective-permute-done | bytes 835616 | tf_op jit(solution)/shard_map/ppermute | solution.py:295
  156.4 1.4 copy-done.7
  157.8 1.3 shard_map.74
  159.1 12.2 %all-to-all-done.9 = bf16[32,16,512]{2,1,0:T(8,128)(2,1)S(1)} async-done(((bf16[32,16,512]{2,1,0:T(8,128)(2,1)}), bf16[32,16,512]{2,1,0:T(8,128)(2,1)S(1)}, u32[]{:S(2)}, u32[]{:S(2)}) %all-to-all-start.9) | async-done | bytes 524320 | tf_op jit(solution)/shard_map/all_to_all | solution.py:286
  171.2 5.8 %all-to-all-start.8 = ((bf16[16,80,384]{2,1,0:T(8,128)(2,1)}), bf16[16,80,384]{2,1,0:T(8,128)(2,1)S(1)}, u32[]{:S(2)}, u32[]{:S(2)}) async-start(bf16[16,80,384]{2,1,0:T(8,128)(2,1)} %bitcast.9), calls=%async_computation.8 | async-start | bytes 1966080 | tf_op jit(solution)/shard_map/all_to_all | solution.py:286
  177.1 0.7 shard_map.76
  177.8 13.2 %all-to-all-done.8.got_ref = bf16[16,80,384]{2,1,0:T(8,128)(2,1)S(1)} async-done(((bf16[16,80,384]{2,1,0:T(8,128)(2,1)}), bf16[16,80,384]{2,1,0:T(8,128)(2,1)S(1)}, u32[]{:S(2)}, u32[]{:S(2)}) %all-to-all-start.8) | async-done | bytes 983072 | tf_op jit(solution)/shard_map/all_to_all | solution.py:286
  191.1 0.0 copy-done.17
  191.1 0.8 shard_map.75
  191.9 0.6 reduce
  (20 shorter events, 0.1 us)
Async XLA Ops:
  0.6 9.4 %copy-start.15 = (bf16[16,2048]{1,0:T(8,128)(2,1)S(1)}, bf16[16,2048]{1,0:T(8,128)(2,1)}, u32[]{:S(2)}) copy-start(bf16[16,2048]{1,0:T(8,128)(2,1)} %y_ref.1) | copy-start | bytes 196612
  2.5 30.8 %copy-start.20 = (f32[384]{0:T(512)S(1)}, f32[384]{0:T(512)}, u32[]{:S(2)}) copy-start(f32[384]{0:T(512)} %param.6) | copy-start | bytes 4612
  2.5 20.6 %all-to-all-start = ((bf16[16,64,384]{2,1,0:T(8,128)(2,1)}), bf16[16,64,384]{2,1,0:T(8,128)(2,1)S(1)}, u32[]{:S(2)}, u32[]{:S(2)}) async-start(bf16[16,64,384]{2,1,0:T(8,128)(2,1)} %broadcast_in_dim.4), calls=%async_computation | async-start | bytes 1572864 | tf_op jit(solution)/shard_map/all_to_all | solution.py:286
  23.1 28.3 %copy-start = (bf16[16,64,384]{2,1,0:T(8,128)(2,1)}, bf16[16,64,384]{2,1,0:T(8,128)(2,1)S(1)}, u32[]{:S(2)}) copy-start(bf16[16,64,384]{2,1,0:T(8,128)(2,1)S(1)} %all-to-all-done) | copy-start | bytes 2359300
  24.0 25.6 %all-to-all-start.1 = ((bf16[32,16,512]{2,1,0:T(8,128)(2,1)}), bf16[32,16,512]{2,1,0:T(8,128)(2,1)S(1)}, u32[]{:S(2)}, u32[]{:S(2)}) async-start(bf16[32,16,512]{2,1,0:T(8,128)(2,1)} %bitcast.4), calls=%async_computation.1 | async-start | bytes 1048576 | tf_op jit(solution)/shard_map/all_to_all | solution.py:286
  33.2 17.3 %collective-permute-start = (bf16[16,64,384]{2,1,0:T(8,128)(2,1)S(1)}, bf16[16,64,384]{2,1,0:T(8,128)(2,1)S(1)}, u32[]{:S(2)}, u32[]{:S(2)}) collective-permute-start(bf16[16,64,384]{2,1,0:T(8,128)(2,1)S(1)} %all-to-all-done), channel_id=1, source_target_pairs={{0,1},{1,0},{2,3},{3,2},{4,5},{5,4},{6,7},{7,6},{8,9},{9,8},{10,11... | collective-permute-start | bytes 2359304 | tf_op jit(solution)/shard_map/ppermute | solution.py:295
  49.6 0.8 copy-start.2
  50.4 0.9 copy-start.8
  51.4 1.1 copy-start.1
  52.5 1.0 copy-start.3
  53.5 1.1 copy-start.9
  57.9 1.2 copy-start.4
  59.1 0.8 copy-start.10
  59.9 0.7 copy-start.13
  60.6 0.7 copy-start.16
  61.4 14.5 %all-to-all-start.2 = ((f32[32,16,128]{2,1,0:T(8,128)}), f32[32,16,128]{2,1,0:T(8,128)S(1)}, u32[]{:S(2)}, u32[]{:S(2)}) async-start(f32[32,16,128]{2,1,0:T(8,128)} %copy-done.16), calls=%async_computation.2 | async-start | bytes 524288 | tf_op jit(solution)/shard_map/all_to_all | solution.py:286
  75.9 6.1 %copy-start.18 = (f32[2048]{0:T(1024)S(1)}, f32[2048]{0:T(1024)}, u32[]{:S(2)}) copy-start(f32[2048]{0:T(1024)} %param.7) | copy-start | bytes 24580
  78.6 11.3 %all-to-all-start.3 = ((f32[8,8,128]{2,1,0:T(8,128)}), f32[8,8,128]{2,1,0:T(8,128)S(1)}, u32[]{:S(2)}, u32[]{:S(2)}) async-start(f32[8,8,128]{2,1,0:T(8,128)} %get-tuple-element.21), calls=%async_computation.3 | async-start | bytes 65536 | tf_op jit(solution)/shard_map/all_to_all | solution.py:286
  130.7 12.5 %copy-start.5 = (bf16[512,1536]{1,0:T(8,128)(2,1)S(1)}, bf16[512,1536]{1,0:T(8,128)(2,1)}, u32[]{:S(2)}) copy-start(bf16[512,1536]{1,0:T(8,128)(2,1)} %copy-done.4) | copy-start | bytes 4718596
  130.7 12.5 %copy-start.11 = (bf16[512,512]{1,0:T(8,128)(2,1)S(1)}, bf16[512,512]{1,0:T(8,128)(2,1)}, u32[]{:S(2)}) copy-start(bf16[512,512]{1,0:T(8,128)(2,1)} %copy-done.10) | copy-start | bytes 1572868
  130.7 12.5 %copy-start.14 = (f32[512,128]{1,0:T(8,128)S(1)}, f32[512,128]{1,0:T(8,128)}, u32[]{:S(2)}) copy-start(f32[512,128]{1,0:T(8,128)} %copy-done.13) | copy-start | bytes 786436
  147.0 1.2 copy-start.6
  148.1 0.8 copy-start.12
  148.9 0.9 copy-start.19
  149.8 21.4 %all-to-all-start.9 = ((bf16[32,16,512]{2,1,0:T(8,128)(2,1)}), bf16[32,16,512]{2,1,0:T(8,128)(2,1)S(1)}, u32[]{:S(2)}, u32[]{:S(2)}) async-start(bf16[32,16,512]{2,1,0:T(8,128)(2,1)} %bitcast.24), calls=%async_computation.9 | async-start | bytes 1048576 | tf_op jit(solution)/shard_map/all_to_all | solution.py:286
  153.7 2.7 %collective-permute-start.1 = (bf16[4,272,384]{2,1,0:T(8,128)(2,1)}, bf16[4,272,384]{2,1,0:T(8,128)(2,1)S(1)}, u32[]{:S(2)}, u32[]{:S(2)}) collective-permute-start(bf16[4,272,384]{2,1,0:T(8,128)(2,1)} %copy-done.19), channel_id=1, source_target_pairs={{0,1},{1,0},{2,3},{3,2},{4,5},{5,4},{6,7},{7,6},{8,9},{9,8},{10,11... | collective-permute-start | bytes 2506760 | tf_op jit(solution)/shard_map/ppermute | solution.py:295
  156.4 1.4 copy-start.7
  159.1 32.0 %copy-start.17 = (bf16[64,384]{1,0:T(8,128)(2,1)S(1)}, bf16[64,384]{1,0:T(8,128)(2,1)}, u32[]{:S(2)}) copy-start(bf16[64,384]{1,0:T(8,128)(2,1)} %x_ref.1) | copy-start | bytes 147460
  171.2 19.8 %all-to-all-start.8 = ((bf16[16,80,384]{2,1,0:T(8,128)(2,1)}), bf16[16,80,384]{2,1,0:T(8,128)(2,1)S(1)}, u32[]{:S(2)}, u32[]{:S(2)}) async-start(bf16[16,80,384]{2,1,0:T(8,128)(2,1)} %bitcast.9), calls=%async_computation.8 | async-start | bytes 1966080 | tf_op jit(solution)/shard_map/all_to_all | solution.py:286

commit v2 on v1

v2 whole, which is shorter than its diff:
```python
import functools
import math

import jax
import jax.numpy as jnp
from jax import lax
from jax.experimental import pallas as pl
from jax.experimental.pallas import tpu as pltpu
from jax.sharding import Mesh
from jax.sharding import PartitionSpec as P

ITERS = 3
BLUR = 0.05
LOG2E = 1.0 / math.log(2.0)
F32 = jnp.float32
BF16 = jnp.bfloat16
LANES = 128
STEP = 64


def cdiv(a, b):
    return -(-a // b)


def padded(n, m):
    return cdiv(n, m) * m


def log2_of(x):
    return jnp.log(x) * LOG2E


def merged(parts):
    high = jnp.max(parts, axis=0)
    return high + log2_of(jnp.sum(jnp.exp2(parts - high[None]), axis=0))


def rows_of_tiles(vec, tiles):
    return [vec[:, t * LANES : (t + 1) * LANES] for t in range(tiles)]


def to_column(lines, column_ref, tiles):
    for t in range(tiles):
        wide = jnp.broadcast_to(lines[t : t + 1, :], (LANES, LANES))
        column_ref[t * LANES : (t + 1) * LANES, :] = wide.T


def row_sweep(d_ref, column_ref, lines_ref):
    cols = d_ref.shape[0]
    chunks = cols // STEP
    tiles = d_ref.shape[1] // LANES

    def one(t, carry):
        lanes = pl.ds(pl.multiple_of(t * LANES, LANES), LANES)

        def score(c):
            at = slice(c * STEP, (c + 1) * STEP)
            return column_ref[at, :] + d_ref[at, lanes]

        top = score(0)
        for c in range(1, chunks):
            top = jnp.maximum(top, score(c))
        top = jnp.max(top, axis=0, keepdims=True)
        total = jnp.exp2(score(0) - top)
        for c in range(1, chunks):
            total = total + jnp.exp2(score(c) - top)
        total = jnp.sum(total, axis=0, keepdims=True)
        lines_ref[pl.ds(t, 1), :] = top + log2_of(total)
        return carry

    lax.fori_loop(0, tiles, one, 0, unroll=4)


def column_sweep(d_ref, lines, column_ref):
    cols = d_ref.shape[0]
    tiles = d_ref.shape[1] // LANES

    def one(c, carry):
        at = pl.ds(pl.multiple_of(c * STEP, STEP), STEP)

        def score(t):
            return lines[t : t + 1, :] + d_ref[at, t * LANES : (t + 1) * LANES]

        top = score(0)
        for t in range(1, tiles):
            top = jnp.maximum(top, score(t))
        top = jnp.max(top, axis=1, keepdims=True)
        total = jnp.exp2(score(0) - top)
        for t in range(1, tiles):
            total = total + jnp.exp2(score(t) - top)
        total = jnp.sum(total, axis=1, keepdims=True)
        column_ref[at, :] = jnp.broadcast_to(top + log2_of(total), (STEP, LANES))
        return carry

    lax.fori_loop(0, cols // STEP, one, 0, unroll=4)


def from_column(column_ref, lines_ref, tiles):
    for t in range(tiles):
        square = column_ref[t * LANES : (t + 1) * LANES, :].T
        lines_ref[t : t + 1, :] = square[0:1, :]


def setup_kernel(scale, grid, here_ref, *refs):
    nrow, ncol, depth, width = grid
    own_refs, other_refs = refs[:ncol], refs[ncol : 2 * ncol]
    y_hbm, la_ref, d_ref, sqx_ref, sqy_ref, out_ref, x_hbm, x_ref, y_ref, column_ref, lines_ref, sems = refs[2 * ncol :]
    core, across, along = here_ref[0], here_ref[1], here_ref[2]
    fetch_y = pltpu.make_async_copy(y_hbm, y_ref, sems.at[0])
    fetch_y.start()
    copies, n = [], 1
    for side, group in ((core, own_refs), (1 - core, other_refs)):
        for sx in range(ncol):
            c = lax.rem(across - sx + ncol, ncol)
            at = pl.multiple_of((2 * c + side) * depth, depth)
            for sy in range(nrow):
                r = lax.rem(along - sy + nrow, nrow)
                lanes = pl.multiple_of(r * width, LANES)
                copy = pltpu.make_async_copy(
                    group[sx].at[sy], x_ref.at[pl.ds(at, depth), pl.ds(lanes, width)], sems.at[n])
                copy.start()
                copies.append(copy)
                n += 1
    fetch_y.wait()
    ctiles = y_ref.shape[1] // LANES
    lines_ref[...] = jnp.zeros_like(lines_ref)
    for t in range(ctiles):
        part = y_ref[:, t * LANES : (t + 1) * LANES].astype(F32)
        lines_ref[t : t + 1, :] = jnp.sum(part * part, axis=0, keepdims=True)
    to_column(lines_ref[...], column_ref, ctiles)
    sqy_ref[...] = lines_ref[: sqy_ref.shape[0], :]
    column_ref[...] = column_ref[...] * (-0.5 * scale)
    for copy in copies:
        copy.wait()
    store_x = pltpu.make_async_copy(x_ref, x_hbm, sems.at[n])
    store_x.start()
    tiles = x_ref.shape[1] // LANES
    sqx_ref[...] = jnp.zeros_like(sqx_ref)
    for t in range(tiles):
        part = x_ref[:, t * LANES : (t + 1) * LANES].astype(F32)
        sqx_ref[t : t + 1, :] = jnp.sum(part * part, axis=0, keepdims=True)
    for r in range(nrow):
        cross = lax.dot_general(
            y_ref[...], x_ref[:, r * width : (r + 1) * width], (((0,), (0,)), ((), ())),
            preferred_element_type=F32)
        d_ref[:, r * width : (r + 1) * width] = cross * scale
    lines_ref[...] = jnp.zeros_like(lines_ref)
    row_sweep(d_ref, column_ref, lines_ref)
    wtiles = width // LANES
    lines_ref[tiles : tiles + wtiles, :] = la_ref[0:wtiles, :]
    out_ref[...] = jnp.broadcast_to(lines_ref[...][None], out_ref.shape)
    store_x.wait()


def row_kernel(parts_ref, lb_ref, d_ref, out_ref, column_ref, lines_ref):
    ctiles = d_ref.shape[0] // LANES
    g = lb_ref[...] - merged(parts_ref[...])
    to_column(g, column_ref, ctiles)
    lines_ref[...] = jnp.zeros_like(lines_ref)
    row_sweep(d_ref, column_ref, lines_ref)
    out_ref[...] = jnp.broadcast_to(lines_ref[...][None], out_ref.shape)


def column_kernel(parts_ref, la_ref, d_ref, f_ref, out_ref, column_ref, lines_ref):
    ctiles = d_ref.shape[0] // LANES
    f = la_ref[...] - merged(parts_ref[...])
    f_ref[...] = f
    column_sweep(d_ref, f, column_ref)
    lines_ref[...] = jnp.zeros_like(lines_ref)
    from_column(column_ref, lines_ref, ctiles)
    out_ref[...] = jnp.broadcast_to(lines_ref[...][None], out_ref.shape)


def three_pieces(v):
    high = v.astype(BF16)
    rest = v - high.astype(F32)
    mid = rest.astype(BF16)
    low = (rest - mid.astype(F32)).astype(BF16)
    return high, mid, low


def put_pieces(block_ref, at, row, values):
    block_ref[at + (slice(row, row + 16),)] = jnp.zeros((16, block_ref.shape[-1]), BF16)
    for n, v in enumerate(values):
        for m, piece in enumerate(three_pieces(v)):
            block_ref[at + (slice(row + 3 * n + m, row + 3 * n + m + 1),)] = piece


def pieces_sum(block, n):
    one, two, three = (block[3 * n + m : 3 * n + m + 1].astype(F32) for m in range(3))
    return one + two + three


def balanced(values):
    while len(values) > 1:
        half = len(values) // 2
        values = [values[k] + values[k + half] for k in range(half)]
    return values[0]


def plan_kernel(scale, emb, grid, here_ref, parts_ref, lb_ref, f_ref, sqx_ref, sqy_ref, d_ref, y_hbm, x_hbm,
                keep_hbm, send_ref, sums_ref, xsum_hbm, keep_ref, xsum_ref, column_ref, square_ref, plan_ref, y_ref, ys_ref, x_ref,
                lines_ref, sems):
    core = here_ref[0]
    nrow, ncol, depth, width = grid
    half = ncol * depth
    cols, rows = d_ref.shape
    ctiles, tiles, chunks = cols // LANES, rows // LANES, cols // STEP
    copies = [pltpu.make_async_copy(y_hbm, y_ref, sems.at[0]), pltpu.make_async_copy(x_hbm, x_ref, sems.at[1])]
    for copy in copies:
        copy.start()
    g = lb_ref[...] - merged(parts_ref[...])
    to_column(g, column_ref, ctiles)
    back = 1.0 / emb
    unit = 2.0 / (emb * scale)
    to_column(sqy_ref[...], square_ref, ctiles)

    def one(t, carry):
        lanes = pl.ds(pl.multiple_of(t * LANES, LANES), LANES)
        f = f_ref[pl.ds(t, 1), :]
        sq = sqx_ref[pl.ds(t, 1), :]
        mass = jnp.zeros((STEP, LANES), F32)
        paid = jnp.zeros((STEP, LANES), F32)
        for c in range(chunks):
            at = slice(c * STEP, (c + 1) * STEP)
            d = d_ref[at, lanes]
            p = jnp.exp2(column_ref[at, :] + d + f)
            plan_ref[at, lanes] = p.astype(BF16)
            mass = mass + p
            paid = paid + p * ((sq + square_ref[at, :]) * back - d * unit)
        lines_ref[0, pl.ds(t, 1), :] = jnp.sum(mass, axis=0, keepdims=True)
        lines_ref[1, pl.ds(t, 1), :] = jnp.sum(paid, axis=0, keepdims=True)
        return carry

    lax.fori_loop(0, tiles, one, 0, unroll=2)
    sums_ref[...] = jnp.zeros_like(sums_ref)
    wtiles = width // LANES
    for r in range(nrow):
        for w in range(wtiles):
            t = r * wtiles + w
            for n in range(2):
                sums_ref[r, n : n + 1, w * LANES : (w + 1) * LANES] = lines_ref[n, t : t + 1, :]
    for copy in copies:
        copy.wait()
    xsum = lax.dot_general(x_ref[...], plan_ref[...], (((1,), (1,)), ((), ())), preferred_element_type=F32)
    xsum_ref[...] = xsum.astype(BF16)
    copies = [pltpu.make_async_copy(xsum_ref, xsum_hbm, sems.at[2]), pltpu.make_async_copy(keep_ref, keep_hbm, sems.at[3])]
    copies[0].start()
    for c in range(ncol):
        mine = pl.multiple_of((2 * c + core) * depth, depth)
        theirs = pl.multiple_of((2 * c + 1 - core) * depth, depth)
        ys_ref[c * depth : (c + 1) * depth, :] = y_ref[pl.ds(mine, depth), :]
        ys_ref[half + c * depth : half + (c + 1) * depth, :] = y_ref[pl.ds(theirs, depth), :]
    for r in range(nrow):
        part = plan_ref[:, r * width : (r + 1) * width]
        pulled = lax.dot_general(ys_ref[...], part, (((1,), (0,)), ((), ())), preferred_element_type=F32)
        keep_ref[r] = pulled[:half].astype(BF16)
        send_ref[r, :half] = pulled[half:].astype(BF16)
        put_pieces(send_ref, (r,), half, [sums_ref[r, n : n + 1] for n in range(2)])
    copies[1].start()
    for copy in copies:
        copy.wait()


def pair_kernel(here_ref, keep_hbm, sums_ref, got_ref, *refs):
    outs, keep_ref, sems = refs[:-2], refs[-2], refs[-1]
    fetch = pltpu.make_async_copy(keep_hbm, keep_ref, sems.at[0])
    fetch.start()
    nrow, deep, width = outs[0].shape
    depth, ncol = deep - 16, len(outs)
    half = ncol * depth
    across = here_ref[1]
    fetch.wait()
    for r in range(nrow):
        extra = got_ref[r, half : half + 16]
        totals = [sums_ref[r, n : n + 1] + pieces_sum(extra, n) for n in range(2)]
        for s, out in enumerate(outs):
            c = lax.rem(across + s, ncol)
            at = pl.ds(pl.multiple_of(c * depth, depth), depth)
            out[r, :depth] = (keep_ref[r, at].astype(F32) + got_ref[r, at].astype(F32)).astype(BF16)
            put_pieces(out, (r,), depth, totals)


def across_kernel(here_ref, *refs):
    ins, outs = refs[: len(refs) // 2], refs[len(refs) // 2 :]
    nrow, deep, width = ins[0].shape
    depth = deep - 16
    along = here_ref[2]
    for s, out in enumerate(outs):
        r = lax.rem(along + s, nrow)
        out[:depth] = balanced([one[r, :depth].astype(F32) for one in ins]).astype(BF16)
        extras = [one[r, depth:deep] for one in ins]
        put_pieces(out, (), depth, [balanced([pieces_sum(extra, n) for extra in extras]) for n in range(2)])


def roll_kernel(here_ref, *refs):
    ins, (x_ref, pull_ref, reward_ref) = refs[:-3], refs[-3:]
    depth, deep = x_ref.shape[0], ins[0].shape[0]
    total = balanced([one[:depth].astype(F32) for one in ins])
    sums = [balanced([pieces_sum(one[depth:deep], n) for one in ins]) for n in range(2)]
    reward_ref[...] = -sums[1] / sums[0]
    pull_ref[...] = sums[0] * x_ref[...].astype(F32) - total


def expert_kernel(got_ref, y_ref, b_ref, pull_ref):
    nz, ny, _, cols = got_ref.shape
    for q in range(ny):
        total = got_ref[0, q].astype(F32)
        for k in range(1, nz):
            total = total + got_ref[k, q].astype(F32)
        at = slice(q * cols, (q + 1) * cols)
        pull_ref[:, at] = b_ref[:, at] * y_ref[:, at].astype(F32) - total


def call(body, outs, scratch, *args, smem=0, far=(), far_out=(), sems=0, limit=None):
    spec = pl.BlockSpec(memory_space=pltpu.VMEM)
    scalar = pl.BlockSpec(memory_space=pltpu.SMEM)
    away = pl.BlockSpec(memory_space=pltpu.HBM)
    ins = [scalar if n < smem else away if n in far else spec for n in range(len(args))]
    args = [pltpu.with_memory_space_constraint(a, pltpu.HBM) if n in far else a for n, a in enumerate(args)]
    scratches = [pltpu.VMEM(s, t) for s, t in scratch]
    if sems:
        scratches.append(pltpu.SemaphoreType.DMA((sems,)))
    return pl.pallas_call(
        body,
        out_shape=[pltpu.HBM(s, t) if n in far_out else jax.ShapeDtypeStruct(s, t) for n, (s, t) in enumerate(outs)],
        in_specs=ins,
        out_specs=[away if n in far_out else spec for n in range(len(outs))],
        scratch_shapes=scratches,
        compiler_params=pltpu.CompilerParams(vmem_limit_bytes=limit),
    )(*args)


def exchanged(x, axes):
    return lax.all_to_all(x, axes, split_axis=0, concat_axis=0, tiled=True)


def as_lines(v, lines):
    count = v.shape[0] // LANES
    return jnp.pad(v.reshape(count, LANES), ((0, lines - count), (0, 0)))


def swapped(x):
    return lax.ppermute(x, "core", [(0, 1), (1, 0)])


def shifted(x, axis, by):
    n = lax.axis_size(axis)
    return lax.ppermute(x, axis, [(i, (i + by) % n) for i in range(n)])


def shards(roll_embed, expert_embed, roll_weight, expert_weight):
    nz, ny, nx, nk = (lax.axis_size(a) for a in ("z", "y", "x", "core"))
    depth, width = roll_embed.shape
    thin, wide = expert_embed.shape
    emb = thin * nz * ny
    cols = wide // ny
    rows = width * ny
    scale = 2.0 * LOG2E / (emb * BLUR)
    grid = (ny, nx, depth, width)
    quarter = lax.axis_index("y")
    here = jnp.stack([lax.axis_index(a).astype(jnp.int32) for a in ("core", "x", "y")])

    y_blocks = jnp.moveaxis(expert_embed.reshape(thin, ny, cols), 1, 0)
    y_send = jnp.broadcast_to(y_blocks[None], (nz, ny, thin, cols)).reshape(nz * ny, thin, cols)
    y_all = exchanged(y_send, ("z", "y")).reshape(emb, cols)
    x_line = jnp.stack([roll_embed] + [shifted(roll_embed, "y", s) for s in range(1, ny)])
    x_own = [x_line] + [shifted(x_line, "x", s) for s in range(1, nx)]
    x_other = [swapped(x) for x in x_own]

    wtiles = width // LANES
    f_lines = padded(rows // LANES + wtiles, 8)
    g_lines = padded(cols // LANES, 8)
    la_own = as_lines(log2_of(roll_weight), 8)
    lb = as_lines(log2_of(lax.dynamic_slice_in_dim(expert_weight, quarter * cols, cols, 0)), g_lines)
    crowd = ny * nx * nk

    column = ((cols, LANES), F32)
    f_shape, g_shape = (crowd, f_lines, LANES), (nz, g_lines, LANES)
    ins = (here, *x_own, *x_other, y_all, la_own)
    d, sqx, sqy, out, x_all = call(
        functools.partial(setup_kernel, scale, grid),
        [((cols, rows), F32), ((f_lines, LANES), F32), ((g_lines, LANES), F32), (f_shape, F32),
         ((emb, rows), BF16)],
        [((emb, rows), BF16), ((emb, cols), BF16), column, ((f_lines, LANES), F32)],
        *ins, smem=1, far=range(1, 2 * nx + 2), far_out=(4,), sems=2 * nx * ny + 2, limit=24 << 20)
    la = None
    for step in range(ITERS):
        if step:
            (out,) = call(row_kernel, [(f_shape, F32)], [column, ((f_lines, LANES), F32)],
                          got, lb, d, limit=12 << 20)
        got = exchanged(out, ("y", "x", "core"))
        if step == 0:
            firsts = got.reshape(ny, nx * nk, f_lines, LANES)[:, 0, rows // LANES : rows // LANES + wtiles]
            la = jnp.pad(firsts.reshape(rows // LANES, LANES), ((0, f_lines - rows // LANES), (0, 0)))
        f, out = call(column_kernel, [((f_lines, LANES), F32), (g_shape, F32)],
                      [column, ((g_lines, LANES), F32)], got, la, d, limit=12 << 20)
        got = exchanged(out, ("z",))

    half = nx * depth
    keep, send, sums, xsum = call(
        functools.partial(plan_kernel, scale, emb, grid),
        [((ny, half, width), BF16), ((ny, half + 16, width), BF16), ((ny, 8, width), F32), ((emb, cols), BF16)],
        [((ny, half, width), BF16), ((emb, cols), BF16), column, column, ((cols, rows), BF16), ((emb, cols), BF16),
         ((emb, cols), BF16), ((emb, rows), BF16), ((2, f_lines, LANES), F32)],
        here, got, lb, f, sqx, sqy, d, y_all, x_all, smem=1, far=(7, 8), far_out=(0, 3), sems=4, limit=32 << 20)
    xsum_got = exchanged(xsum.reshape(nz * ny, thin, cols), ("z", "y"))
    line = ((ny, depth + 16, width), BF16)
    pairs = call(pair_kernel, [line] * nx, [((ny, half, width), BF16)], here, keep, sums, swapped(send),
                 smem=1, far=(1,), sems=1, limit=16 << 20)
    lines = [pairs[0]] + [shifted(pairs[s], "x", s) for s in range(1, nx)]
    ends = call(across_kernel, [(line[0][1:], BF16)] * ny, [], here, *lines, smem=1, limit=16 << 20)
    ends = [ends[0]] + [shifted(ends[s], "y", s) for s in range(1, ny)]
    roll_pull, reward = call(roll_kernel, [((depth, width), F32), ((1, width), F32)], [],
                             here, *ends, roll_embed, smem=1, limit=8 << 20)
    (expert_pull,) = call(expert_kernel, [((thin, wide), F32)], [],
                          xsum_got.reshape(nz, ny, thin, cols), expert_embed, expert_weight.reshape(1, wide),
                          limit=8 << 20)
    return (reward.reshape(width), roll_pull, expert_pull)


def solution(mesh):
    z, y = 8, 4
    torus = Mesh(mesh.devices.reshape(z, y, 4, 2), ("z", "y", "x", "core"))
    row, col = ("z", "y"), ("x", "core")
    return jax.shard_map(
        shards,
        mesh=torus,
        in_specs=(P(col, row), P(row, col), P(row), P(col)),
        out_specs=(P(row), P(col, row), P(row, col)),
        check_vma=False,
    )
```

time: 193 us -> 166 us (0.86)
  waiting for transfers between devices: 72.6 us -> 38.1 us
  starting transfers between devices: 36.9 us -> 52.1 us
  local copies, waits for them, and re-layouts: 15.6 us -> 3.92 us
    all_to_all x6 -> x4, waiting for transfers between devices: 70.1 us -> 15.5 us  [exchanged(): return lax.all_to_all(x, axes, split_axis=0, concat_axis=0, tiled=True)]
    ppermute x0 -> x12, waiting for transfers between devices: none -> 22 us  [shifted(): return lax.ppermute(x, axis, [(i, (i + by) % n) for i in range(n)])]
    ppermute x0 -> x12, starting transfers between devices: none -> 21.4 us  [shifted(): return lax.ppermute(x, axis, [(i, (i + by) % n) for i in range(n)])]
    unnamed x43 -> x27, local copies, waits for them, and re-layouts: 12.8 us -> 2.15 us
    all_to_all x6 -> x4, starting transfers between devices: 36.7 us -> 30.6 us  [exchanged(): return lax.all_to_all(x, axes, split_axis=0, concat_axis=0, tiled=True)]
    pallas_call x10 -> x11, Pallas kernels: 20.2 us -> 21.5 us  [call(): pl.pallas_call(body, out_shape=[pltpu.HBM(s, t) if n in far_out else jax....]
  transfers between devices with their start and end apart: 8 -> 21, of which waited for: 7 -> 13; matrix products, arithmetic and copies ran while one was open for 0% -> 1% of each run, Pallas kernels for 1% -> 2%
where the time goes in v2:
time: 166 us; the launch traced here: 164 us
  starting transfers between devices  52.1 us (31%)
  blocking collectives  45.6 us (27%)
  waiting for transfers between devices  38.1 us (23%)
  Pallas kernels  21.5 us (13%)
  local copies, waits for them, and re-layouts  3.92 us (2%)
  other arithmetic  2.27 us (1%)
    all_to_all x4, blocking collectives, exchanged(): return lax.all_to_all(x, axes, split_axis=0, concat_axis=0, tiled=True)  45.6 us
    all_to_all x4, starting transfers between devices, exchanged(): return lax.all_to_all(x, axes, split_axis=0, concat_axis=0, tiled=True)  30.6 us
    ppermute x12, waiting for transfers between devices, shifted(): return lax.ppermute(x, axis, [(i, (i + by) % n) for i in range(n)])  22 us
    pallas_call x11, Pallas kernels, call(): pl.pallas_call(body, out_shape=[pltpu.HBM(s, t) if n in far_out else jax....  21.5 us
    ppermute x12, starting transfers between devices, shifted(): return lax.ppermute(x, axis, [(i, (i + by) % n) for i in range(n)])  21.4 us
    all_to_all x4, waiting for transfers between devices, exchanged(): return lax.all_to_all(x, axes, split_axis=0, concat_axis=0, tiled=True)  15.5 us
  transfers between devices with their start and end apart: 21, of which 13 were waited for; matrix products, arithmetic and copies ran while one was open for 1% of the time, Pallas kernels for 2%

profile of v2, /device:TPU:2, one launch (start us, length us, event | category | flops | bytes accessed | tf_op | source)
XLA Modules:
  0.0 164.4 jit_solution(14898723139634229322)
XLA Ops:
  0.6 0.9 reshape.37
  1.5 0.8 broadcast_in_dim.2
  2.4 11.5 %all-to-all-start = ((bf16[32,16,512]{2,1,0:T(8,128)(2,1)}), bf16[32,16,512]{2,1,0:T(8,128)(2,1)S(1)}, u32[]{:S(2)}, u32[]{:S(2)}) async-start(bf16[32,16,512]{2,1,0:T(8,128)(2,1)} %bitcast.8), calls=%async_computation | async-start | bytes 1048576 | tf_op jit(solution)/shard_map/all_to_all | solution.py:335
  13.9 3.4 %collective-permute-start.1 = (bf16[64,384]{1,0:T(8,128)(2,1)}, bf16[64,384]{1,0:T(8,128)(2,1)S(1)}, u32[]{:S(2)}, u32[]{:S(2)}) collective-permute-start(bf16[64,384]{1,0:T(8,128)(2,1)} %refs_4_.1), channel_id=1, source_target_pairs={{0,16},{8,24},{16,0},{24,8},{1,17},{9,25},{17,1},{25,9},{2,18},{10... | collective-permute-start | bytes 147464 | tf_op jit(solution)/shard_map/ppermute | solution.py:349
  17.2 0.6 collective-permute-start
  17.8 2.7 %collective-permute-start.2 = (bf16[64,384]{1,0:T(8,128)(2,1)}, bf16[64,384]{1,0:T(8,128)(2,1)S(1)}, u32[]{:S(2)}, u32[]{:S(2)}) collective-permute-start(bf16[64,384]{1,0:T(8,128)(2,1)} %refs_4_.1), channel_id=1, source_target_pairs={{0,24},{8,0},{16,8},{24,16},{1,25},{9,1},{17,9},{25,17},{2,26},{10... | collective-permute-start | bytes 147464 | tf_op jit(solution)/shard_map/ppermute | solution.py:349
  20.5 0.0 collective-permute-done.1
  20.5 2.3 %collective-permute-done = bf16[64,384]{1,0:T(8,128)(2,1)S(1)} collective-permute-done((bf16[64,384]{1,0:T(8,128)(2,1)}, bf16[64,384]{1,0:T(8,128)(2,1)S(1)}, u32[]{:S(2)}, u32[]{:S(2)}) %collective-permute-start) | collective-permute-done | bytes 49184 | tf_op jit(solution)/shard_map/ppermute | solution.py:349
  22.8 0.1 collective-permute-done.2
  22.9 0.8 pad_maximum_fusion.refs_0_
  23.8 0.0 copy-start.3
  23.8 0.6 collective-permute-start.5
  24.4 2.4 %collective-permute-start.4 = (bf16[4,64,384]{2,1,0:T(8,128)(2,1)S(1)}, bf16[4,64,384]{2,1,0:T(8,128)(2,1)S(1)}, u32[]{:S(2)}, u32[]{:S(2)}) collective-permute-start(bf16[4,64,384]{2,1,0:T(8,128)(2,1)S(1)} %pad_maximum_fusion.refs_0_), channel_id=1, source_target_pairs={{0,4},{2,6},{4,0},{6,2},{1,5},{3,7},{5,1},{7,3},{8,12},{10,14},{12... | collective-permute-start | bytes 589832 | tf_op jit(solution)/shard_map/ppermute | solution.py:349
  26.8 1.8 %collective-permute-start.3 = (bf16[4,64,384]{2,1,0:T(8,128)(2,1)S(1)}, bf16[4,64,384]{2,1,0:T(8,128)(2,1)S(1)}, u32[]{:S(2)}, u32[]{:S(2)}) collective-permute-start(bf16[4,64,384]{2,1,0:T(8,128)(2,1)S(1)} %pad_maximum_fusion.refs_0_), channel_id=1, source_target_pairs={{0,2},{2,4},{4,6},{6,0},{1,3},{3,5},{5,7},{7,1},{8,10},{10,12},{12... | collective-permute-start | bytes 589832 | tf_op jit(solution)/shard_map/ppermute | solution.py:349
  28.6 0.0 collective-permute-start.6
  28.6 3.0 %collective-permute-done.5.refs_3_ = bf16[4,64,384]{2,1,0:T(8,128)(2,1)S(1)} collective-permute-done((bf16[4,64,384]{2,1,0:T(8,128)(2,1)S(1)}, bf16[4,64,384]{2,1,0:T(8,128)(2,1)S(1)}, u32[]{:S(2)}, u32[]{:S(2)}) %collective-permute-start.5) | collective-permute-done | bytes 196640 | tf_op jit(solution)/shard_map/ppermute | solution.py:349
  31.7 2.5 %collective-permute-done.4.refs_2_ = bf16[4,64,384]{2,1,0:T(8,128)(2,1)S(1)} collective-permute-done((bf16[4,64,384]{2,1,0:T(8,128)(2,1)S(1)}, bf16[4,64,384]{2,1,0:T(8,128)(2,1)S(1)}, u32[]{:S(2)}, u32[]{:S(2)}) %collective-permute-start.4) | collective-permute-done | bytes 196640 | tf_op jit(solution)/shard_map/ppermute | solution.py:349
  34.2 0.0 collective-permute-start.8
  34.2 0.9 collective-permute-done.3.refs_1_
  35.0 0.7 multiply_bitcast_fusion.1
  35.7 0.1 pad_add_fusion.here_ref
  35.8 0.0 collective-permute-done.9.refs_7_
  35.8 0.6 collective-permute-done.7.refs_5_
  36.5 0.1 copy-done.10
  36.6 0.1 copy-done.11
  36.6 0.5 copy-done.12
  37.1 0.8 copy-done.4
  37.9 4.5 %shard_map.67 = (f32[512,1536]{1,0:T(8,128)S(1)}, f32[16,128]{1,0:T(8,128)S(1)}, f32[8,128]{1,0:T(8,128)S(1)}, f32[32,16,128]{2,1,0:T(8,128)S(1)}, bf16[512,1536]{1,0:T(8,128)(2,1)}) custom-call(s32[3]{0:T(128)S(1)} %pad_add_fusion.here_ref, bf16[4,64,384]{2,1,0:T(8,128)(2,1)} %copy-done.5, bf16[4,64,384]{2,1,0:T(8,128)(2,1)} %copy-done.8, ...), custom_call_target="tpu_custom_call" | custom-call | tf_op jit(solution)/shard_map/pallas_call | solution.py:324
  42.5 0.7 copy-done.1
  43.2 7.9 %all-to-all-start.1 = ((f32[32,16,128]{2,1,0:T(8,128)}), f32[32,16,128]{2,1,0:T(8,128)S(1)}, u32[]{:S(2)}, u32[]{:S(2)}) async-start(f32[32,16,128]{2,1,0:T(8,128)} %copy-done.1), calls=%async_computation.1 | async-start | bytes 524288 | tf_op jit(solution)/shard_map/all_to_all | solution.py:335
  51.1 7.6 %all-to-all-done.1.parts_ref = f32[32,16,128]{2,1,0:T(8,128)S(1)} async-done(((f32[32,16,128]{2,1,0:T(8,128)}), f32[32,16,128]{2,1,0:T(8,128)S(1)}, u32[]{:S(2)}, u32[]{:S(2)}) %all-to-all-start.1) | async-done | bytes 262176 | tf_op jit(solution)/shard_map/all_to_all | solution.py:335
  58.7 1.6 shard_map.68
  60.4 7.3 %all-to-all-start.2 = ((f32[8,8,128]{2,1,0:T(8,128)}), f32[8,8,128]{2,1,0:T(8,128)S(1)}, u32[]{:S(2)}, u32[]{:S(2)}) async-start(f32[8,8,128]{2,1,0:T(8,128)} %get-tuple-element.28), calls=%async_computation.2 | async-start | bytes 65536 | tf_op jit(solution)/shard_map/all_to_all | solution.py:335
  67.7 0.1 multiply_bitcast_fusion
  67.8 7.9 %all-to-all-done.2.parts_ref = f32[8,8,128]{2,1,0:T(8,128)S(1)} async-done(((f32[8,8,128]{2,1,0:T(8,128)}), f32[8,8,128]{2,1,0:T(8,128)S(1)}, u32[]{:S(2)}, u32[]{:S(2)}) %all-to-all-start.2) | async-done | bytes 32800 | tf_op jit(solution)/shard_map/all_to_all | solution.py:335
  75.7 1.1 shard_map.69
  76.8 12.4 %all_to_all.40.parts_ref = f32[32,16,128]{2,1,0:T(8,128)S(1)} all-to-all(f32[32,16,128]{2,1,0:T(8,128)S(1)} %shard_map.69), channel_id=1, replica_groups=mesh['z'=8,'y'=4,'x'=4,'core'=2] {'y','x','core'}, dimensions={0} | all-to-all | bytes 524288 | tf_op jit(solution)/shard_map/all_to_all | solution.py:335
  89.3 1.1 shard_map.70
  90.4 10.4 %all_to_all.41.parts_ref = f32[8,8,128]{2,1,0:T(8,128)S(1)} all-to-all(f32[8,8,128]{2,1,0:T(8,128)S(1)} %get-tuple-element.29), channel_id=1, replica_groups=mesh['z'=8,'y'=4,'x'=4,'core'=2] {'z'}, dimensions={0} | all-to-all | bytes 65536 | tf_op jit(solution)/shard_map/all_to_all | solution.py:335
  100.8 1.1 shard_map.71
  101.9 12.4 %all_to_all.42.parts_ref = f32[32,16,128]{2,1,0:T(8,128)S(1)} all-to-all(f32[32,16,128]{2,1,0:T(8,128)S(1)} %shard_map.71), channel_id=1, replica_groups=mesh['z'=8,'y'=4,'x'=4,'core'=2] {'y','x','core'}, dimensions={0} | all-to-all | bytes 524288 | tf_op jit(solution)/shard_map/all_to_all | solution.py:335
  114.3 1.0 shard_map.72
  115.3 10.4 %all_to_all.43.parts_ref = f32[8,8,128]{2,1,0:T(8,128)S(1)} all-to-all(f32[8,8,128]{2,1,0:T(8,128)S(1)} %get-tuple-element.30), channel_id=1, replica_groups=mesh['z'=8,'y'=4,'x'=4,'core'=2] {'z'}, dimensions={0} | all-to-all | bytes 65536 | tf_op jit(solution)/shard_map/all_to_all | solution.py:335
  125.7 6.1 %shard_map.73 = (bf16[4,256,384]{2,1,0:T(8,128)(2,1)}, bf16[4,272,384]{2,1,0:T(8,128)(2,1)}, f32[4,8,384]{2,1,0:T(8,128)S(1)}, bf16[512,512]{1,0:T(8,128)(2,1)}) custom-call(s32[3]{0:T(128)S(1)} %pad_add_fusion.here_ref, f32[8,8,128]{2,1,0:T(8,128)S(1)} %all_to_all.43.parts_ref, f32[8,128]{1,0:T(8,128)S(1)} %pad.14.lb_ref, ...), custom_call_target="tpu_custom_call" | custom-call | tf_op jit(solution)/shard_map/pallas_call | solution.py:324
  131.9 0.0 copy-start
  131.9 0.0 copy-start.2
  131.9 0.1 collective-permute-start.10
  132.0 3.9 %all-to-all-start.7 = ((bf16[32,16,512]{2,1,0:T(8,128)(2,1)}), bf16[32,16,512]{2,1,0:T(8,128)(2,1)S(1)}, u32[]{:S(2)}, u32[]{:S(2)}) async-start(bf16[32,16,512]{2,1,0:T(8,128)(2,1)} %bitcast.28), calls=%async_computation.7 | async-start | bytes 1048576 | tf_op jit(solution)/shard_map/all_to_all | solution.py:335
  135.9 2.1 %shard_map.74 = (bf16[4,80,384]{2,1,0:T(8,128)(2,1)S(1)}, bf16[4,80,384]{2,1,0:T(8,128)(2,1)S(1)}, bf16[4,80,384]{2,1,0:T(8,128)(2,1)S(1)}, bf16[4,80,384]{2,1,0:T(8,128)(2,1)S(1)}) custom-call(s32[3]{0:T(128)S(1)} %pad_add_fusion.here_ref, bf16[4,256,384]{2,1,0:T(8,128)(2,1)} %get-tuple-element.35.keep_hbm, f32[4,8,384]{2,1,0:T(8,128)S(1)} %get-tuple-element.36.sums_ref, ...), custom_call_target="tpu_custom_call" | custom-call | tf_op jit(solution)/shard_map/pallas_call | solution.py:324
  138.0 0.6 collective-permute-start.11
  138.6 3.0 %collective-permute-start.12 = (bf16[4,80,384]{2,1,0:T(8,128)(2,1)S(1)}, bf16[4,80,384]{2,1,0:T(8,128)(2,1)S(1)}, u32[]{:S(2)}, u32[]{:S(2)}) collective-permute-start(bf16[4,80,384]{2,1,0:T(8,128)(2,1)S(1)} %get-tuple-element.40), channel_id=1, source_target_pairs={{0,4},{2,6},{4,0},{6,2},{1,5},{3,7},{5,1},{7,3},{8,12},{10,14},{12... | collective-permute-start | bytes 737288 | tf_op jit(solution)/shard_map/ppermute | solution.py:349
  141.6 0.7 collective-permute-start.13
  142.3 4.6 %collective-permute-done.11.refs_1_ = bf16[4,80,384]{2,1,0:T(8,128)(2,1)S(1)} collective-permute-done((bf16[4,80,384]{2,1,0:T(8,128)(2,1)S(1)}, bf16[4,80,384]{2,1,0:T(8,128)(2,1)S(1)}, u32[]{:S(2)}, u32[]{:S(2)}) %collective-permute-start.11) | collective-permute-done | bytes 245792 | tf_op jit(solution)/shard_map/ppermute | solution.py:349
  146.9 2.1 %collective-permute-done.12.refs_2_ = bf16[4,80,384]{2,1,0:T(8,128)(2,1)S(1)} collective-permute-done((bf16[4,80,384]{2,1,0:T(8,128)(2,1)S(1)}, bf16[4,80,384]{2,1,0:T(8,128)(2,1)S(1)}, u32[]{:S(2)}, u32[]{:S(2)}) %collective-permute-start.12) | collective-permute-done | bytes 245792 | tf_op jit(solution)/shard_map/ppermute | solution.py:349
  149.0 4.5 %collective-permute-done.13.refs_3_ = bf16[4,80,384]{2,1,0:T(8,128)(2,1)S(1)} collective-permute-done((bf16[4,80,384]{2,1,0:T(8,128)(2,1)S(1)}, bf16[4,80,384]{2,1,0:T(8,128)(2,1)S(1)}, u32[]{:S(2)}, u32[]{:S(2)}) %collective-permute-start.13) | collective-permute-done | bytes 245792 | tf_op jit(solution)/shard_map/ppermute | solution.py:349
  153.4 0.8 shard_map.75
  154.2 1.5 collective-permute-start.14
  155.7 2.7 %collective-permute-start.15 = (bf16[80,384]{1,0:T(8,128)(2,1)S(1)}, bf16[80,384]{1,0:T(8,128)(2,1)S(1)}, u32[]{:S(2)}, u32[]{:S(2)}) collective-permute-start(bf16[80,384]{1,0:T(8,128)(2,1)S(1)} %get-tuple-element.44), channel_id=1, source_target_pairs={{0,16},{8,24},{16,0},{24,8},{1,17},{9,25},{17,1},{25,9},{2,18},{10... | collective-permute-start | bytes 184328 | tf_op jit(solution)/shard_map/ppermute | solution.py:349
  158.3 1.5 collective-permute-start.16
  159.8 0.7 shard_map.77
  160.6 1.0 collective-permute-done.15.refs_2_
  161.6 1.0 collective-permute-done.16.refs_3_
  162.6 1.2 shard_map.76
  163.8 0.6 reduce
  (32 shorter events, 0.1 us)
Async XLA Ops:
  2.4 34.1 %all-to-all-start = ((bf16[32,16,512]{2,1,0:T(8,128)(2,1)}), bf16[32,16,512]{2,1,0:T(8,128)(2,1)S(1)}, u32[]{:S(2)}, u32[]{:S(2)}) async-start(bf16[32,16,512]{2,1,0:T(8,128)(2,1)} %bitcast.8), calls=%async_computation | async-start | bytes 1048576 | tf_op jit(solution)/shard_map/all_to_all | solution.py:335
  13.9 6.6 %collective-permute-start.1 = (bf16[64,384]{1,0:T(8,128)(2,1)}, bf16[64,384]{1,0:T(8,128)(2,1)S(1)}, u32[]{:S(2)}, u32[]{:S(2)}) collective-permute-start(bf16[64,384]{1,0:T(8,128)(2,1)} %refs_4_.1), channel_id=1, source_target_pairs={{0,16},{8,24},{16,0},{24,8},{1,17},{9,25},{17,1},{25,9},{2,18},{10... | collective-permute-start | bytes 147464 | tf_op jit(solution)/shard_map/ppermute | solution.py:349
  17.2 5.5 %collective-permute-start = (bf16[64,384]{1,0:T(8,128)(2,1)}, bf16[64,384]{1,0:T(8,128)(2,1)S(1)}, u32[]{:S(2)}, u32[]{:S(2)}) collective-permute-start(bf16[64,384]{1,0:T(8,128)(2,1)} %refs_4_.1), channel_id=1, source_target_pairs={{0,8},{8,16},{16,24},{24,0},{1,9},{9,17},{17,25},{25,1},{2,10},{10... | collective-permute-start | bytes 147464 | tf_op jit(solution)/shard_map/ppermute | solution.py:349
  17.8 5.1 %collective-permute-start.2 = (bf16[64,384]{1,0:T(8,128)(2,1)}, bf16[64,384]{1,0:T(8,128)(2,1)S(1)}, u32[]{:S(2)}, u32[]{:S(2)}) collective-permute-start(bf16[64,384]{1,0:T(8,128)(2,1)} %refs_4_.1), channel_id=1, source_target_pairs={{0,24},{8,0},{16,8},{24,16},{1,25},{9,1},{17,9},{25,17},{2,26},{10... | collective-permute-start | bytes 147464 | tf_op jit(solution)/shard_map/ppermute | solution.py:349
  23.8 14.2 %copy-start.5 = (bf16[4,64,384]{2,1,0:T(8,128)(2,1)}, bf16[4,64,384]{2,1,0:T(8,128)(2,1)S(1)}, u32[]{:S(2)}) copy-start(bf16[4,64,384]{2,1,0:T(8,128)(2,1)S(1)} %pad_maximum_fusion.refs_0_) | copy-start | bytes 589828
  23.8 43.9 %copy-start.3 = (f32[2048]{0:T(1024)S(1)}, f32[2048]{0:T(1024)}, u32[]{:S(2)}) copy-start(f32[2048]{0:T(1024)} %param.7) | copy-start | bytes 24580
  23.8 7.9 %collective-permute-start.5 = (bf16[4,64,384]{2,1,0:T(8,128)(2,1)S(1)}, bf16[4,64,384]{2,1,0:T(8,128)(2,1)S(1)}, u32[]{:S(2)}, u32[]{:S(2)}) collective-permute-start(bf16[4,64,384]{2,1,0:T(8,128)(2,1)S(1)} %pad_maximum_fusion.refs_0_), channel_id=1, source_target_pairs={{0,6},{2,0},{4,2},{6,4},{1,7},{3,1},{5,3},{7,5},{8,14},{10,8},{12,... | collective-permute-start | bytes 589832 | tf_op jit(solution)/shard_map/ppermute | solution.py:349
  24.4 9.8 %collective-permute-start.4 = (bf16[4,64,384]{2,1,0:T(8,128)(2,1)S(1)}, bf16[4,64,384]{2,1,0:T(8,128)(2,1)S(1)}, u32[]{:S(2)}, u32[]{:S(2)}) collective-permute-start(bf16[4,64,384]{2,1,0:T(8,128)(2,1)S(1)} %pad_maximum_fusion.refs_0_), channel_id=1, source_target_pairs={{0,4},{2,6},{4,0},{6,2},{1,5},{3,7},{5,1},{7,3},{8,12},{10,14},{12... | collective-permute-start | bytes 589832 | tf_op jit(solution)/shard_map/ppermute | solution.py:349
  26.8 8.2 %collective-permute-start.3 = (bf16[4,64,384]{2,1,0:T(8,128)(2,1)S(1)}, bf16[4,64,384]{2,1,0:T(8,128)(2,1)S(1)}, u32[]{:S(2)}, u32[]{:S(2)}) collective-permute-start(bf16[4,64,384]{2,1,0:T(8,128)(2,1)S(1)} %pad_maximum_fusion.refs_0_), channel_id=1, source_target_pairs={{0,2},{2,4},{4,6},{6,0},{1,3},{3,5},{5,7},{7,1},{8,10},{10,12},{12... | collective-permute-start | bytes 589832 | tf_op jit(solution)/shard_map/ppermute | solution.py:349
  28.6 7.2 %collective-permute-start.6 = (bf16[4,64,384]{2,1,0:T(8,128)(2,1)S(1)}, bf16[4,64,384]{2,1,0:T(8,128)(2,1)S(1)}, u32[]{:S(2)}, u32[]{:S(2)}) collective-permute-start(bf16[4,64,384]{2,1,0:T(8,128)(2,1)S(1)} %pad_maximum_fusion.refs_0_), channel_id=1, source_target_pairs={{0,1},{1,0},{2,3},{3,2},{4,5},{5,4},{6,7},{7,6},{8,9},{9,8},{10,11... | collective-permute-start | bytes 589832 | tf_op jit(solution)/shard_map/ppermute | solution.py:344
  31.7 4.8 %copy-start.6 = (bf16[4,64,384]{2,1,0:T(8,128)(2,1)}, bf16[4,64,384]{2,1,0:T(8,128)(2,1)S(1)}, u32[]{:S(2)}) copy-start(bf16[4,64,384]{2,1,0:T(8,128)(2,1)S(1)} %collective-permute-done.5.refs_3_) | copy-start | bytes 589828
  31.7 4.2 %collective-permute-start.9 = (bf16[4,64,384]{2,1,0:T(8,128)(2,1)S(1)}, bf16[4,64,384]{2,1,0:T(8,128)(2,1)S(1)}, u32[]{:S(2)}, u32[]{:S(2)}) collective-permute-start(bf16[4,64,384]{2,1,0:T(8,128)(2,1)S(1)} %collective-permute-done.5.refs_3_), channel_id=1, source_target_pairs={{0,1},{1,0},{2,3},{3,2},{4,5},{5,4},{6,7},{7,6},{8,9},{9,8},{10,11... | collective-permute-start | bytes 589832 | tf_op jit(solution)/shard_map/ppermute | solution.py:344
  34.2 2.3 %copy-start.7 = (bf16[4,64,384]{2,1,0:T(8,128)(2,1)}, bf16[4,64,384]{2,1,0:T(8,128)(2,1)S(1)}, u32[]{:S(2)}) copy-start(bf16[4,64,384]{2,1,0:T(8,128)(2,1)S(1)} %collective-permute-done.4.refs_2_) | copy-start | bytes 589828
  34.2 1.7 %collective-permute-start.8 = (bf16[4,64,384]{2,1,0:T(8,128)(2,1)S(1)}, bf16[4,64,384]{2,1,0:T(8,128)(2,1)S(1)}, u32[]{:S(2)}, u32[]{:S(2)}) collective-permute-start(bf16[4,64,384]{2,1,0:T(8,128)(2,1)S(1)} %collective-permute-done.4.refs_2_), channel_id=1, source_target_pairs={{0,1},{1,0},{2,3},{3,2},{4,5},{5,4},{6,7},{7,6},{8,9},{9,8},{10,11... | collective-permute-start | bytes 589832 | tf_op jit(solution)/shard_map/ppermute | solution.py:344
  35.0 1.5 copy-start.8
  35.0 1.4 collective-permute-start.7
  35.8 0.7 copy-start.9
  35.8 0.8 copy-start.10
  35.8 0.8 copy-start.11
  36.5 0.7 copy-start.12
  37.1 0.8 copy-start.4
  42.5 0.7 copy-start.1
  43.2 15.5 %all-to-all-start.1 = ((f32[32,16,128]{2,1,0:T(8,128)}), f32[32,16,128]{2,1,0:T(8,128)S(1)}, u32[]{:S(2)}, u32[]{:S(2)}) async-start(f32[32,16,128]{2,1,0:T(8,128)} %copy-done.1), calls=%async_computation.1 | async-start | bytes 524288 | tf_op jit(solution)/shard_map/all_to_all | solution.py:335
  60.4 15.3 %all-to-all-start.2 = ((f32[8,8,128]{2,1,0:T(8,128)}), f32[8,8,128]{2,1,0:T(8,128)S(1)}, u32[]{:S(2)}, u32[]{:S(2)}) async-start(f32[8,8,128]{2,1,0:T(8,128)} %get-tuple-element.28), calls=%async_computation.2 | async-start | bytes 65536 | tf_op jit(solution)/shard_map/all_to_all | solution.py:335
  131.9 28.0 %copy-start = (bf16[16,2048]{1,0:T(8,128)(2,1)S(1)}, bf16[16,2048]{1,0:T(8,128)(2,1)}, u32[]{:S(2)}) copy-start(bf16[16,2048]{1,0:T(8,128)(2,1)} %y_ref.1) | copy-start | bytes 196612
  131.9 30.7 %copy-start.2 = (bf16[64,384]{1,0:T(8,128)(2,1)S(1)}, bf16[64,384]{1,0:T(8,128)(2,1)}, u32[]{:S(2)}) copy-start(bf16[64,384]{1,0:T(8,128)(2,1)} %refs_4_.1) | copy-start | bytes 147460
  131.9 4.0 %collective-permute-start.10 = (bf16[4,272,384]{2,1,0:T(8,128)(2,1)}, bf16[4,272,384]{2,1,0:T(8,128)(2,1)S(1)}, u32[]{:S(2)}, u32[]{:S(2)}) collective-permute-start(bf16[4,272,384]{2,1,0:T(8,128)(2,1)} %get-tuple-element.37), channel_id=1, source_target_pairs={{0,1},{1,0},{2,3},{3,2},{4,5},{5,4},{6,7},{7,6},{8,9},{9,8},{10,11... | collective-permute-start | bytes 2506760 | tf_op jit(solution)/shard_map/ppermute | solution.py:344
  132.0 27.8 %all-to-all-start.7 = ((bf16[32,16,512]{2,1,0:T(8,128)(2,1)}), bf16[32,16,512]{2,1,0:T(8,128)(2,1)S(1)}, u32[]{:S(2)}, u32[]{:S(2)}) async-start(bf16[32,16,512]{2,1,0:T(8,128)(2,1)} %bitcast.28), calls=%async_computation.7 | async-start | bytes 1048576 | tf_op jit(solution)/shard_map/all_to_all | solution.py:335
  138.0 8.9 %collective-permute-start.11 = (bf16[4,80,384]{2,1,0:T(8,128)(2,1)S(1)}, bf16[4,80,384]{2,1,0:T(8,128)(2,1)S(1)}, u32[]{:S(2)}, u32[]{:S(2)}) collective-permute-start(bf16[4,80,384]{2,1,0:T(8,128)(2,1)S(1)} %get-tuple-element.39), channel_id=1, source_target_pairs={{0,2},{2,4},{4,6},{6,0},{1,3},{3,5},{5,7},{7,1},{8,10},{10,12},{12... | collective-permute-start | bytes 737288 | tf_op jit(solution)/shard_map/ppermute | solution.py:349
  138.6 10.4 %collective-permute-start.12 = (bf16[4,80,384]{2,1,0:T(8,128)(2,1)S(1)}, bf16[4,80,384]{2,1,0:T(8,128)(2,1)S(1)}, u32[]{:S(2)}, u32[]{:S(2)}) collective-permute-start(bf16[4,80,384]{2,1,0:T(8,128)(2,1)S(1)} %get-tuple-element.40), channel_id=1, source_target_pairs={{0,4},{2,6},{4,0},{6,2},{1,5},{3,7},{5,1},{7,3},{8,12},{10,14},{12... | collective-permute-start | bytes 737288 | tf_op jit(solution)/shard_map/ppermute | solution.py:349
  141.6 11.9 %collective-permute-start.13 = (bf16[4,80,384]{2,1,0:T(8,128)(2,1)S(1)}, bf16[4,80,384]{2,1,0:T(8,128)(2,1)S(1)}, u32[]{:S(2)}, u32[]{:S(2)}) collective-permute-start(bf16[4,80,384]{2,1,0:T(8,128)(2,1)S(1)} %get-tuple-element.41), channel_id=1, source_target_pairs={{0,6},{2,0},{4,2},{6,4},{1,7},{3,1},{5,3},{7,5},{8,14},{10,8},{12,... | collective-permute-start | bytes 737288 | tf_op jit(solution)/shard_map/ppermute | solution.py:349
  154.2 6.4 %collective-permute-start.14 = (bf16[80,384]{1,0:T(8,128)(2,1)S(1)}, bf16[80,384]{1,0:T(8,128)(2,1)S(1)}, u32[]{:S(2)}, u32[]{:S(2)}) collective-permute-start(bf16[80,384]{1,0:T(8,128)(2,1)S(1)} %get-tuple-element.43), channel_id=1, source_target_pairs={{0,8},{8,16},{16,24},{24,0},{1,9},{9,17},{17,25},{25,1},{2,10},{10... | collective-permute-start | bytes 184328 | tf_op jit(solution)/shard_map/ppermute | solution.py:349
  155.7 5.9 %collective-permute-start.15 = (bf16[80,384]{1,0:T(8,128)(2,1)S(1)}, bf16[80,384]{1,0:T(8,128)(2,1)S(1)}, u32[]{:S(2)}, u32[]{:S(2)}) collective-permute-start(bf16[80,384]{1,0:T(8,128)(2,1)S(1)} %get-tuple-element.44), channel_id=1, source_target_pairs={{0,16},{8,24},{16,0},{24,8},{1,17},{9,25},{17,1},{25,9},{2,18},{10... | collective-permute-start | bytes 184328 | tf_op jit(solution)/shard_map/ppermute | solution.py:349
  158.3 4.2 %collective-permute-start.16 = (bf16[80,384]{1,0:T(8,128)(2,1)S(1)}, bf16[80,384]{1,0:T(8,128)(2,1)S(1)}, u32[]{:S(2)}, u32[]{:S(2)}) collective-permute-start(bf16[80,384]{1,0:T(8,128)(2,1)S(1)} %get-tuple-element.45), channel_id=1, source_target_pairs={{0,24},{8,0},{16,8},{24,16},{1,25},{9,1},{17,9},{25,17},{2,26},{10... | collective-permute-start | bytes 184328 | tf_op jit(solution)/shard_map/ppermute | solution.py:349

commit v3 on v2

--- a/solution.py
+++ b/solution.py
@@ -33,10 +33,6 @@
 def merged(parts):
     high = jnp.max(parts, axis=0)
     return high + log2_of(jnp.sum(jnp.exp2(parts - high[None]), axis=0))
-
-
-def rows_of_tiles(vec, tiles):
-    return [vec[:, t * LANES : (t + 1) * LANES] for t in range(tiles)]
 
 
 def to_column(lines, column_ref, tiles):
@@ -101,23 +97,28 @@
         lines_ref[t : t + 1, :] = square[0:1, :]
 
 
+def gather_moves(nrow):
+    return ((0, 0), (1, 0), (3, 0), (2, 0), (2, nrow // 2))
+
+
 def setup_kernel(scale, grid, here_ref, *refs):
     nrow, ncol, depth, width = grid
-    own_refs, other_refs = refs[:ncol], refs[ncol : 2 * ncol]
-    y_hbm, la_ref, d_ref, sqx_ref, sqy_ref, out_ref, x_hbm, x_ref, y_ref, column_ref, lines_ref, sems = refs[2 * ncol :]
+    moves = gather_moves(nrow)
+    own_refs, other_refs = refs[: len(moves)], refs[len(moves) : 2 * len(moves)]
+    y_hbm, la_ref, d_ref, sqx_ref, sqy_ref, out_ref, x_hbm, x_ref, y_ref, column_ref, lines_ref, sems = refs[2 * len(moves) :]
     core, across, along = here_ref[0], here_ref[1], here_ref[2]
     fetch_y = pltpu.make_async_copy(y_hbm, y_ref, sems.at[0])
     fetch_y.start()
     copies, n = [], 1
     for side, group in ((core, own_refs), (1 - core, other_refs)):
-        for sx in range(ncol):
+        for (sx, first), ref in zip(moves, group):
             c = lax.rem(across - sx + ncol, ncol)
             at = pl.multiple_of((2 * c + side) * depth, depth)
-            for sy in range(nrow):
-                r = lax.rem(along - sy + nrow, nrow)
+            for k in range(ref.shape[0]):
+                r = lax.rem(along - (first + k) + nrow, nrow)
                 lanes = pl.multiple_of(r * width, LANES)
                 copy = pltpu.make_async_copy(
-                    group[sx].at[sy], x_ref.at[pl.ds(at, depth), pl.ds(lanes, width)], sems.at[n])
+                    ref.at[k], x_ref.at[pl.ds(at, depth), pl.ds(lanes, width)], sems.at[n])
                 copy.start()
                 copies.append(copy)
                 n += 1
@@ -266,31 +267,41 @@
     outs, keep_ref, sems = refs[:-2], refs[-2], refs[-1]
     fetch = pltpu.make_async_copy(keep_hbm, keep_ref, sems.at[0])
     fetch.start()
-    nrow, deep, width = outs[0].shape
-    depth, ncol = deep - 16, len(outs)
-    half = ncol * depth
+    nrow, deep, _ = outs[0].shape
+    half = keep_ref.shape[1]
+    depth = deep - 16
+    ncol = half // depth
     across = here_ref[1]
-    fetch.wait()
+    totals = []
     for r in range(nrow):
         extra = got_ref[r, half : half + 16]
-        totals = [sums_ref[r, n : n + 1] + pieces_sum(extra, n) for n in range(2)]
-        for s, out in enumerate(outs):
-            c = lax.rem(across + s, ncol)
-            at = pl.ds(pl.multiple_of(c * depth, depth), depth)
-            out[r, :depth] = (keep_ref[r, at].astype(F32) + got_ref[r, at].astype(F32)).astype(BF16)
-            put_pieces(out, (r,), depth, totals)
+        totals.append([sums_ref[r, n : n + 1] + pieces_sum(extra, n) for n in range(2)])
+    fetch.wait()
+    for (s, first), out in zip(gather_moves(nrow), outs):
+        c = lax.rem(across + s, ncol)
+        at = pl.ds(pl.multiple_of(c * depth, depth), depth)
+        for k in range(out.shape[0]):
+            r = first + k
+            out[k, :depth] = (keep_ref[r, at].astype(F32) + got_ref[r, at].astype(F32)).astype(BF16)
+            put_pieces(out, (k,), depth, totals[r])
 
 
 def across_kernel(here_ref, *refs):
-    ins, outs = refs[: len(refs) // 2], refs[len(refs) // 2 :]
-    nrow, deep, width = ins[0].shape
+    moves = gather_moves(refs[0].shape[0])
+    ins, outs = refs[: len(moves)], refs[len(moves) : 2 * len(moves) - 1]
+    total_ref, extra_ref = refs[2 * len(moves) - 1 :]
+    nrow, deep, _ = ins[0].shape
     depth = deep - 16
     along = here_ref[2]
+    for r in range(nrow):
+        ends = [ins[0][r], ins[1][r], ins[3 + 2 * r // nrow][r % (nrow // 2)], ins[2][r]]
+        total_ref[r] = balanced([one[:depth].astype(F32) for one in ends])
+        for n in range(2):
+            extra_ref[r, n : n + 1] = balanced([pieces_sum(one[depth:deep], n) for one in ends])
     for s, out in enumerate(outs):
         r = lax.rem(along + s, nrow)
-        out[:depth] = balanced([one[r, :depth].astype(F32) for one in ins]).astype(BF16)
-        extras = [one[r, depth:deep] for one in ins]
-        put_pieces(out, (), depth, [balanced([pieces_sum(extra, n) for extra in extras]) for n in range(2)])
+        out[:depth] = total_ref[r].astype(BF16)
+        put_pieces(out, (), depth, [extra_ref[r, n : n + 1] for n in range(2)])
 
 
 def roll_kernel(here_ref, *refs):
@@ -361,11 +372,15 @@
     quarter = lax.axis_index("y")
     here = jnp.stack([lax.axis_index(a).astype(jnp.int32) for a in ("core", "x", "y")])
 
+    x_line = [roll_embed] + [shifted(roll_embed, "y", s) for s in range(1, ny)]
     y_blocks = jnp.moveaxis(expert_embed.reshape(thin, ny, cols), 1, 0)
     y_send = jnp.broadcast_to(y_blocks[None], (nz, ny, thin, cols)).reshape(nz * ny, thin, cols)
-    y_all = exchanged(y_send, ("z", "y")).reshape(emb, cols)
-    x_line = jnp.stack([roll_embed] + [shifted(roll_embed, "y", s) for s in range(1, ny)])
-    x_own = [x_line] + [shifted(x_line, "x", s) for s in range(1, nx)]
+    y_all = exchanged(y_send, ("z", "y"))
+    y_all = y_all.reshape(emb, cols)
+    middle = ny // 2
+    x_line = jnp.stack(x_line)
+    behind, ahead = shifted(x_line, "x", 1), shifted(x_line, "x", -1)
+    x_own = [x_line, behind, ahead, shifted(behind[:middle], "x", 1), shifted(ahead[middle:], "x", -1)]
     x_other = [swapped(x) for x in x_own]
 
     wtiles = width // LANES
@@ -383,7 +398,7 @@
         [((cols, rows), F32), ((f_lines, LANES), F32), ((g_lines, LANES), F32), (f_shape, F32),
          ((emb, rows), BF16)],
         [((emb, rows), BF16), ((emb, cols), BF16), column, ((f_lines, LANES), F32)],
-        *ins, smem=1, far=range(1, 2 * nx + 2), far_out=(4,), sems=2 * nx * ny + 2, limit=24 << 20)
+        *ins, smem=1, far=range(1, 12), far_out=(4,), sems=2 * nx * ny + 2, limit=24 << 20)
     la = None
     for step in range(ITERS):
         if step:
@@ -406,10 +421,14 @@
         here, got, lb, f, sqx, sqy, d, y_all, x_all, smem=1, far=(7, 8), far_out=(0, 3), sems=4, limit=32 << 20)
     xsum_got = exchanged(xsum.reshape(nz * ny, thin, cols), ("z", "y"))
     line = ((ny, depth + 16, width), BF16)
-    pairs = call(pair_kernel, [line] * nx, [((ny, half, width), BF16)], here, keep, sums, swapped(send),
-                 smem=1, far=(1,), sems=1, limit=16 << 20)
-    lines = [pairs[0]] + [shifted(pairs[s], "x", s) for s in range(1, nx)]
-    ends = call(across_kernel, [(line[0][1:], BF16)] * ny, [], here, *lines, smem=1, limit=16 << 20)
+    short = ((middle, depth + 16, width), BF16)
+    own, one, three, two, other_two = call(
+        pair_kernel, [line] * 3 + [short] * 2, [((ny, half, width), BF16)], here, keep, sums, swapped(send),
+        smem=1, far=(1,), sems=1, limit=16 << 20)
+    two, other_two = shifted(two, "x", 1), shifted(other_two, "x", -1)
+    lines = [own, shifted(one, "x", 1), shifted(three, "x", -1), shifted(two, "x", 1), shifted(other_two, "x", -1)]
+    ends = call(across_kernel, [(line[0][1:], BF16)] * ny, [((ny, depth, width), F32), ((ny, 8, width), F32)],
+                here, *lines, smem=1, limit=16 << 20)
     ends = [ends[0]] + [shifted(ends[s], "y", s) for s in range(1, ny)]
     roll_pull, reward = call(roll_kernel, [((depth, width), F32), ((1, width), F32)], [],
                              here, *ends, roll_embed, smem=1, limit=8 << 20)
@@ -423,6 +442,7 @@
     z, y = 8, 4
     torus = Mesh(mesh.devices.reshape(z, y, 4, 2), ("z", "y", "x", "core"))
     row, col = ("z", "y"), ("x", "core")
+
     return jax.shard_map(
         shards,
         mesh=torus,

time: 166 us -> 167 us (level)
  waiting for transfers between devices: 38.1 us -> 35.8 us
  starting transfers between devices: 52.1 us -> 54.3 us
    ppermute x12 -> x16, waiting for transfers between devices: 22 us -> 19.1 us  [shifted(): return lax.ppermute(x, axis, [(i, (i + by) % n) for i in range(n)])]
    ppermute x12 -> x16, starting transfers between devices: 21.4 us -> 23.3 us  [shifted(): return lax.ppermute(x, axis, [(i, (i + by) % n) for i in range(n)])]
  transfers between devices with their start and end apart: 21 -> 26, of which waited for: 13 -> 14; matrix products, arithmetic and copies ran while one was open for 1% -> 1% of each run, Pallas kernels for 2% -> 2%
where the time goes in v3:
time: 167 us; the launch traced here: 164 us
  starting transfers between devices  54.3 us (33%)
  blocking collectives  45.6 us (27%)
  waiting for transfers between devices  35.8 us (21%)
  Pallas kernels  21.4 us (13%)
  local copies, waits for them, and re-layouts  4 us (2%)
  other arithmetic  2.27 us (1%)
    all_to_all x4, blocking collectives, exchanged(): return lax.all_to_all(x, axes, split_axis=0, concat_axis=0, tiled=True)  45.6 us
    all_to_all x4, starting transfers between devices, exchanged(): return lax.all_to_all(x, axes, split_axis=0, concat_axis=0, tiled=True)  30.4 us
    ppermute x16, starting transfers between devices, shifted(): return lax.ppermute(x, axis, [(i, (i + by) % n) for i in range(n)])  23.3 us
    pallas_call x11, Pallas kernels, call(): pl.pallas_call(body, out_shape=[pltpu.HBM(s, t) if n in far_out else jax....  21.4 us
    ppermute x16, waiting for transfers between devices, shifted(): return lax.ppermute(x, axis, [(i, (i + by) % n) for i in range(n)])  19.1 us
    all_to_all x4, waiting for transfers between devices, exchanged(): return lax.all_to_all(x, axes, split_axis=0, concat_axis=0, tiled=True)  15.5 us
  transfers between devices with their start and end apart: 26, of which 14 were waited for; matrix products, arithmetic and copies ran while one was open for 1% of the time, Pallas kernels for 2%

profile of v3, /device:TPU:2, one launch (start us, length us, event | category | flops | bytes accessed | tf_op | source)
XLA Modules:
  0.0 164.4 jit_solution(9375477343022666849)
XLA Ops:
  0.6 0.9 reshape.37
  1.5 0.9 broadcast_in_dim.2
  2.4 11.5 %all-to-all-start = ((bf16[32,16,512]{2,1,0:T(8,128)(2,1)}), bf16[32,16,512]{2,1,0:T(8,128)(2,1)S(1)}, u32[]{:S(2)}, u32[]{:S(2)}) async-start(bf16[32,16,512]{2,1,0:T(8,128)(2,1)} %bitcast.8), calls=%async_computation | async-start | bytes 1048576 | tf_op jit(solution)/shard_map/all_to_all | solution.py:346
  13.9 3.4 %collective-permute-start.1 = (bf16[64,384]{1,0:T(8,128)(2,1)}, bf16[64,384]{1,0:T(8,128)(2,1)S(1)}, u32[]{:S(2)}, u32[]{:S(2)}) collective-permute-start(bf16[64,384]{1,0:T(8,128)(2,1)} %refs_4_.1), channel_id=1, source_target_pairs={{0,16},{8,24},{16,0},{24,8},{1,17},{9,25},{17,1},{25,9},{2,18},{10... | collective-permute-start | bytes 147464 | tf_op jit(solution)/shard_map/ppermute | solution.py:360
  17.3 0.6 collective-permute-start
  17.8 2.7 %collective-permute-start.2 = (bf16[64,384]{1,0:T(8,128)(2,1)}, bf16[64,384]{1,0:T(8,128)(2,1)S(1)}, u32[]{:S(2)}, u32[]{:S(2)}) collective-permute-start(bf16[64,384]{1,0:T(8,128)(2,1)} %refs_4_.1), channel_id=1, source_target_pairs={{0,24},{8,0},{16,8},{24,16},{1,25},{9,1},{17,9},{25,17},{2,26},{10... | collective-permute-start | bytes 147464 | tf_op jit(solution)/shard_map/ppermute | solution.py:360
  20.5 2.3 %collective-permute-done = bf16[64,384]{1,0:T(8,128)(2,1)S(1)} collective-permute-done((bf16[64,384]{1,0:T(8,128)(2,1)}, bf16[64,384]{1,0:T(8,128)(2,1)S(1)}, u32[]{:S(2)}, u32[]{:S(2)}) %collective-permute-start) | collective-permute-done | bytes 49184 | tf_op jit(solution)/shard_map/ppermute | solution.py:360
  22.8 0.1 collective-permute-done.2
  23.0 0.8 pad_maximum_fusion.refs_0_
  23.8 0.6 collective-permute-start.4
  24.4 1.5 collective-permute-start.3
  25.9 3.6 %collective-permute-done.4.refs_2_ = bf16[4,64,384]{2,1,0:T(8,128)(2,1)S(1)} collective-permute-done((bf16[4,64,384]{2,1,0:T(8,128)(2,1)S(1)}, bf16[4,64,384]{2,1,0:T(8,128)(2,1)S(1)}, u32[]{:S(2)}, u32[]{:S(2)}) %collective-permute-start.4) | collective-permute-done | bytes 196640 | tf_op jit(solution)/shard_map/ppermute | solution.py:360
  29.6 0.9 collective-permute-start.6
  30.5 0.4 collective-permute-done.3.refs_1_
  30.8 0.0 copy-start.3
  30.9 0.9 collective-permute-start.5
  31.8 0.5 collective-permute-start.8
  32.3 0.7 multiply_bitcast_fusion.1
  33.0 1.3 collective-permute-done.6.refs_4_
  34.3 2.6 %collective-permute-done.5.refs_3_ = bf16[2,64,384]{2,1,0:T(8,128)(2,1)S(1)} collective-permute-done((bf16[2,64,384]{2,1,0:T(8,128)(2,1)S(1)}, bf16[2,64,384]{2,1,0:T(8,128)(2,1)S(1)}, u32[]{:S(2)}, u32[]{:S(2)}) %collective-permute-start.5) | collective-permute-done | bytes 98336 | tf_op jit(solution)/shard_map/ppermute | solution.py:360
  36.9 0.1 pad_add_fusion.here_ref
  37.0 1.2 collective-permute-done.10.refs_8_
  38.2 0.6 copy-done.14
  38.8 0.1 copy-done.10
  38.9 0.8 copy-done.4
  39.7 4.5 %shard_map.67 = (f32[512,1536]{1,0:T(8,128)S(1)}, f32[16,128]{1,0:T(8,128)S(1)}, f32[8,128]{1,0:T(8,128)S(1)}, f32[32,16,128]{2,1,0:T(8,128)S(1)}, bf16[512,1536]{1,0:T(8,128)(2,1)}) custom-call(s32[3]{0:T(128)S(1)} %pad_add_fusion.here_ref, bf16[4,64,384]{2,1,0:T(8,128)(2,1)} %copy-done.5, bf16[4,64,384]{2,1,0:T(8,128)(2,1)} %copy-done.7, ...), custom_call_target="tpu_custom_call" | custom-call | tf_op jit(solution)/shard_map/pallas_call | solution.py:335
  44.2 0.7 copy-done.1
  44.9 8.3 %all-to-all-start.1 = ((f32[32,16,128]{2,1,0:T(8,128)}), f32[32,16,128]{2,1,0:T(8,128)S(1)}, u32[]{:S(2)}, u32[]{:S(2)}) async-start(f32[32,16,128]{2,1,0:T(8,128)} %copy-done.1), calls=%async_computation.1 | async-start | bytes 524288 | tf_op jit(solution)/shard_map/all_to_all | solution.py:346
  53.3 7.6 %all-to-all-done.1.parts_ref = f32[32,16,128]{2,1,0:T(8,128)S(1)} async-done(((f32[32,16,128]{2,1,0:T(8,128)}), f32[32,16,128]{2,1,0:T(8,128)S(1)}, u32[]{:S(2)}, u32[]{:S(2)}) %all-to-all-start.1) | async-done | bytes 262176 | tf_op jit(solution)/shard_map/all_to_all | solution.py:346
  60.9 1.6 shard_map.68
  62.5 6.7 %all-to-all-start.2 = ((f32[8,8,128]{2,1,0:T(8,128)}), f32[8,8,128]{2,1,0:T(8,128)S(1)}, u32[]{:S(2)}, u32[]{:S(2)}) async-start(f32[8,8,128]{2,1,0:T(8,128)} %get-tuple-element.29), calls=%async_computation.2 | async-start | bytes 65536 | tf_op jit(solution)/shard_map/all_to_all | solution.py:346
  69.2 0.1 multiply_bitcast_fusion
  69.3 7.9 %all-to-all-done.2.parts_ref = f32[8,8,128]{2,1,0:T(8,128)S(1)} async-done(((f32[8,8,128]{2,1,0:T(8,128)}), f32[8,8,128]{2,1,0:T(8,128)S(1)}, u32[]{:S(2)}, u32[]{:S(2)}) %all-to-all-start.2) | async-done | bytes 32800 | tf_op jit(solution)/shard_map/all_to_all | solution.py:346
  77.2 1.1 shard_map.69
  78.3 12.4 %all_to_all.40.parts_ref = f32[32,16,128]{2,1,0:T(8,128)S(1)} all-to-all(f32[32,16,128]{2,1,0:T(8,128)S(1)} %shard_map.69), channel_id=1, replica_groups=mesh['z'=8,'y'=4,'x'=4,'core'=2] {'y','x','core'}, dimensions={0} | all-to-all | bytes 524288 | tf_op jit(solution)/shard_map/all_to_all | solution.py:346
  90.8 1.1 shard_map.70
  91.9 10.4 %all_to_all.41.parts_ref = f32[8,8,128]{2,1,0:T(8,128)S(1)} all-to-all(f32[8,8,128]{2,1,0:T(8,128)S(1)} %get-tuple-element.30), channel_id=1, replica_groups=mesh['z'=8,'y'=4,'x'=4,'core'=2] {'z'}, dimensions={0} | all-to-all | bytes 65536 | tf_op jit(solution)/shard_map/all_to_all | solution.py:346
  102.3 1.1 shard_map.71
  103.4 12.4 %all_to_all.42.parts_ref = f32[32,16,128]{2,1,0:T(8,128)S(1)} all-to-all(f32[32,16,128]{2,1,0:T(8,128)S(1)} %shard_map.71), channel_id=1, replica_groups=mesh['z'=8,'y'=4,'x'=4,'core'=2] {'y','x','core'}, dimensions={0} | all-to-all | bytes 524288 | tf_op jit(solution)/shard_map/all_to_all | solution.py:346
  115.8 1.0 shard_map.72
  116.8 10.4 %all_to_all.43.parts_ref = f32[8,8,128]{2,1,0:T(8,128)S(1)} all-to-all(f32[8,8,128]{2,1,0:T(8,128)S(1)} %get-tuple-element.31), channel_id=1, replica_groups=mesh['z'=8,'y'=4,'x'=4,'core'=2] {'z'}, dimensions={0} | all-to-all | bytes 65536 | tf_op jit(solution)/shard_map/all_to_all | solution.py:346
  127.2 6.1 %shard_map.73 = (bf16[4,256,384]{2,1,0:T(8,128)(2,1)}, bf16[4,272,384]{2,1,0:T(8,128)(2,1)}, f32[4,8,384]{2,1,0:T(8,128)S(1)}, bf16[512,512]{1,0:T(8,128)(2,1)}) custom-call(s32[3]{0:T(128)S(1)} %pad_add_fusion.here_ref, f32[8,8,128]{2,1,0:T(8,128)S(1)} %all_to_all.43.parts_ref, f32[8,128]{1,0:T(8,128)S(1)} %pad.14.lb_ref, ...), custom_call_target="tpu_custom_call" | custom-call | tf_op jit(solution)/shard_map/pallas_call | solution.py:335
  133.3 0.0 copy-start
  133.3 0.1 collective-permute-start.12
  133.4 3.9 %all-to-all-start.7 = ((bf16[32,16,512]{2,1,0:T(8,128)(2,1)}), bf16[32,16,512]{2,1,0:T(8,128)(2,1)S(1)}, u32[]{:S(2)}, u32[]{:S(2)}) async-start(bf16[32,16,512]{2,1,0:T(8,128)(2,1)} %bitcast.28), calls=%async_computation.7 | async-start | bytes 1048576 | tf_op jit(solution)/shard_map/all_to_all | solution.py:346
  137.4 2.0 %shard_map.74 = (bf16[4,80,384]{2,1,0:T(8,128)(2,1)S(1)}, bf16[4,80,384]{2,1,0:T(8,128)(2,1)S(1)}, bf16[4,80,384]{2,1,0:T(8,128)(2,1)S(1)}, bf16[2,80,384]{2,1,0:T(8,128)(2,1)S(1)}, bf16[2,80,384]{2,1,0:T(8,128)(2,1)S(1)}) custom-call(s32[3]{0:T(128)S(1)} %pad_add_fusion.here_ref, bf16[4,256,384]{2,1,0:T(8,128)(2,1)} %get-tuple-element.36.keep_hbm, ...), custom_call_target="tpu_custom_call" | custom-call | tf_op jit(solution)/shard_map/pallas_call | solution.py:335
  139.4 0.6 collective-permute-start.15
  140.1 1.5 collective-permute-start.17
  141.5 0.6 collective-permute-start.13
  142.1 2.1 %collective-permute-start.14 = (bf16[4,80,384]{2,1,0:T(8,128)(2,1)S(1)}, bf16[4,80,384]{2,1,0:T(8,128)(2,1)S(1)}, u32[]{:S(2)}, u32[]{:S(2)}) collective-permute-start(bf16[4,80,384]{2,1,0:T(8,128)(2,1)S(1)} %get-tuple-element.41), channel_id=1, source_target_pairs={{0,6},{2,0},{4,2},{6,4},{1,7},{3,1},{5,3},{7,5},{8,14},{10,8},{12,... | collective-permute-start | bytes 737288 | tf_op jit(solution)/shard_map/ppermute | solution.py:360
  144.2 1.3 collective-permute-done.15
  145.5 0.8 collective-permute-start.16
  146.2 1.6 collective-permute-start.18
  147.9 5.2 %collective-permute-done.16.refs_3_ = bf16[2,80,384]{2,1,0:T(8,128)(2,1)S(1)} collective-permute-done((bf16[2,80,384]{2,1,0:T(8,128)(2,1)S(1)}, bf16[2,80,384]{2,1,0:T(8,128)(2,1)S(1)}, u32[]{:S(2)}, u32[]{:S(2)}) %collective-permute-start.16) | collective-permute-done | bytes 122912 | tf_op jit(solution)/shard_map/ppermute | solution.py:360
  153.1 0.3 collective-permute-done.18.refs_4_
  153.4 0.8 shard_map.75
  154.2 1.5 collective-permute-start.19
  155.6 2.7 %collective-permute-start.20 = (bf16[80,384]{1,0:T(8,128)(2,1)S(1)}, bf16[80,384]{1,0:T(8,128)(2,1)S(1)}, u32[]{:S(2)}, u32[]{:S(2)}) collective-permute-start(bf16[80,384]{1,0:T(8,128)(2,1)S(1)} %get-tuple-element.46), channel_id=1, source_target_pairs={{0,16},{8,24},{16,0},{24,8},{1,17},{9,25},{17,1},{25,9},{2,18},{10... | collective-permute-start | bytes 184328 | tf_op jit(solution)/shard_map/ppermute | solution.py:360
  158.3 1.5 collective-permute-start.21
  159.8 0.7 shard_map.77
  160.5 0.8 collective-permute-done.20.refs_2_
  161.4 1.2 collective-permute-done.21.refs_3_
  162.6 1.2 shard_map.76
  163.8 0.6 reduce
  (48 shorter events, 0.2 us)
Async XLA Ops:
  2.4 35.8 %all-to-all-start = ((bf16[32,16,512]{2,1,0:T(8,128)(2,1)}), bf16[32,16,512]{2,1,0:T(8,128)(2,1)S(1)}, u32[]{:S(2)}, u32[]{:S(2)}) async-start(bf16[32,16,512]{2,1,0:T(8,128)(2,1)} %bitcast.8), calls=%async_computation | async-start | bytes 1048576 | tf_op jit(solution)/shard_map/all_to_all | solution.py:346
  13.9 6.6 %collective-permute-start.1 = (bf16[64,384]{1,0:T(8,128)(2,1)}, bf16[64,384]{1,0:T(8,128)(2,1)S(1)}, u32[]{:S(2)}, u32[]{:S(2)}) collective-permute-start(bf16[64,384]{1,0:T(8,128)(2,1)} %refs_4_.1), channel_id=1, source_target_pairs={{0,16},{8,24},{16,0},{24,8},{1,17},{9,25},{17,1},{25,9},{2,18},{10... | collective-permute-start | bytes 147464 | tf_op jit(solution)/shard_map/ppermute | solution.py:360
  17.3 5.5 %collective-permute-start = (bf16[64,384]{1,0:T(8,128)(2,1)}, bf16[64,384]{1,0:T(8,128)(2,1)S(1)}, u32[]{:S(2)}, u32[]{:S(2)}) collective-permute-start(bf16[64,384]{1,0:T(8,128)(2,1)} %refs_4_.1), channel_id=1, source_target_pairs={{0,8},{8,16},{16,24},{24,0},{1,9},{9,17},{17,25},{25,1},{2,10},{10... | collective-permute-start | bytes 147464 | tf_op jit(solution)/shard_map/ppermute | solution.py:360
  17.8 5.1 %collective-permute-start.2 = (bf16[64,384]{1,0:T(8,128)(2,1)}, bf16[64,384]{1,0:T(8,128)(2,1)S(1)}, u32[]{:S(2)}, u32[]{:S(2)}) collective-permute-start(bf16[64,384]{1,0:T(8,128)(2,1)} %refs_4_.1), channel_id=1, source_target_pairs={{0,24},{8,0},{16,8},{24,16},{1,25},{9,1},{17,9},{25,17},{2,26},{10... | collective-permute-start | bytes 147464 | tf_op jit(solution)/shard_map/ppermute | solution.py:360
  23.8 15.9 %copy-start.5 = (bf16[4,64,384]{2,1,0:T(8,128)(2,1)}, bf16[4,64,384]{2,1,0:T(8,128)(2,1)S(1)}, u32[]{:S(2)}) copy-start(bf16[4,64,384]{2,1,0:T(8,128)(2,1)S(1)} %pad_maximum_fusion.refs_0_) | copy-start | bytes 589828
  23.8 5.7 %collective-permute-start.4 = (bf16[4,64,384]{2,1,0:T(8,128)(2,1)S(1)}, bf16[4,64,384]{2,1,0:T(8,128)(2,1)S(1)}, u32[]{:S(2)}, u32[]{:S(2)}) collective-permute-start(bf16[4,64,384]{2,1,0:T(8,128)(2,1)S(1)} %pad_maximum_fusion.refs_0_), channel_id=1, source_target_pairs={{0,6},{2,0},{4,2},{6,4},{1,7},{3,1},{5,3},{7,5},{8,14},{10,8},{12,... | collective-permute-start | bytes 589832 | tf_op jit(solution)/shard_map/ppermute | solution.py:360
  24.4 6.4 %collective-permute-start.3 = (bf16[4,64,384]{2,1,0:T(8,128)(2,1)S(1)}, bf16[4,64,384]{2,1,0:T(8,128)(2,1)S(1)}, u32[]{:S(2)}, u32[]{:S(2)}) collective-permute-start(bf16[4,64,384]{2,1,0:T(8,128)(2,1)S(1)} %pad_maximum_fusion.refs_0_), channel_id=1, source_target_pairs={{0,2},{2,4},{4,6},{6,0},{1,3},{3,5},{5,7},{7,1},{8,10},{10,12},{12... | collective-permute-start | bytes 589832 | tf_op jit(solution)/shard_map/ppermute | solution.py:360
  25.9 11.0 %collective-permute-start.7 = (bf16[4,64,384]{2,1,0:T(8,128)(2,1)S(1)}, bf16[4,64,384]{2,1,0:T(8,128)(2,1)S(1)}, u32[]{:S(2)}, u32[]{:S(2)}) collective-permute-start(bf16[4,64,384]{2,1,0:T(8,128)(2,1)S(1)} %pad_maximum_fusion.refs_0_), channel_id=1, source_target_pairs={{0,1},{1,0},{2,3},{3,2},{4,5},{5,4},{6,7},{7,6},{8,9},{9,8},{10,11... | collective-permute-start | bytes 589832 | tf_op jit(solution)/shard_map/ppermute | solution.py:355
  29.6 8.6 %copy-start.6 = (bf16[4,64,384]{2,1,0:T(8,128)(2,1)}, bf16[4,64,384]{2,1,0:T(8,128)(2,1)S(1)}, u32[]{:S(2)}) copy-start(bf16[4,64,384]{2,1,0:T(8,128)(2,1)S(1)} %collective-permute-done.4.refs_2_) | copy-start | bytes 589828
  29.6 4.7 %collective-permute-start.6 = (bf16[2,64,384]{2,1,0:T(8,128)(2,1)S(1)}, bf16[2,64,384]{2,1,0:T(8,128)(2,1)S(1)}, u32[]{:S(2)}, u32[]{:S(2)}) collective-permute-start(bf16[2,64,384]{2,1,0:T(8,128)(2,1)S(1)} %slice.13), channel_id=1, source_target_pairs={{0,6},{2,0},{4,2},{6,4},{1,7},{3,1},{5,3},{7,5},{8,14},{10,8},{12,... | collective-permute-start | bytes 294920 | tf_op jit(solution)/shard_map/ppermute | solution.py:360
  30.8 7.4 %copy-start.7 = (bf16[4,64,384]{2,1,0:T(8,128)(2,1)}, bf16[4,64,384]{2,1,0:T(8,128)(2,1)S(1)}, u32[]{:S(2)}) copy-start(bf16[4,64,384]{2,1,0:T(8,128)(2,1)S(1)} %collective-permute-done.3.refs_1_) | copy-start | bytes 589828
  30.8 38.3 %copy-start.3 = (f32[2048]{0:T(1024)S(1)}, f32[2048]{0:T(1024)}, u32[]{:S(2)}) copy-start(f32[2048]{0:T(1024)} %param.7) | copy-start | bytes 24580
  30.9 6.0 %collective-permute-start.5 = (bf16[2,64,384]{2,1,0:T(8,128)(2,1)S(1)}, bf16[2,64,384]{2,1,0:T(8,128)(2,1)S(1)}, u32[]{:S(2)}, u32[]{:S(2)}) collective-permute-start(bf16[2,64,384]{2,1,0:T(8,128)(2,1)S(1)} %slice.12), channel_id=1, source_target_pairs={{0,2},{2,4},{4,6},{6,0},{1,3},{3,5},{5,7},{7,1},{8,10},{10,12},{12... | collective-permute-start | bytes 294920 | tf_op jit(solution)/shard_map/ppermute | solution.py:360
  31.8 5.2 %collective-permute-start.9 = (bf16[4,64,384]{2,1,0:T(8,128)(2,1)S(1)}, bf16[4,64,384]{2,1,0:T(8,128)(2,1)S(1)}, u32[]{:S(2)}, u32[]{:S(2)}) collective-permute-start(bf16[4,64,384]{2,1,0:T(8,128)(2,1)S(1)} %collective-permute-done.4.refs_2_), channel_id=1, source_target_pairs={{0,1},{1,0},{2,3},{3,2},{4,5},{5,4},{6,7},{7,6},{8,9},{9,8},{10,11... | collective-permute-start | bytes 589832 | tf_op jit(solution)/shard_map/ppermute | solution.py:355
  31.8 6.4 %collective-permute-start.8 = (bf16[4,64,384]{2,1,0:T(8,128)(2,1)S(1)}, bf16[4,64,384]{2,1,0:T(8,128)(2,1)S(1)}, u32[]{:S(2)}, u32[]{:S(2)}) collective-permute-start(bf16[4,64,384]{2,1,0:T(8,128)(2,1)S(1)} %collective-permute-done.3.refs_1_), channel_id=1, source_target_pairs={{0,1},{1,0},{2,3},{3,2},{4,5},{5,4},{6,7},{7,6},{8,9},{9,8},{10,11... | collective-permute-start | bytes 589832 | tf_op jit(solution)/shard_map/ppermute | solution.py:355
  34.3 5.4 %copy-start.11 = (bf16[2,64,384]{2,1,0:T(8,128)(2,1)}, bf16[2,64,384]{2,1,0:T(8,128)(2,1)S(1)}, u32[]{:S(2)}) copy-start(bf16[2,64,384]{2,1,0:T(8,128)(2,1)S(1)} %collective-permute-done.6.refs_4_) | copy-start | bytes 294916
  34.3 2.7 %collective-permute-start.11 = (bf16[2,64,384]{2,1,0:T(8,128)(2,1)S(1)}, bf16[2,64,384]{2,1,0:T(8,128)(2,1)S(1)}, u32[]{:S(2)}, u32[]{:S(2)}) collective-permute-start(bf16[2,64,384]{2,1,0:T(8,128)(2,1)S(1)} %collective-permute-done.6.refs_4_), channel_id=1, source_target_pairs={{0,1},{1,0},{2,3},{3,2},{4,5},{5,4},{6,7},{7,6},{8,9},{9,8},{10,11... | collective-permute-start | bytes 294920 | tf_op jit(solution)/shard_map/ppermute | solution.py:355
  36.9 1.3 copy-start.12
  36.9 1.3 collective-permute-start.10
  36.9 1.3 copy-start.8
  37.0 1.3 copy-start.13
  37.0 1.3 copy-start.9
  38.2 0.6 copy-start.14
  38.2 0.7 copy-start.10
  38.9 0.8 copy-start.4
  44.2 0.7 copy-start.1
  44.9 15.9 %all-to-all-start.1 = ((f32[32,16,128]{2,1,0:T(8,128)}), f32[32,16,128]{2,1,0:T(8,128)S(1)}, u32[]{:S(2)}, u32[]{:S(2)}) async-start(f32[32,16,128]{2,1,0:T(8,128)} %copy-done.1), calls=%async_computation.1 | async-start | bytes 524288 | tf_op jit(solution)/shard_map/all_to_all | solution.py:346
  62.5 14.7 %all-to-all-start.2 = ((f32[8,8,128]{2,1,0:T(8,128)}), f32[8,8,128]{2,1,0:T(8,128)S(1)}, u32[]{:S(2)}, u32[]{:S(2)}) async-start(f32[8,8,128]{2,1,0:T(8,128)} %get-tuple-element.29), calls=%async_computation.2 | async-start | bytes 65536 | tf_op jit(solution)/shard_map/all_to_all | solution.py:346
  133.3 26.5 %copy-start = (bf16[16,2048]{1,0:T(8,128)(2,1)S(1)}, bf16[16,2048]{1,0:T(8,128)(2,1)}, u32[]{:S(2)}) copy-start(bf16[16,2048]{1,0:T(8,128)(2,1)} %y_ref.1) | copy-start | bytes 196612
  133.3 29.2 %copy-start.2 = (bf16[64,384]{1,0:T(8,128)(2,1)S(1)}, bf16[64,384]{1,0:T(8,128)(2,1)}, u32[]{:S(2)}) copy-start(bf16[64,384]{1,0:T(8,128)(2,1)} %refs_4_.1) | copy-start | bytes 147460
  133.3 4.0 %collective-permute-start.12 = (bf16[4,272,384]{2,1,0:T(8,128)(2,1)}, bf16[4,272,384]{2,1,0:T(8,128)(2,1)S(1)}, u32[]{:S(2)}, u32[]{:S(2)}) collective-permute-start(bf16[4,272,384]{2,1,0:T(8,128)(2,1)} %get-tuple-element.38), channel_id=1, source_target_pairs={{0,1},{1,0},{2,3},{3,2},{4,5},{5,4},{6,7},{7,6},{8,9},{9,8},{10,11... | collective-permute-start | bytes 2506760 | tf_op jit(solution)/shard_map/ppermute | solution.py:355
  133.4 26.3 %all-to-all-start.7 = ((bf16[32,16,512]{2,1,0:T(8,128)(2,1)}), bf16[32,16,512]{2,1,0:T(8,128)(2,1)S(1)}, u32[]{:S(2)}, u32[]{:S(2)}) async-start(bf16[32,16,512]{2,1,0:T(8,128)(2,1)} %bitcast.28), calls=%async_computation.7 | async-start | bytes 1048576 | tf_op jit(solution)/shard_map/all_to_all | solution.py:346
  139.4 6.0 %collective-permute-start.15 = (bf16[2,80,384]{2,1,0:T(8,128)(2,1)S(1)}, bf16[2,80,384]{2,1,0:T(8,128)(2,1)S(1)}, u32[]{:S(2)}, u32[]{:S(2)}) collective-permute-start(bf16[2,80,384]{2,1,0:T(8,128)(2,1)S(1)} %get-tuple-element.42), channel_id=1, source_target_pairs={{0,2},{2,4},{4,6},{6,0},{1,3},{3,5},{5,7},{7,1},{8,10},{10,12},{12... | collective-permute-start | bytes 368648 | tf_op jit(solution)/shard_map/ppermute | solution.py:360
  140.1 6.2 %collective-permute-start.17 = (bf16[2,80,384]{2,1,0:T(8,128)(2,1)S(1)}, bf16[2,80,384]{2,1,0:T(8,128)(2,1)S(1)}, u32[]{:S(2)}, u32[]{:S(2)}) collective-permute-start(bf16[2,80,384]{2,1,0:T(8,128)(2,1)S(1)} %get-tuple-element.43), channel_id=1, source_target_pairs={{0,6},{2,0},{4,2},{6,4},{1,7},{3,1},{5,3},{7,5},{8,14},{10,8},{12,... | collective-permute-start | bytes 368648 | tf_op jit(solution)/shard_map/ppermute | solution.py:360
  141.5 11.9 %collective-permute-start.13 = (bf16[4,80,384]{2,1,0:T(8,128)(2,1)S(1)}, bf16[4,80,384]{2,1,0:T(8,128)(2,1)S(1)}, u32[]{:S(2)}, u32[]{:S(2)}) collective-permute-start(bf16[4,80,384]{2,1,0:T(8,128)(2,1)S(1)} %get-tuple-element.40), channel_id=1, source_target_pairs={{0,2},{2,4},{4,6},{6,0},{1,3},{3,5},{5,7},{7,1},{8,10},{10,12},{12... | collective-permute-start | bytes 737288 | tf_op jit(solution)/shard_map/ppermute | solution.py:360
  142.1 11.3 %collective-permute-start.14 = (bf16[4,80,384]{2,1,0:T(8,128)(2,1)S(1)}, bf16[4,80,384]{2,1,0:T(8,128)(2,1)S(1)}, u32[]{:S(2)}, u32[]{:S(2)}) collective-permute-start(bf16[4,80,384]{2,1,0:T(8,128)(2,1)S(1)} %get-tuple-element.41), channel_id=1, source_target_pairs={{0,6},{2,0},{4,2},{6,4},{1,7},{3,1},{5,3},{7,5},{8,14},{10,8},{12,... | collective-permute-start | bytes 737288 | tf_op jit(solution)/shard_map/ppermute | solution.py:360
  145.5 7.7 %collective-permute-start.16 = (bf16[2,80,384]{2,1,0:T(8,128)(2,1)S(1)}, bf16[2,80,384]{2,1,0:T(8,128)(2,1)S(1)}, u32[]{:S(2)}, u32[]{:S(2)}) collective-permute-start(bf16[2,80,384]{2,1,0:T(8,128)(2,1)S(1)} %collective-permute-done.15), channel_id=1, source_target_pairs={{0,2},{2,4},{4,6},{6,0},{1,3},{3,5},{5,7},{7,1},{8,10},{10,12},{12... | collective-permute-start | bytes 368648 | tf_op jit(solution)/shard_map/ppermute | solution.py:360
  146.2 7.1 %collective-permute-start.18 = (bf16[2,80,384]{2,1,0:T(8,128)(2,1)S(1)}, bf16[2,80,384]{2,1,0:T(8,128)(2,1)S(1)}, u32[]{:S(2)}, u32[]{:S(2)}) collective-permute-start(bf16[2,80,384]{2,1,0:T(8,128)(2,1)S(1)} %collective-permute-done.17), channel_id=1, source_target_pairs={{0,6},{2,0},{4,2},{6,4},{1,7},{3,1},{5,3},{7,5},{8,14},{10,8},{12,... | collective-permute-start | bytes 368648 | tf_op jit(solution)/shard_map/ppermute | solution.py:360
  154.2 6.4 %collective-permute-start.19 = (bf16[80,384]{1,0:T(8,128)(2,1)S(1)}, bf16[80,384]{1,0:T(8,128)(2,1)S(1)}, u32[]{:S(2)}, u32[]{:S(2)}) collective-permute-start(bf16[80,384]{1,0:T(8,128)(2,1)S(1)} %get-tuple-element.45), channel_id=1, source_target_pairs={{0,8},{8,16},{16,24},{24,0},{1,9},{9,17},{17,25},{25,1},{2,10},{10... | collective-permute-start | bytes 184328 | tf_op jit(solution)/shard_map/ppermute | solution.py:360
  155.6 5.7 %collective-permute-start.20 = (bf16[80,384]{1,0:T(8,128)(2,1)S(1)}, bf16[80,384]{1,0:T(8,128)(2,1)S(1)}, u32[]{:S(2)}, u32[]{:S(2)}) collective-permute-start(bf16[80,384]{1,0:T(8,128)(2,1)S(1)} %get-tuple-element.46), channel_id=1, source_target_pairs={{0,16},{8,24},{16,0},{24,8},{1,17},{9,25},{17,1},{25,9},{2,18},{10... | collective-permute-start | bytes 184328 | tf_op jit(solution)/shard_map/ppermute | solution.py:360
  158.3 4.2 %collective-permute-start.21 = (bf16[80,384]{1,0:T(8,128)(2,1)S(1)}, bf16[80,384]{1,0:T(8,128)(2,1)S(1)}, u32[]{:S(2)}, u32[]{:S(2)}) collective-permute-start(bf16[80,384]{1,0:T(8,128)(2,1)S(1)} %get-tuple-element.47), channel_id=1, source_target_pairs={{0,24},{8,0},{16,8},{24,16},{1,25},{9,1},{17,9},{25,17},{2,26},{10... | collective-permute-start | bytes 184328 | tf_op jit(solution)/shard_map/ppermute | solution.py:360

commit v4 on v3

--- a/solution.py
+++ b/solution.py
@@ -309,7 +309,7 @@
     depth, deep = x_ref.shape[0], ins[0].shape[0]
     total = balanced([one[:depth].astype(F32) for one in ins])
     sums = [balanced([pieces_sum(one[depth:deep], n) for one in ins]) for n in range(2)]
-    reward_ref[...] = -sums[1] / sums[0]
+    reward_ref[...] = (-sums[1] / sums[0])[0]
     pull_ref[...] = sums[0] * x_ref[...].astype(F32) - total
 
 
@@ -399,6 +399,7 @@
          ((emb, rows), BF16)],
         [((emb, rows), BF16), ((emb, cols), BF16), column, ((f_lines, LANES), F32)],
         *ins, smem=1, far=range(1, 12), far_out=(4,), sems=2 * nx * ny + 2, limit=24 << 20)
+    out, lb = lax.optimization_barrier((out, lb))
     la = None
     for step in range(ITERS):
         if step:
@@ -430,12 +431,12 @@
     ends = call(across_kernel, [(line[0][1:], BF16)] * ny, [((ny, depth, width), F32), ((ny, 8, width), F32)],
                 here, *lines, smem=1, limit=16 << 20)
     ends = [ends[0]] + [shifted(ends[s], "y", s) for s in range(1, ny)]
-    roll_pull, reward = call(roll_kernel, [((depth, width), F32), ((1, width), F32)], [],
+    roll_pull, reward = call(roll_kernel, [((depth, width), F32), ((width,), F32)], [],
                              here, *ends, roll_embed, smem=1, limit=8 << 20)
     (expert_pull,) = call(expert_kernel, [((thin, wide), F32)], [],
                           xsum_got.reshape(nz, ny, thin, cols), expert_embed, expert_weight.reshape(1, wide),
                           limit=8 << 20)
-    return (reward.reshape(width), roll_pull, expert_pull)
+    return (reward, roll_pull, expert_pull)
 
 
 def solution(mesh):

time: 167 us -> 165 us (0.988)
  blocking collectives: 45.6 us -> 75.8 us
  waiting for transfers between devices: 35.8 us -> 19.5 us
  starting transfers between devices: 54.3 us -> 39.3 us
    all_to_all x4 -> x6, blocking collectives: 45.6 us -> 75.8 us  [exchanged(): return lax.all_to_all(x, axes, split_axis=0, concat_axis=0, tiled=True)]
    all_to_all x4 -> x2, waiting for transfers between devices: 15.5 us -> 0.01 us  [exchanged(): return lax.all_to_all(x, axes, split_axis=0, concat_axis=0, tiled=True)]
    all_to_all x4 -> x2, starting transfers between devices: 30.4 us -> 15.4 us  [exchanged(): return lax.all_to_all(x, axes, split_axis=0, concat_axis=0, tiled=True)]
  transfers between devices with their start and end apart: 26 -> 24, of which waited for: 14 -> 12; matrix products, arithmetic and copies ran while one was open for 1% -> 1% of each run, Pallas kernels for 2% -> 2%
where the time goes in v4:
time: 165 us; the launch traced here: 162 us
  blocking collectives  75.8 us (46%)
  starting transfers between devices  39.3 us (24%)
  Pallas kernels  20.9 us (13%)
  waiting for transfers between devices  19.5 us (12%)
  local copies, waits for them, and re-layouts  3.32 us (2%)
  other arithmetic  2.35 us (1%)
    all_to_all x6, blocking collectives, exchanged(): return lax.all_to_all(x, axes, split_axis=0, concat_axis=0, tiled=True)  75.8 us
    ppermute x16, starting transfers between devices, shifted(): return lax.ppermute(x, axis, [(i, (i + by) % n) for i in range(n)])  23.4 us
    pallas_call x11, Pallas kernels, call(): pl.pallas_call(body, out_shape=[pltpu.HBM(s, t) if n in far_out else jax....  20.9 us
    ppermute x16, waiting for transfers between devices, shifted(): return lax.ppermute(x, axis, [(i, (i + by) % n) for i in range(n)])  18.3 us
    all_to_all x2, starting transfers between devices, exchanged(): return lax.all_to_all(x, axes, split_axis=0, concat_axis=0, tiled=True)  15.4 us
  transfers between devices with their start and end apart: 24, of which 12 were waited for; matrix products, arithmetic and copies ran while one was open for 1% of the time, Pallas kernels for 2%

profile of v4, /device:TPU:2, one launch (start us, length us, event | category | flops | bytes accessed | tf_op | source)
XLA Modules:
  0.0 162.2 jit_solution(13822253620383906250)
XLA Ops:
  0.6 0.9 reshape.34
  1.5 0.9 broadcast_in_dim.2
  2.4 11.5 %all-to-all-start = ((bf16[32,16,512]{2,1,0:T(8,128)(2,1)}), bf16[32,16,512]{2,1,0:T(8,128)(2,1)S(1)}, u32[]{:S(2)}, u32[]{:S(2)}) async-start(bf16[32,16,512]{2,1,0:T(8,128)(2,1)} %bitcast.8), calls=%async_computation | async-start | bytes 1048576 | tf_op jit(solution)/shard_map/all_to_all | solution.py:346
  13.9 3.4 %collective-permute-start.1 = (bf16[64,384]{1,0:T(8,128)(2,1)}, bf16[64,384]{1,0:T(8,128)(2,1)S(1)}, u32[]{:S(2)}, u32[]{:S(2)}) collective-permute-start(bf16[64,384]{1,0:T(8,128)(2,1)} %refs_4_.1), channel_id=1, source_target_pairs={{0,16},{8,24},{16,0},{24,8},{1,17},{9,25},{17,1},{25,9},{2,18},{10... | collective-permute-start | bytes 147464 | tf_op jit(solution)/shard_map/ppermute | solution.py:360
  17.3 0.6 collective-permute-start
  17.8 2.7 %collective-permute-start.2 = (bf16[64,384]{1,0:T(8,128)(2,1)}, bf16[64,384]{1,0:T(8,128)(2,1)S(1)}, u32[]{:S(2)}, u32[]{:S(2)}) collective-permute-start(bf16[64,384]{1,0:T(8,128)(2,1)} %refs_4_.1), channel_id=1, source_target_pairs={{0,24},{8,0},{16,8},{24,16},{1,25},{9,1},{17,9},{25,17},{2,26},{10... | collective-permute-start | bytes 147464 | tf_op jit(solution)/shard_map/ppermute | solution.py:360
  20.5 0.0 collective-permute-done.1
  20.5 2.3 %collective-permute-done = bf16[64,384]{1,0:T(8,128)(2,1)S(1)} collective-permute-done((bf16[64,384]{1,0:T(8,128)(2,1)}, bf16[64,384]{1,0:T(8,128)(2,1)S(1)}, u32[]{:S(2)}, u32[]{:S(2)}) %collective-permute-start) | collective-permute-done | bytes 49184 | tf_op jit(solution)/shard_map/ppermute | solution.py:360
  22.8 0.1 collective-permute-done.2
  23.0 0.8 pad_maximum_fusion.refs_0_
  23.8 0.6 collective-permute-start.4
  24.4 1.5 collective-permute-start.3
  25.9 0.7 multiply_bitcast_fusion.1
  26.6 0.0 collective-permute-start.7
  26.6 3.0 %collective-permute-done.4.refs_2_ = bf16[4,64,384]{2,1,0:T(8,128)(2,1)S(1)} collective-permute-done((bf16[4,64,384]{2,1,0:T(8,128)(2,1)S(1)}, bf16[4,64,384]{2,1,0:T(8,128)(2,1)S(1)}, u32[]{:S(2)}, u32[]{:S(2)}) %collective-permute-start.4) | collective-permute-done | bytes 196640 | tf_op jit(solution)/shard_map/ppermute | solution.py:360
  29.6 0.9 collective-permute-start.6
  30.5 0.4 collective-permute-done.3.refs_1_
  30.8 0.9 collective-permute-start.5
  31.8 0.5 collective-permute-start.8
  32.3 0.8 multiply_bitcast_fusion
  33.1 1.2 collective-permute-done.6.refs_4_
  34.3 0.0 collective-permute-start.11
  34.3 2.6 %collective-permute-done.5.refs_3_ = bf16[2,64,384]{2,1,0:T(8,128)(2,1)S(1)} collective-permute-done((bf16[2,64,384]{2,1,0:T(8,128)(2,1)S(1)}, bf16[2,64,384]{2,1,0:T(8,128)(2,1)S(1)}, u32[]{:S(2)}, u32[]{:S(2)}) %collective-permute-start.5) | collective-permute-done | bytes 98336 | tf_op jit(solution)/shard_map/ppermute | solution.py:360
  36.8 0.1 pad_add_fusion.here_ref
  37.0 1.2 collective-permute-done.10.refs_8_
  38.2 0.6 copy-done.13
  38.8 0.1 copy-done.9
  38.9 0.8 copy-done.3
  39.7 4.5 %shard_map.67 = (f32[512,1536]{1,0:T(8,128)S(1)}, f32[16,128]{1,0:T(8,128)S(1)}, f32[8,128]{1,0:T(8,128)S(1)}, f32[32,16,128]{2,1,0:T(8,128)S(1)}, bf16[512,1536]{1,0:T(8,128)(2,1)}) custom-call(s32[3]{0:T(128)S(1)} %pad_add_fusion.here_ref, bf16[4,64,384]{2,1,0:T(8,128)(2,1)} %copy-done.4, bf16[4,64,384]{2,1,0:T(8,128)(2,1)} %copy-done.6, ...), custom_call_target="tpu_custom_call" | custom-call | tf_op jit(solution)/shard_map/pallas_call | solution.py:335
  44.2 15.7 %all_to_all.40.parts_ref = f32[32,16,128]{2,1,0:T(8,128)S(1)} all-to-all(f32[32,16,128]{2,1,0:T(8,128)S(1)} %get-tuple-element.30), channel_id=1, replica_groups=mesh['z'=8,'y'=4,'x'=4,'core'=2] {'y','x','core'}, dimensions={0} | all-to-all | bytes 524288 | tf_op jit(solution)/shard_map/all_to_all | solution.py:346
  60.0 1.1 shard_map.68
  61.1 14.5 %all_to_all.41.parts_ref = f32[8,8,128]{2,1,0:T(8,128)S(1)} all-to-all(f32[8,8,128]{2,1,0:T(8,128)S(1)} %get-tuple-element.32), channel_id=1, replica_groups=mesh['z'=8,'y'=4,'x'=4,'core'=2] {'z'}, dimensions={0} | all-to-all | bytes 65536 | tf_op jit(solution)/shard_map/all_to_all | solution.py:346
  75.6 1.1 shard_map.69
  76.7 12.4 %all_to_all.42.parts_ref = f32[32,16,128]{2,1,0:T(8,128)S(1)} all-to-all(f32[32,16,128]{2,1,0:T(8,128)S(1)} %shard_map.69), channel_id=1, replica_groups=mesh['z'=8,'y'=4,'x'=4,'core'=2] {'y','x','core'}, dimensions={0} | all-to-all | bytes 524288 | tf_op jit(solution)/shard_map/all_to_all | solution.py:346
  89.1 1.1 shard_map.70
  90.2 10.4 %all_to_all.43.parts_ref = f32[8,8,128]{2,1,0:T(8,128)S(1)} all-to-all(f32[8,8,128]{2,1,0:T(8,128)S(1)} %get-tuple-element.34), channel_id=1, replica_groups=mesh['z'=8,'y'=4,'x'=4,'core'=2] {'z'}, dimensions={0} | all-to-all | bytes 65536 | tf_op jit(solution)/shard_map/all_to_all | solution.py:346
  100.6 1.1 shard_map.71
  101.8 12.4 %all_to_all.44.parts_ref = f32[32,16,128]{2,1,0:T(8,128)S(1)} all-to-all(f32[32,16,128]{2,1,0:T(8,128)S(1)} %shard_map.71), channel_id=1, replica_groups=mesh['z'=8,'y'=4,'x'=4,'core'=2] {'y','x','core'}, dimensions={0} | all-to-all | bytes 524288 | tf_op jit(solution)/shard_map/all_to_all | solution.py:346
  114.2 1.0 shard_map.72
  115.2 10.4 %all_to_all.45.parts_ref = f32[8,8,128]{2,1,0:T(8,128)S(1)} all-to-all(f32[8,8,128]{2,1,0:T(8,128)S(1)} %get-tuple-element.35), channel_id=1, replica_groups=mesh['z'=8,'y'=4,'x'=4,'core'=2] {'z'}, dimensions={0} | all-to-all | bytes 65536 | tf_op jit(solution)/shard_map/all_to_all | solution.py:346
  125.6 6.1 %shard_map.73 = (bf16[4,256,384]{2,1,0:T(8,128)(2,1)}, bf16[4,272,384]{2,1,0:T(8,128)(2,1)}, f32[4,8,384]{2,1,0:T(8,128)S(1)}, bf16[512,512]{1,0:T(8,128)(2,1)}) custom-call(s32[3]{0:T(128)S(1)} %pad_add_fusion.here_ref, f32[8,8,128]{2,1,0:T(8,128)S(1)} %all_to_all.45.parts_ref, f32[8,128]{1,0:T(8,128)S(1)} %pad.13.lb_ref, ...), custom_call_target="tpu_custom_call" | custom-call | tf_op jit(solution)/shard_map/pallas_call | solution.py:335
  131.7 0.0 copy-start
  131.7 0.0 copy-start.2
  131.7 0.0 copy-start.1
  131.7 0.1 collective-permute-start.12
  131.8 3.9 %all-to-all-start.7 = ((bf16[32,16,512]{2,1,0:T(8,128)(2,1)}), bf16[32,16,512]{2,1,0:T(8,128)(2,1)S(1)}, u32[]{:S(2)}, u32[]{:S(2)}) async-start(bf16[32,16,512]{2,1,0:T(8,128)(2,1)} %bitcast.28), calls=%async_computation.7 | async-start | bytes 1048576 | tf_op jit(solution)/shard_map/all_to_all | solution.py:346
  135.8 2.1 %shard_map.74 = (bf16[4,80,384]{2,1,0:T(8,128)(2,1)S(1)}, bf16[4,80,384]{2,1,0:T(8,128)(2,1)S(1)}, bf16[4,80,384]{2,1,0:T(8,128)(2,1)S(1)}, bf16[2,80,384]{2,1,0:T(8,128)(2,1)S(1)}, bf16[2,80,384]{2,1,0:T(8,128)(2,1)S(1)}) custom-call(s32[3]{0:T(128)S(1)} %pad_add_fusion.here_ref, bf16[4,256,384]{2,1,0:T(8,128)(2,1)} %get-tuple-element.40.keep_hbm, ...), custom_call_target="tpu_custom_call" | custom-call | tf_op jit(solution)/shard_map/pallas_call | solution.py:335
  137.8 0.6 collective-permute-start.15
  138.5 1.5 collective-permute-start.17
  139.9 0.6 collective-permute-start.13
  140.5 2.1 %collective-permute-start.14 = (bf16[4,80,384]{2,1,0:T(8,128)(2,1)S(1)}, bf16[4,80,384]{2,1,0:T(8,128)(2,1)S(1)}, u32[]{:S(2)}, u32[]{:S(2)}) collective-permute-start(bf16[4,80,384]{2,1,0:T(8,128)(2,1)S(1)} %get-tuple-element.45), channel_id=1, source_target_pairs={{0,6},{2,0},{4,2},{6,4},{1,7},{3,1},{5,3},{7,5},{8,14},{10,8},{12,... | collective-permute-start | bytes 737288 | tf_op jit(solution)/shard_map/ppermute | solution.py:360
  142.6 1.3 collective-permute-done.15
  143.9 0.8 collective-permute-start.16
  144.7 1.6 %collective-permute-start.18 = (bf16[2,80,384]{2,1,0:T(8,128)(2,1)S(1)}, bf16[2,80,384]{2,1,0:T(8,128)(2,1)S(1)}, u32[]{:S(2)}, u32[]{:S(2)}) collective-permute-start(bf16[2,80,384]{2,1,0:T(8,128)(2,1)S(1)} %collective-permute-done.17), channel_id=1, source_target_pairs={{0,6},{2,0},{4,2},{6,4},{1,7},{3,1},{5,3},{7,5},{8,14},{10,8},{12,... | collective-permute-start | bytes 368648 | tf_op jit(solution)/shard_map/ppermute | solution.py:360
  146.3 5.2 %collective-permute-done.16.refs_3_ = bf16[2,80,384]{2,1,0:T(8,128)(2,1)S(1)} collective-permute-done((bf16[2,80,384]{2,1,0:T(8,128)(2,1)S(1)}, bf16[2,80,384]{2,1,0:T(8,128)(2,1)S(1)}, u32[]{:S(2)}, u32[]{:S(2)}) %collective-permute-start.16) | collective-permute-done | bytes 122912 | tf_op jit(solution)/shard_map/ppermute | solution.py:360
  151.5 0.3 collective-permute-done.18.refs_4_
  151.8 0.8 shard_map.75
  152.6 1.5 collective-permute-start.19
  154.1 2.7 %collective-permute-start.20 = (bf16[80,384]{1,0:T(8,128)(2,1)S(1)}, bf16[80,384]{1,0:T(8,128)(2,1)S(1)}, u32[]{:S(2)}, u32[]{:S(2)}) collective-permute-start(bf16[80,384]{1,0:T(8,128)(2,1)S(1)} %get-tuple-element.50), channel_id=1, source_target_pairs={{0,16},{8,24},{16,0},{24,8},{1,17},{9,25},{17,1},{25,9},{2,18},{10... | collective-permute-start | bytes 184328 | tf_op jit(solution)/shard_map/ppermute | solution.py:360
  156.7 1.5 collective-permute-start.21
  158.2 0.7 shard_map.77
  159.0 0.8 collective-permute-done.20.refs_2_
  159.8 1.2 collective-permute-done.21.refs_3_
  161.0 1.2 shard_map.76
  (43 shorter events, 0.1 us)
Async XLA Ops:
  2.4 35.8 %all-to-all-start = ((bf16[32,16,512]{2,1,0:T(8,128)(2,1)}), bf16[32,16,512]{2,1,0:T(8,128)(2,1)S(1)}, u32[]{:S(2)}, u32[]{:S(2)}) async-start(bf16[32,16,512]{2,1,0:T(8,128)(2,1)} %bitcast.8), calls=%async_computation | async-start | bytes 1048576 | tf_op jit(solution)/shard_map/all_to_all | solution.py:346
  13.9 6.6 %collective-permute-start.1 = (bf16[64,384]{1,0:T(8,128)(2,1)}, bf16[64,384]{1,0:T(8,128)(2,1)S(1)}, u32[]{:S(2)}, u32[]{:S(2)}) collective-permute-start(bf16[64,384]{1,0:T(8,128)(2,1)} %refs_4_.1), channel_id=1, source_target_pairs={{0,16},{8,24},{16,0},{24,8},{1,17},{9,25},{17,1},{25,9},{2,18},{10... | collective-permute-start | bytes 147464 | tf_op jit(solution)/shard_map/ppermute | solution.py:360
  17.3 5.5 %collective-permute-start = (bf16[64,384]{1,0:T(8,128)(2,1)}, bf16[64,384]{1,0:T(8,128)(2,1)S(1)}, u32[]{:S(2)}, u32[]{:S(2)}) collective-permute-start(bf16[64,384]{1,0:T(8,128)(2,1)} %refs_4_.1), channel_id=1, source_target_pairs={{0,8},{8,16},{16,24},{24,0},{1,9},{9,17},{17,25},{25,1},{2,10},{10... | collective-permute-start | bytes 147464 | tf_op jit(solution)/shard_map/ppermute | solution.py:360
  17.8 5.1 %collective-permute-start.2 = (bf16[64,384]{1,0:T(8,128)(2,1)}, bf16[64,384]{1,0:T(8,128)(2,1)S(1)}, u32[]{:S(2)}, u32[]{:S(2)}) collective-permute-start(bf16[64,384]{1,0:T(8,128)(2,1)} %refs_4_.1), channel_id=1, source_target_pairs={{0,24},{8,0},{16,8},{24,16},{1,25},{9,1},{17,9},{25,17},{2,26},{10... | collective-permute-start | bytes 147464 | tf_op jit(solution)/shard_map/ppermute | solution.py:360
  23.8 15.9 %copy-start.4 = (bf16[4,64,384]{2,1,0:T(8,128)(2,1)}, bf16[4,64,384]{2,1,0:T(8,128)(2,1)S(1)}, u32[]{:S(2)}) copy-start(bf16[4,64,384]{2,1,0:T(8,128)(2,1)S(1)} %pad_maximum_fusion.refs_0_) | copy-start | bytes 589828
  23.8 5.7 %collective-permute-start.4 = (bf16[4,64,384]{2,1,0:T(8,128)(2,1)S(1)}, bf16[4,64,384]{2,1,0:T(8,128)(2,1)S(1)}, u32[]{:S(2)}, u32[]{:S(2)}) collective-permute-start(bf16[4,64,384]{2,1,0:T(8,128)(2,1)S(1)} %pad_maximum_fusion.refs_0_), channel_id=1, source_target_pairs={{0,6},{2,0},{4,2},{6,4},{1,7},{3,1},{5,3},{7,5},{8,14},{10,8},{12,... | collective-permute-start | bytes 589832 | tf_op jit(solution)/shard_map/ppermute | solution.py:360
  24.4 6.4 %collective-permute-start.3 = (bf16[4,64,384]{2,1,0:T(8,128)(2,1)S(1)}, bf16[4,64,384]{2,1,0:T(8,128)(2,1)S(1)}, u32[]{:S(2)}, u32[]{:S(2)}) collective-permute-start(bf16[4,64,384]{2,1,0:T(8,128)(2,1)S(1)} %pad_maximum_fusion.refs_0_), channel_id=1, source_target_pairs={{0,2},{2,4},{4,6},{6,0},{1,3},{3,5},{5,7},{7,1},{8,10},{10,12},{12... | collective-permute-start | bytes 589832 | tf_op jit(solution)/shard_map/ppermute | solution.py:360
  26.6 10.3 %collective-permute-start.7 = (bf16[4,64,384]{2,1,0:T(8,128)(2,1)S(1)}, bf16[4,64,384]{2,1,0:T(8,128)(2,1)S(1)}, u32[]{:S(2)}, u32[]{:S(2)}) collective-permute-start(bf16[4,64,384]{2,1,0:T(8,128)(2,1)S(1)} %pad_maximum_fusion.refs_0_), channel_id=1, source_target_pairs={{0,1},{1,0},{2,3},{3,2},{4,5},{5,4},{6,7},{7,6},{8,9},{9,8},{10,11... | collective-permute-start | bytes 589832 | tf_op jit(solution)/shard_map/ppermute | solution.py:355
  29.5 8.6 %copy-start.5 = (bf16[4,64,384]{2,1,0:T(8,128)(2,1)}, bf16[4,64,384]{2,1,0:T(8,128)(2,1)S(1)}, u32[]{:S(2)}) copy-start(bf16[4,64,384]{2,1,0:T(8,128)(2,1)S(1)} %collective-permute-done.4.refs_2_) | copy-start | bytes 589828
  29.6 4.7 %collective-permute-start.6 = (bf16[2,64,384]{2,1,0:T(8,128)(2,1)S(1)}, bf16[2,64,384]{2,1,0:T(8,128)(2,1)S(1)}, u32[]{:S(2)}, u32[]{:S(2)}) collective-permute-start(bf16[2,64,384]{2,1,0:T(8,128)(2,1)S(1)} %slice.13), channel_id=1, source_target_pairs={{0,6},{2,0},{4,2},{6,4},{1,7},{3,1},{5,3},{7,5},{8,14},{10,8},{12,... | collective-permute-start | bytes 294920 | tf_op jit(solution)/shard_map/ppermute | solution.py:360
  30.8 7.4 %copy-start.6 = (bf16[4,64,384]{2,1,0:T(8,128)(2,1)}, bf16[4,64,384]{2,1,0:T(8,128)(2,1)S(1)}, u32[]{:S(2)}) copy-start(bf16[4,64,384]{2,1,0:T(8,128)(2,1)S(1)} %collective-permute-done.3.refs_1_) | copy-start | bytes 589828
  30.8 6.0 %collective-permute-start.5 = (bf16[2,64,384]{2,1,0:T(8,128)(2,1)S(1)}, bf16[2,64,384]{2,1,0:T(8,128)(2,1)S(1)}, u32[]{:S(2)}, u32[]{:S(2)}) collective-permute-start(bf16[2,64,384]{2,1,0:T(8,128)(2,1)S(1)} %slice.12), channel_id=1, source_target_pairs={{0,2},{2,4},{4,6},{6,0},{1,3},{3,5},{5,7},{7,1},{8,10},{10,12},{12... | collective-permute-start | bytes 294920 | tf_op jit(solution)/shard_map/ppermute | solution.py:360
  31.8 5.2 %collective-permute-start.9 = (bf16[4,64,384]{2,1,0:T(8,128)(2,1)S(1)}, bf16[4,64,384]{2,1,0:T(8,128)(2,1)S(1)}, u32[]{:S(2)}, u32[]{:S(2)}) collective-permute-start(bf16[4,64,384]{2,1,0:T(8,128)(2,1)S(1)} %collective-permute-done.4.refs_2_), channel_id=1, source_target_pairs={{0,1},{1,0},{2,3},{3,2},{4,5},{5,4},{6,7},{7,6},{8,9},{9,8},{10,11... | collective-permute-start | bytes 589832 | tf_op jit(solution)/shard_map/ppermute | solution.py:355
  31.8 6.4 %collective-permute-start.8 = (bf16[4,64,384]{2,1,0:T(8,128)(2,1)S(1)}, bf16[4,64,384]{2,1,0:T(8,128)(2,1)S(1)}, u32[]{:S(2)}, u32[]{:S(2)}) collective-permute-start(bf16[4,64,384]{2,1,0:T(8,128)(2,1)S(1)} %collective-permute-done.3.refs_1_), channel_id=1, source_target_pairs={{0,1},{1,0},{2,3},{3,2},{4,5},{5,4},{6,7},{7,6},{8,9},{9,8},{10,11... | collective-permute-start | bytes 589832 | tf_op jit(solution)/shard_map/ppermute | solution.py:355
  34.3 5.4 %copy-start.10 = (bf16[2,64,384]{2,1,0:T(8,128)(2,1)}, bf16[2,64,384]{2,1,0:T(8,128)(2,1)S(1)}, u32[]{:S(2)}) copy-start(bf16[2,64,384]{2,1,0:T(8,128)(2,1)S(1)} %collective-permute-done.6.refs_4_) | copy-start | bytes 294916
  34.3 2.7 %collective-permute-start.11 = (bf16[2,64,384]{2,1,0:T(8,128)(2,1)S(1)}, bf16[2,64,384]{2,1,0:T(8,128)(2,1)S(1)}, u32[]{:S(2)}, u32[]{:S(2)}) collective-permute-start(bf16[2,64,384]{2,1,0:T(8,128)(2,1)S(1)} %collective-permute-done.6.refs_4_), channel_id=1, source_target_pairs={{0,1},{1,0},{2,3},{3,2},{4,5},{5,4},{6,7},{7,6},{8,9},{9,8},{10,11... | collective-permute-start | bytes 294920 | tf_op jit(solution)/shard_map/ppermute | solution.py:355
  36.8 1.3 copy-start.11
  36.8 1.3 collective-permute-start.10
  36.9 1.3 copy-start.7
  36.9 1.3 copy-start.12
  37.0 1.3 copy-start.8
  38.1 0.6 copy-start.13
  38.2 0.7 copy-start.9
  38.9 0.8 copy-start.3
  131.7 26.5 %copy-start = (bf16[16,2048]{1,0:T(8,128)(2,1)S(1)}, bf16[16,2048]{1,0:T(8,128)(2,1)}, u32[]{:S(2)}) copy-start(bf16[16,2048]{1,0:T(8,128)(2,1)} %y_ref.1) | copy-start | bytes 196612
  131.7 26.5 %copy-start.2 = (f32[2048]{0:T(1024)S(1)}, f32[2048]{0:T(1024)}, u32[]{:S(2)}) copy-start(f32[2048]{0:T(1024)} %param.7) | copy-start | bytes 24580
  131.7 29.2 %copy-start.1 = (bf16[64,384]{1,0:T(8,128)(2,1)S(1)}, bf16[64,384]{1,0:T(8,128)(2,1)}, u32[]{:S(2)}) copy-start(bf16[64,384]{1,0:T(8,128)(2,1)} %refs_4_.1) | copy-start | bytes 147460
  131.7 4.0 %collective-permute-start.12 = (bf16[4,272,384]{2,1,0:T(8,128)(2,1)}, bf16[4,272,384]{2,1,0:T(8,128)(2,1)S(1)}, u32[]{:S(2)}, u32[]{:S(2)}) collective-permute-start(bf16[4,272,384]{2,1,0:T(8,128)(2,1)} %get-tuple-element.42), channel_id=1, source_target_pairs={{0,1},{1,0},{2,3},{3,2},{4,5},{5,4},{6,7},{7,6},{8,9},{9,8},{10,11... | collective-permute-start | bytes 2506760 | tf_op jit(solution)/shard_map/ppermute | solution.py:355
  131.8 26.4 %all-to-all-start.7 = ((bf16[32,16,512]{2,1,0:T(8,128)(2,1)}), bf16[32,16,512]{2,1,0:T(8,128)(2,1)S(1)}, u32[]{:S(2)}, u32[]{:S(2)}) async-start(bf16[32,16,512]{2,1,0:T(8,128)(2,1)} %bitcast.28), calls=%async_computation.7 | async-start | bytes 1048576 | tf_op jit(solution)/shard_map/all_to_all | solution.py:346
  137.8 6.0 %collective-permute-start.15 = (bf16[2,80,384]{2,1,0:T(8,128)(2,1)S(1)}, bf16[2,80,384]{2,1,0:T(8,128)(2,1)S(1)}, u32[]{:S(2)}, u32[]{:S(2)}) collective-permute-start(bf16[2,80,384]{2,1,0:T(8,128)(2,1)S(1)} %get-tuple-element.46), channel_id=1, source_target_pairs={{0,2},{2,4},{4,6},{6,0},{1,3},{3,5},{5,7},{7,1},{8,10},{10,12},{12... | collective-permute-start | bytes 368648 | tf_op jit(solution)/shard_map/ppermute | solution.py:360
  138.5 6.2 %collective-permute-start.17 = (bf16[2,80,384]{2,1,0:T(8,128)(2,1)S(1)}, bf16[2,80,384]{2,1,0:T(8,128)(2,1)S(1)}, u32[]{:S(2)}, u32[]{:S(2)}) collective-permute-start(bf16[2,80,384]{2,1,0:T(8,128)(2,1)S(1)} %get-tuple-element.47), channel_id=1, source_target_pairs={{0,6},{2,0},{4,2},{6,4},{1,7},{3,1},{5,3},{7,5},{8,14},{10,8},{12,... | collective-permute-start | bytes 368648 | tf_op jit(solution)/shard_map/ppermute | solution.py:360
  139.9 11.9 %collective-permute-start.13 = (bf16[4,80,384]{2,1,0:T(8,128)(2,1)S(1)}, bf16[4,80,384]{2,1,0:T(8,128)(2,1)S(1)}, u32[]{:S(2)}, u32[]{:S(2)}) collective-permute-start(bf16[4,80,384]{2,1,0:T(8,128)(2,1)S(1)} %get-tuple-element.44), channel_id=1, source_target_pairs={{0,2},{2,4},{4,6},{6,0},{1,3},{3,5},{5,7},{7,1},{8,10},{10,12},{12... | collective-permute-start | bytes 737288 | tf_op jit(solution)/shard_map/ppermute | solution.py:360
  140.5 11.3 %collective-permute-start.14 = (bf16[4,80,384]{2,1,0:T(8,128)(2,1)S(1)}, bf16[4,80,384]{2,1,0:T(8,128)(2,1)S(1)}, u32[]{:S(2)}, u32[]{:S(2)}) collective-permute-start(bf16[4,80,384]{2,1,0:T(8,128)(2,1)S(1)} %get-tuple-element.45), channel_id=1, source_target_pairs={{0,6},{2,0},{4,2},{6,4},{1,7},{3,1},{5,3},{7,5},{8,14},{10,8},{12,... | collective-permute-start | bytes 737288 | tf_op jit(solution)/shard_map/ppermute | solution.py:360
  143.9 7.7 %collective-permute-start.16 = (bf16[2,80,384]{2,1,0:T(8,128)(2,1)S(1)}, bf16[2,80,384]{2,1,0:T(8,128)(2,1)S(1)}, u32[]{:S(2)}, u32[]{:S(2)}) collective-permute-start(bf16[2,80,384]{2,1,0:T(8,128)(2,1)S(1)} %collective-permute-done.15), channel_id=1, source_target_pairs={{0,2},{2,4},{4,6},{6,0},{1,3},{3,5},{5,7},{7,1},{8,10},{10,12},{12... | collective-permute-start | bytes 368648 | tf_op jit(solution)/shard_map/ppermute | solution.py:360
  144.7 7.1 %collective-permute-start.18 = (bf16[2,80,384]{2,1,0:T(8,128)(2,1)S(1)}, bf16[2,80,384]{2,1,0:T(8,128)(2,1)S(1)}, u32[]{:S(2)}, u32[]{:S(2)}) collective-permute-start(bf16[2,80,384]{2,1,0:T(8,128)(2,1)S(1)} %collective-permute-done.17), channel_id=1, source_target_pairs={{0,6},{2,0},{4,2},{6,4},{1,7},{3,1},{5,3},{7,5},{8,14},{10,8},{12,... | collective-permute-start | bytes 368648 | tf_op jit(solution)/shard_map/ppermute | solution.py:360
  152.6 6.4 %collective-permute-start.19 = (bf16[80,384]{1,0:T(8,128)(2,1)S(1)}, bf16[80,384]{1,0:T(8,128)(2,1)S(1)}, u32[]{:S(2)}, u32[]{:S(2)}) collective-permute-start(bf16[80,384]{1,0:T(8,128)(2,1)S(1)} %get-tuple-element.49), channel_id=1, source_target_pairs={{0,8},{8,16},{16,24},{24,0},{1,9},{9,17},{17,25},{25,1},{2,10},{10... | collective-permute-start | bytes 184328 | tf_op jit(solution)/shard_map/ppermute | solution.py:360
  154.1 5.7 %collective-permute-start.20 = (bf16[80,384]{1,0:T(8,128)(2,1)S(1)}, bf16[80,384]{1,0:T(8,128)(2,1)S(1)}, u32[]{:S(2)}, u32[]{:S(2)}) collective-permute-start(bf16[80,384]{1,0:T(8,128)(2,1)S(1)} %get-tuple-element.50), channel_id=1, source_target_pairs={{0,16},{8,24},{16,0},{24,8},{1,17},{9,25},{17,1},{25,9},{2,18},{10... | collective-permute-start | bytes 184328 | tf_op jit(solution)/shard_map/ppermute | solution.py:360
  156.7 4.2 %collective-permute-start.21 = (bf16[80,384]{1,0:T(8,128)(2,1)S(1)}, bf16[80,384]{1,0:T(8,128)(2,1)S(1)}, u32[]{:S(2)}, u32[]{:S(2)}) collective-permute-start(bf16[80,384]{1,0:T(8,128)(2,1)S(1)} %get-tuple-element.51), channel_id=1, source_target_pairs={{0,24},{8,0},{16,8},{24,16},{1,25},{9,1},{17,9},{25,17},{2,26},{10... | collective-permute-start | bytes 184328 | tf_op jit(solution)/shard_map/ppermute | solution.py:360
